TPU v7x, 32 devices: a whole 2x2x4 slice. The times are simulated.
32 devices in a mesh: dp: 8 (over z, x), expert: 4 (over y, core).
Axes of the slice: x: 2, y: 2, z: 4, core: 2. Of those that a mesh axis runs over, the one named last changes fastest.
Arguments:
- images: bfloat16 [128, 197, 512], P(('dp', 'expert')), may hold values from -6 to 6
- adapter_ids: int32 [128], P(('dp', 'expert')), may hold values from 0 to 7
- expert_ids: int32 [128, 197, 2], P(('dp', 'expert')), may hold values from 0 to 15, all different within a row; in each aligned block of 788 rows (0 to 787, 788 to 1575, ..., all dimensions but the last counted through in order) at most 246 rows name the same one
- cotangent: bfloat16 [128, 197, 512], P(('dp', 'expert')), may hold values from -6 to 6
- ln_gain1: bfloat16 [512], replicated, may hold values from 0.099609375 to 1.8984375
- ln_gain2: bfloat16 [512], replicated, may hold values from 0.099609375 to 1.8984375
- qkv_weight: bfloat16 [512, 1536], replicated, may hold values from -0.25 to 0.25
- out_weight: bfloat16 [512, 512], replicated, may hold values from -1 to 1
- router_weight: bfloat16 [512, 16], replicated, may hold values from -0.1875 to 0.1875
- up_weight: bfloat16 [16, 512, 2048], P('expert'), may hold values from -0.25 to 0.25
- down_weight: bfloat16 [16, 2048, 512], P('expert'), may hold values from -0.125 to 0.125
- qkv_a: bfloat16 [8, 512, 16], replicated, may hold values from -0.25 to 0.25
- qkv_b: bfloat16 [8, 16, 1536], replicated, may hold values from -1 to 1
- out_a: bfloat16 [8, 512, 16], replicated, may hold values from -0.25 to 0.25
- out_b: bfloat16 [8, 16, 512], replicated, may hold values from -3 to 3
- router_a: bfloat16 [8, 512, 16], replicated, may hold values from -0.25 to 0.25
- router_b: bfloat16 [8, 16, 16], replicated, may hold values from -0.75 to 0.75
- up_a: bfloat16 [16, 8, 512, 16], P('expert'), may hold values from -0.25 to 0.25
- up_b: bfloat16 [16, 8, 16, 2048], P('expert'), may hold values from -1 to 1
- down_a: bfloat16 [16, 8, 2048, 16], P('expert'), may hold values from -0.125 to 0.125
- down_b: bfloat16 [16, 8, 16, 512], P('expert'), may hold values from -1 to 1
Outputs:
- block_out: bfloat16 [128, 197, 512], P(('dp', 'expert'))
- input_grad: float32 [128, 197, 512], P(('dp', 'expert'))
- grad_qkv_a: float32 [8, 512, 16], replicated
- grad_qkv_b: float32 [8, 16, 1536], replicated
- grad_out_a: float32 [8, 512, 16], replicated
- grad_out_b: float32 [8, 16, 512], replicated
- grad_router_a: float32 [8, 512, 16], replicated
- grad_router_b: float32 [8, 16, 16], replicated
- grad_up_a: float32 [16, 8, 512, 16], P('expert')
- grad_up_b: float32 [16, 8, 16, 2048], P('expert')
- grad_down_a: float32 [16, 8, 2048, 16], P('expert')
- grad_down_b: float32 [16, 8, 16, 512], P('expert')
Inputs may be any that keep to these rules, and one draw needn't show every extreme that they name: `expert_ids`: each token names 2 different experts; among the tokens of one device no expert is named more than min(246, 788) times, and some expert is named exactly that often.
All inputs are finite; a program needn't handle non-finite values.
Results may differ from a plain program's by a relative error of at most 0.017.
Values may be sent and summed in bfloat16 or wider, within the bound.
A program may use at most 256 MiB of HBM per device.

v0:
```python
import jax
import jax.numpy as jnp
from jax import lax
from jax.sharding import PartitionSpec as P

HEADS = 8


EPSILON = 1e-06


def product(left, right):
    return jnp.dot(left, right, preferred_element_type=jnp.float32)


def contract(form, left, right):
    return jnp.einsum(form, left, right, preferred_element_type=jnp.float32)


def norm_parts(values, gain):
    average = jnp.mean(values, axis=-1, keepdims=True)
    centred = values - average
    spread = jnp.mean(centred * centred, axis=-1, keepdims=True)
    factor = lax.rsqrt(spread + EPSILON)
    normed = centred * factor
    return (normed * gain, normed, factor)


def norm_back(grad, normed, factor, gain):
    scaled = grad * gain
    return factor * (
        scaled
        - jnp.mean(scaled, axis=-1, keepdims=True)
        - normed * jnp.mean(scaled * normed, axis=-1, keepdims=True)
    )


def gelu_exact(values):
    return jax.nn.gelu(values, approximate=False)


def body(
    images,
    adapter_ids,
    expert_ids,
    cotangent,
    ln_gain1,
    ln_gain2,
    qkv_weight,
    out_weight,
    router_weight,
    up_weight,
    down_weight,
    qkv_a,
    qkv_b,
    out_a,
    out_b,
    router_a,
    router_b,
    up_a,
    up_b,
    down_a,
    down_b,
):
    low_type = jnp.bfloat16
    n_images = images.shape[0]
    seq_len = images.shape[1]
    width = images.shape[2]
    tokens = n_images * seq_len
    n_adapt = qkv_a.shape[0]
    rank = qkv_a.shape[2]
    low_cols = n_adapt * rank
    head_size = width // HEADS
    head_scale = head_size ** (-0.5)
    n_experts = router_weight.shape[1]
    local_experts = up_weight.shape[0]
    ff_width = up_weight.shape[2]
    groups = lax.axis_size("expert")
    capacity = max(2, tokens * 2 * 5 // (4 * n_experts))
    gain_one = ln_gain1.astype(jnp.float32)
    gain_two = ln_gain2.astype(jnp.float32)
    token_ids = jnp.repeat(adapter_ids, seq_len)
    picked = (token_ids[:, None] == jnp.arange(n_adapt, dtype=jnp.int32)[None, :]).astype(
        jnp.float32
    )
    columns = jnp.repeat(picked, rank, axis=1)
    qkv_a_flat = qkv_a.transpose(1, 0, 2).reshape(width, low_cols)
    qkv_b_flat = qkv_b.reshape(low_cols, 3 * width)
    out_a_flat = out_a.transpose(1, 0, 2).reshape(width, low_cols)
    out_b_flat = out_b.reshape(low_cols, width)
    router_a_flat = router_a.transpose(1, 0, 2).reshape(width, low_cols)
    router_b_flat = router_b.reshape(low_cols, n_experts)
    residual_in = images.reshape(tokens, width).astype(jnp.float32)
    normed_one, plain_one, factor_one = norm_parts(residual_in, gain_one)
    normed_one = normed_one.astype(low_type)
    low_one = (product(normed_one, qkv_a_flat) * columns).astype(low_type)
    projected = (product(normed_one, qkv_weight) + product(low_one, qkv_b_flat)).astype(low_type)
    projected = projected.reshape(n_images, seq_len, 3, HEADS, head_size)
    queries = projected[:, :, 0]
    keys_all = projected[:, :, 1]
    values_all = projected[:, :, 2]
    scores = contract("ishd,ithd->ihst", queries, keys_all) * head_scale
    attention = jax.nn.softmax(scores, axis=-1)
    attention_low = attention.astype(low_type)
    context = (
        contract("ihst,ithd->ishd", attention_low, values_all)
        .astype(low_type)
        .reshape(tokens, width)
    )
    low_two = (product(context, out_a_flat) * columns).astype(low_type)
    hidden_one = residual_in + product(context, out_weight) + product(low_two, out_b_flat)
    normed_two, plain_two, factor_two = norm_parts(hidden_one, gain_two)
    normed_two = normed_two.astype(low_type)
    low_router = (product(normed_two, router_a_flat) * columns).astype(low_type)
    logits = product(normed_two, router_weight) + product(low_router, router_b_flat)
    chosen_ids = expert_ids.reshape(tokens, 2)
    onehot = (
        chosen_ids[:, :, None] == jnp.arange(n_experts, dtype=jnp.int32)[None, None, :]
    ).astype(jnp.int32)
    onehot_float = onehot.astype(jnp.float32)
    chosen = jnp.sum(logits[:, None, :] * onehot_float, axis=-1)
    gates = jax.nn.softmax(chosen, axis=-1)
    before = jnp.cumsum(onehot, axis=0, dtype=jnp.int32) - onehot
    first_total = jnp.sum(onehot[:, 0], axis=0, dtype=jnp.int32)
    place_first = jnp.sum(before[:, 0] * onehot[:, 0], axis=-1, dtype=jnp.int32)
    place_second = jnp.sum(
        (before[:, 1] + first_total[None, :]) * onehot[:, 1], axis=-1, dtype=jnp.int32
    )
    places = jnp.stack([place_first, place_second], axis=1)
    slot_index = jnp.where(places < capacity, chosen_ids * capacity + places, n_experts * capacity)
    owners = jnp.repeat(jnp.arange(tokens, dtype=jnp.int32), 2)
    slot_owner = (
        jnp.full((n_experts * capacity,), tokens, jnp.int32)
        .at[slot_index.reshape(-1)]
        .set(owners, mode="drop")
    )
    padded_rows = jnp.concatenate([normed_two, jnp.zeros((1, width), low_type)], axis=0)
    padded_ids = jnp.concatenate([token_ids, jnp.zeros((1,), jnp.int32)], axis=0)
    send_rows = padded_rows[slot_owner].reshape(groups, local_experts, capacity, width)
    send_ids = padded_ids[slot_owner].reshape(groups, local_experts, capacity)
    slot_rows, slot_ids = (
        lax.all_to_all(send_rows, "expert", split_axis=0, concat_axis=0, tiled=True),
        lax.all_to_all(send_ids, "expert", split_axis=0, concat_axis=0, tiled=True),
    )
    up_a_flat = up_a.transpose(0, 2, 1, 3).reshape(local_experts, width, low_cols)
    up_b_flat = up_b.reshape(local_experts, low_cols, ff_width)
    down_a_flat = down_a.transpose(0, 2, 1, 3).reshape(local_experts, ff_width, low_cols)
    down_b_flat = down_b.reshape(local_experts, low_cols, width)
    slot_pick = (slot_ids[..., None] == jnp.arange(n_adapt, dtype=jnp.int32)).astype(jnp.float32)
    slot_columns = jnp.repeat(slot_pick, rank, axis=-1)
    up_low = (contract("secd,edk->seck", slot_rows, up_a_flat) * slot_columns).astype(low_type)
    preact = contract("secd,edf->secf", slot_rows, up_weight) + contract(
        "seck,ekf->secf", up_low, up_b_flat
    )
    hidden = gelu_exact(preact).astype(low_type)
    down_low = (contract("secf,efk->seck", hidden, down_a_flat) * slot_columns).astype(low_type)
    expert_out = (
        contract("secf,efd->secd", hidden, down_weight)
        + contract("seck,ekd->secd", down_low, down_b_flat)
    ).astype(low_type)
    returned = lax.all_to_all(expert_out, "expert", split_axis=0, concat_axis=0, tiled=True)
    returned_pad = jnp.concatenate(
        [returned.reshape(n_experts * capacity, width), jnp.zeros((1, width), low_type)], axis=0
    )
    pair_float = returned_pad[slot_index].astype(jnp.float32)
    mixture = jnp.sum(gates[:, :, None] * pair_float, axis=1)
    block_out = (hidden_one + mixture).astype(low_type).reshape(n_images, seq_len, width)
    upstream = cotangent.reshape(tokens, width).astype(jnp.float32)
    gate_grad = jnp.sum(upstream[:, None, :] * pair_float, axis=-1)
    pair_grad = (gates[:, :, None] * upstream[:, None, :]).astype(low_type)
    send_grad = (
        jnp.zeros((n_experts * capacity, width), low_type)
        .at[slot_index.reshape(-1)]
        .set(pair_grad.reshape(tokens * 2, width), mode="drop")
    )
    send_grad = send_grad.reshape(groups, local_experts, capacity, width)
    slot_grad = lax.all_to_all(send_grad, "expert", split_axis=0, concat_axis=0, tiled=True)
    down_low_grad = (contract("secd,ekd->seck", slot_grad, down_b_flat) * slot_columns).astype(
        low_type
    )
    grad_down_b = contract("seck,secd->ekd", down_low, slot_grad).reshape(
        local_experts, n_adapt, rank, width
    )
    grad_down_a = (
        contract("secf,seck->efk", hidden, down_low_grad)
        .reshape(local_experts, ff_width, n_adapt, rank)
        .transpose(0, 2, 1, 3)
    )
    hidden_grad = contract("secd,efd->secf", slot_grad, down_weight) + contract(
        "seck,efk->secf", down_low_grad, down_a_flat
    )
    preact_grad = jax.vjp(gelu_exact, preact)[1](hidden_grad)[0].astype(low_type)
    grad_up_b = contract("seck,secf->ekf", up_low, preact_grad).reshape(
        local_experts, n_adapt, rank, ff_width
    )
    up_low_grad = (contract("secf,ekf->seck", preact_grad, up_b_flat) * slot_columns).astype(
        low_type
    )
    grad_up_a = (
        contract("secd,seck->edk", slot_rows, up_low_grad)
        .reshape(local_experts, width, n_adapt, rank)
        .transpose(0, 2, 1, 3)
    )
    rows_grad = (
        contract("secf,edf->secd", preact_grad, up_weight)
        + contract("seck,edk->secd", up_low_grad, up_a_flat)
    ).astype(low_type)
    back_grad = lax.all_to_all(rows_grad, "expert", split_axis=0, concat_axis=0, tiled=True)
    back_pad = jnp.concatenate(
        [back_grad.reshape(n_experts * capacity, width), jnp.zeros((1, width), low_type)], axis=0
    )
    normed_two_grad = jnp.sum(back_pad[slot_index].astype(jnp.float32), axis=1)
    chosen_grad = gates * (gate_grad - jnp.sum(gates * gate_grad, axis=-1, keepdims=True))
    logits_grad = jnp.sum(chosen_grad[:, :, None] * onehot_float, axis=1).astype(low_type)
    grad_router_b = contract("tk,te->ke", low_router, logits_grad).reshape(n_adapt, rank, n_experts)
    router_low_grad = (contract("te,ke->tk", logits_grad, router_b_flat) * columns).astype(low_type)
    grad_router_a = (
        contract("td,tk->dk", normed_two, router_low_grad)
        .reshape(width, n_adapt, rank)
        .transpose(1, 0, 2)
    )
    normed_two_grad = (
        normed_two_grad
        + contract("te,de->td", logits_grad, router_weight)
        + contract("tk,dk->td", router_low_grad, router_a_flat)
    )
    hidden_one_grad = upstream + norm_back(normed_two_grad, plain_two, factor_two, gain_two)
    branch_grad = hidden_one_grad.astype(low_type)
    grad_out_b = contract("tk,td->kd", low_two, branch_grad).reshape(n_adapt, rank, width)
    out_low_grad = (contract("td,kd->tk", branch_grad, out_b_flat) * columns).astype(low_type)
    grad_out_a = (
        contract("td,tk->dk", context, out_low_grad)
        .reshape(width, n_adapt, rank)
        .transpose(1, 0, 2)
    )
    context_grad = (
        contract("td,ed->te", branch_grad, out_weight)
        + contract("tk,dk->td", out_low_grad, out_a_flat)
    ).astype(low_type)
    context_grad = context_grad.reshape(n_images, seq_len, HEADS, head_size)
    values_grad = contract("ihst,ishd->ithd", attention_low, context_grad)
    weights_grad = contract("ishd,ithd->ihst", context_grad, values_all)
    score_grad = (
        attention * (weights_grad - jnp.sum(weights_grad * attention, axis=-1, keepdims=True))
    ).astype(low_type)
    query_grad = contract("ihst,ithd->ishd", score_grad, keys_all) * head_scale
    key_grad = contract("ihst,ishd->ithd", score_grad, queries) * head_scale
    projected_grad = (
        jnp.stack([query_grad, key_grad, values_grad], axis=2)
        .reshape(tokens, 3 * width)
        .astype(low_type)
    )
    grad_qkv_b = contract("tk,te->ke", low_one, projected_grad).reshape(n_adapt, rank, 3 * width)
    qkv_low_grad = (contract("te,ke->tk", projected_grad, qkv_b_flat) * columns).astype(low_type)
    grad_qkv_a = (
        contract("td,tk->dk", normed_one, qkv_low_grad)
        .reshape(width, n_adapt, rank)
        .transpose(1, 0, 2)
    )
    normed_one_grad = contract("te,de->td", projected_grad, qkv_weight) + contract(
        "tk,dk->td", qkv_low_grad, qkv_a_flat
    )
    input_grad = (
        hidden_one_grad + norm_back(normed_one_grad, plain_one, factor_one, gain_one)
    ).reshape(n_images, seq_len, width)
    grad_up_a, grad_up_b, grad_down_a, grad_down_b = lax.psum(
        (grad_up_a, grad_up_b, grad_down_a, grad_down_b), "dp"
    )
    grad_qkv_a, grad_qkv_b, grad_out_a, grad_out_b, grad_router_a, grad_router_b = lax.psum(
        (grad_qkv_a, grad_qkv_b, grad_out_a, grad_out_b, grad_router_a, grad_router_b),
        ("dp", "expert"),
    )
    return (
        block_out,
        input_grad,
        grad_qkv_a,
        grad_qkv_b,
        grad_out_a,
        grad_out_b,
        grad_router_a,
        grad_router_b,
        grad_up_a,
        grad_up_b,
        grad_down_a,
        grad_down_b,
    )


def solution(mesh):
    placed = (
        P(("dp", "expert"), None, None),
        P(("dp", "expert")),
        P(("dp", "expert"), None, None),
        P(("dp", "expert"), None, None),
        P(),
        P(),
        P(),
        P(),
        P(),
        P("expert", None, None),
        P("expert", None, None),
        P(),
        P(),
        P(),
        P(),
        P(),
        P(),
        P("expert", None, None, None),
        P("expert", None, None, None),
        P("expert", None, None, None),
        P("expert", None, None, None),
    )
    return jax.shard_map(
        body,
        mesh=mesh,
        in_specs=placed,
        out_specs=(
            P(("dp", "expert"), None, None),
            P(("dp", "expert"), None, None),
            P(),
            P(),
            P(),
            P(),
            P(),
            P(),
            P("expert", None, None, None),
            P("expert", None, None, None),
            P("expert", None, None, None),
            P("expert", None, None, None),
        ),
        check_vma=False,
    )
```

profile of v0, /device:TPU:0, one launch (start us, length us, event | category | flops | bytes accessed | tf_op | source)
XLA Modules:
  0.0 951.3 jit_solution(18246019455004091791)
XLA Ops:
  9.7 4.0 reduce-window.6
  15.7 8.8 scatter_custom_fusion
  24.7 8.4 gather_fusion.1
  33.8 4.8 all-to-all-start.1
  56.4 7.2 reshape.584
  63.5 4.7 fusion.136
  79.4 5.4 fusion.137
  99.9 9.2 gather_fusion
  111.9 4.5 copy.282
  116.4 4.6 all-to-all-start
  127.6 4.2 mul.312
  131.8 5.4 mul.313
  142.1 17.8 %scatter_custom_fusion.1 = bf16[1968,512]{1,0:T(8,128)(2,1)} fusion(s32[1576]{0:T(1024)} %copy-done.90, f32[1576,512]{1,0:T(8,128)} %mul.313, f32[1576]{0:T(1024)S(1)} %div.62, bf16[]{:T(256)} %constant.49.clone.1), kind=kCustom, calls=%fused_computation.95 | custom fusion | flops 1613824 | bytes 5249696 | tf_op jit(solution)/shard_map/scatter | solution.py:174
  162.8 4.4 copy.297
  167.2 4.5 all-to-all-start.3
  180.3 8.1 fusion.143
  188.3 8.5 all-to-all-done.3
  200.0 8.1 fusion.144
  208.1 47.3 %fusion.10 = (bf16[4,4,123,2048]{3,2,0,1:T(8,128)(2,1)S(1)}, f32[4,4,123,2048]{3,2,0,1:T(8,128)}, f32[4,4,123,2048]{3,2,1,0:T(8,128)}) fusion(f32[4,4,123,2048]{3,2,1,0:T(8,128)} %fusion.143, bf16[4,512,2048]{2,1,0:T(8,128)(2,1)} %param.30, bf16[4,4,123,512]{3,1,2,0:T(4,128)(2,1)} %all-to-all-done), kind=kOutput, calls=%fused_computation.24 | convolution fusion | flops 4393205760 | bytes 66830336 | tf_op jit(solution)/shard_map/secd,edf->secf/dot_general | solution.py:17
  257.9 7.4 fusion.29
  265.3 25.3 %fusion.7 = bf16[4,4,123,2048]{3,2,0,1:T(8,128)(2,1)} fusion(f32[4,4,123,2048]{3,2,0,1:T(8,128)} %get-tuple-element.90, f32[4,4,123,2048]{3,2,1,0:T(8,128)} %fusion.144, f32[4,4,123,2048]{3,2,1,0:T(8,128)} %get-tuple-element.100, bf16[4,2048,512]{2,1,0:T(8,128)(2,1)} %param.31, bf16[4,4,123,512]{3,1,2,0:T(4,128)(2,1)} %all-to-all-done.3), kind=kOutput, calls=%fused_computation.16 | convolution fusion | flops 4187652096 | bytes 66830336 | tf_op jit(solution)/shard_map/secd,efd->secf/dot_general | solution.py:17
  290.7 12.4 %fusion.23 = f32[4,4,123,512]{3,2,1,0:T(8,128)} fusion(bf16[4,4,123,2048]{3,2,0,1:T(8,128)(2,1)} %fusion.7, bf16[4,512,2048]{2,1,0:T(8,128)(2,1)} %param.30), kind=kOutput, calls=%fused_computation.38 | convolution fusion | flops 4127195136 | bytes 20480000 | tf_op jit(solution)/shard_map/secf,edf->secd/dot_general | solution.py:17
  306.6 4.7 all-to-all-start.2
  311.3 5.9 fusion.83
  320.9 6.7 fusion.147
  327.7 8.5 all-to-all-done.2
  336.1 4.4 all-to-all-start.4
  340.6 3.3 copy.291
  348.8 6.0 gather_fusion.2
  354.8 5.0 reshape.566
  359.9 11.2 %multiply_reduce_fusion.2 = (f32[788,2]{1,0:T(8,128)S(1)}, f32[788,512]{1,0:T(8,128)}) fusion(f32[788,2,512]{2,1,0:T(2,128)} %reshape.566, f32[788,512]{1,0:T(8,128)S(1)} %copy-done.10, f32[788,2]{1,0:T(8,128)S(1)} %copy-done.33), kind=kLoop, calls=%fused_computation.58 | loop fusion | flops 2822616 | bytes 6467904 | tf_op jit(solution)/shard_map/reduce_sum | solution.py:169
  373.4 3.3 copy.306
  381.3 6.0 gather_fusion.3
  387.3 5.5 reshape.567
  393.9 7.1 reduce_sum.191
  413.1 5.5 fusion.56
  418.6 7.1 multiply_reduce_fusion
  425.7 4.3 multiply_convert_fusion
  437.8 4.5 copy.317
  442.3 6.8 convert_element_type.198
  452.1 3.7 fusion.40
  458.3 3.4 fusion.47
  461.7 3.4 fusion.42
  465.1 7.0 fusion.148
  474.8 4.1 fusion.145
  483.1 42.4 %psum.75 = f32[8,16,16]{2,1,0:T(8,128)} all-reduce(f32[8,16,16]{2,1,0:T(8,128)S(1)} %bitcast.379), channel_id=1, replica_groups=mesh['dp'=8,'expert'=4] {'dp','expert'}, use_global_device_ids=true, to_apply=%region_31.32 | all-reduce | flops 2048 | bytes 16384 | tf_op jit(solution)/shard_map/psum | solution.py:269
  525.4 70.5 %all-reduce.9.cloned.1.call-done = (f32[8,512,16]{1,2,0:T(8,128)}, f32[8,16,1536]{2,1,0:T(8,128)}, f32[8,512,16]{1,2,0:T(8,128)}, f32[8,16,512]{2,1,0:T(8,128)}, f32[8,512,16]{1,2,0:T(8,128)}) async-done(((f32[8,512,16]{1,2,0:T(8,128)}, f32[8,16,1536]{2,1,0:T(8,128)}, f32[8,512,16]{1,2,0:T(8,128)}, f32[8,16,512]{2,1,0:T(8,128)}, f32[8,512,16]{1,2,0:T(8,128)}), (f32[8,512,16]{1,2,0:T(8,128)}, ...) | async-done | bytes 1835024 | tf_op jit(solution)/shard_map/psum | solution.py:269
  596.0 331.3 %all-reduce.11.cloned.1.call-done = (f32[4,8,512,16]{2,3,1,0:T(8,128)}, f32[4,8,16,2048]{3,2,1,0:T(8,128)}, f32[4,8,2048,16]{2,3,1,0:T(8,128)}, f32[4,8,16,512]{3,2,1,0:T(8,128)}) async-done(((f32[4,8,512,16]{2,3,1,0:T(8,128)}, f32[4,8,16,2048]{3,2,1,0:T(8,128)}, f32[4,8,2048,16]{2,3,1,0:T(8,128)}, f32[4,8,16,512]{3,2,1,0:T(8,128)}), (f32[4,8,512,16]{2,3,1,0:T(8,128)}, f32[4,8,16,2048]{3,2,1,0:T(8,128)}, ...) | async-done | bytes 10485776 | tf_op jit(solution)/shard_map/psum | solution.py:266
  (342 shorter events, 149.0 us)
Async XLA Ops:
  7.2 192.0 %copy-start = (bf16[4,8,2048,16]{2,3,1,0:T(8,128)(2,1)S(1)}, bf16[4,8,2048,16]{2,3,1,0:T(8,128)(2,1)}, u32[]{:S(2)}) copy-start(bf16[4,8,2048,16]{2,3,1,0:T(8,128)(2,1)} %param.40) | copy-start | bytes 6291460
  9.6 130.7 %copy-start.64 = (s32[788,2]{0,1:T(2,128)}, s32[788,2]{0,1:T(2,128)S(1)}, u32[]{:S(2)}) copy-start(s32[788,2]{0,1:T(2,128)S(1)} %eq.56) | copy-start | bytes 18916
  14.4 10.2 %copy-start.83 = (s32[788]{0:T(1024)}, s32[788]{0:T(1024)S(1)}, u32[]{:S(2)}) copy-start(s32[788]{0:T(1024)S(1)} %get-tuple-element.78) | copy-start | bytes 9460
  15.7 8.9 copy-start.90
  24.7 13.9 %copy-start.20 = (bf16[4,197,512]{2,0,1:T(4,128)(2,1)S(1)}, bf16[4,197,512]{2,0,1:T(4,128)(2,1)}, u32[]{:S(2)}) copy-start(bf16[4,197,512]{2,0,1:T(4,128)(2,1)} %param.21) | copy-start | bytes 2420740
  33.1 8.4 copy-start.91
  33.1 8.3 copy-start.92
  33.8 82.6 %all-to-all-start.1 = ((s32[4,4,123]{2,1,0:T(4,128)}), s32[4,4,123]{2,1,0:T(4,128)}, u32[]{:S(2)}, u32[]{:S(2)}) async-start(s32[4,4,123]{2,1,0:T(4,128)} %reshape.493), calls=%async_computation.1 | async-start | bytes 16384 | tf_op jit(solution)/shard_map/all_to_all | solution.py:143
  42.1 11.3 %copy-start.77 = (f32[788]{0:T(1024)}, f32[788]{0:T(1024)S(1)}, u32[]{:S(2)}) copy-start(f32[788]{0:T(1024)S(1)} %div.54) | copy-start | bytes 9460
  42.3 11.1 %copy-start.79 = (f32[788]{0:T(1024)}, f32[788]{0:T(1024)S(1)}, u32[]{:S(2)}) copy-start(f32[788]{0:T(1024)S(1)} %rsqrt.21) | copy-start | bytes 9460
  44.3 93.2 %copy-start.12 = (f32[788,128]{1,0:T(8,128)}, f32[788,128]{1,0:T(8,128)S(1)}, u32[]{:S(2)}) copy-start(f32[788,128]{1,0:T(8,128)S(1)} %copy.267) | copy-start | bytes 1210372
  79.4 6.1 copy-start.50
  87.6 6.8 copy-start.41
  116.4 7.0 copy-start.54
  116.4 50.8 %all-to-all-start = ((bf16[4,4,123,512]{3,1,2,0:T(4,128)(2,1)}), bf16[4,4,123,512]{3,1,2,0:T(4,128)(2,1)}, u32[]{:S(2)}, u32[]{:S(2)}) async-start(bf16[4,4,123,512]{3,1,2,0:T(4,128)(2,1)} %copy.282), calls=%async_computation | async-start | bytes 4030464 | tf_op jit(solution)/shard_map/all_to_all | solution.py:142
  141.9 20.9 %copy-start.32 = (f32[788,2]{1,0:T(8,128)}, f32[788,2]{1,0:T(8,128)S(1)}, u32[]{:S(2)}) copy-start(f32[788,2]{1,0:T(8,128)S(1)} %copy.277) | copy-start | bytes 18916
  159.9 7.3 copy-start.84
  167.2 29.6 %all-to-all-start.3 = ((bf16[4,4,123,512]{3,1,2,0:T(4,128)(2,1)}), bf16[4,4,123,512]{3,1,2,0:T(4,128)(2,1)}, u32[]{:S(2)}, u32[]{:S(2)}) async-start(bf16[4,4,123,512]{3,1,2,0:T(4,128)(2,1)} %copy.297), calls=%async_computation.3 | async-start | bytes 4030464 | tf_op jit(solution)/shard_map/all_to_all | solution.py:177
  255.4 9.9 %copy-start.8 = (bf16[4,4,123,2048]{3,2,0,1:T(8,128)(2,1)}, bf16[4,4,123,2048]{3,2,0,1:T(8,128)(2,1)S(1)}, u32[]{:S(2)}) copy-start(bf16[4,4,123,2048]{3,2,0,1:T(8,128)(2,1)S(1)} %get-tuple-element.89) | copy-start | bytes 24182788
  257.9 45.2 %copy-start.27 = (bf16[4,4,123,128]{3,2,0,1:T(8,128)(2,1)}, bf16[4,4,123,128]{3,2,0,1:T(8,128)(2,1)S(1)}, u32[]{:S(2)}) copy-start(bf16[4,4,123,128]{3,2,0,1:T(8,128)(2,1)S(1)} %fusion.84) | copy-start | bytes 1511428
  290.6 12.4 %copy-start.55 = (bf16[4,8,16,512]{3,2,1,0:T(8,128)(2,1)S(1)}, bf16[4,8,16,512]{3,2,1,0:T(8,128)(2,1)}, u32[]{:S(2)}) copy-start(bf16[4,8,16,512]{3,2,1,0:T(8,128)(2,1)} %param.41) | copy-start | bytes 1572868
  303.7 7.6 copy-start.24
  306.6 29.5 %all-to-all-start.2 = ((bf16[4,4,123,512]{3,1,2,0:T(4,128)(2,1)}), bf16[4,4,123,512]{3,1,2,0:T(4,128)(2,1)}, u32[]{:S(2)}, u32[]{:S(2)}) async-start(bf16[4,4,123,512]{3,1,2,0:T(4,128)(2,1)} %copy.290), calls=%async_computation.2 | async-start | bytes 4030464 | tf_op jit(solution)/shard_map/all_to_all | solution.py:161
  311.3 5.9 copy-start.29
  311.3 5.9 copy-start.56
  336.1 37.2 %all-to-all-start.4 = ((bf16[4,4,123,512]{3,1,2,0:T(4,128)(2,1)}), bf16[4,4,123,512]{3,1,2,0:T(4,128)(2,1)}, u32[]{:S(2)}, u32[]{:S(2)}) async-start(bf16[4,4,123,512]{3,1,2,0:T(4,128)(2,1)} %copy.305), calls=%async_computation.4 | async-start | bytes 4030464 | tf_op jit(solution)/shard_map/all_to_all | solution.py:208
  340.6 255.4 %all-reduce.9.cloned.1.call-start = ((), (), s32[]{:S(2)}) async-start(), calls=%async_computation.5 | async-start | bytes 3670016 | tf_op jit(solution)/shard_map/psum | solution.py:269
  359.8 11.5 %copy-start.63 = (f32[788,2]{0,1:T(2,128)S(1)}, f32[788,2]{0,1:T(2,128)}, u32[]{:S(2)}) copy-start(f32[788,2]{0,1:T(2,128)} %copy-done.62) | copy-start | bytes 18916
  359.8 11.5 %copy-start.72 = (f32[788]{0:T(1024)S(1)}, f32[788]{0:T(1024)}, u32[]{:S(2)}) copy-start(f32[788]{0:T(1024)} %copy-done.71) | copy-start | bytes 9460
  359.8 11.5 %copy-start.82 = (f32[788]{0:T(1024)S(1)}, f32[788]{0:T(1024)}, u32[]{:S(2)}) copy-start(f32[788]{0:T(1024)} %copy-done.81) | copy-start | bytes 9460
  359.9 11.5 %copy-start.65 = (s32[788,2]{0,1:T(2,128)S(1)}, s32[788,2]{0,1:T(2,128)}, u32[]{:S(2)}) copy-start(s32[788,2]{0,1:T(2,128)} %copy-done.64) | copy-start | bytes 18916
  359.9 11.6 %copy-start.13 = (f32[788,128]{1,0:T(8,128)S(1)}, f32[788,128]{1,0:T(8,128)}, u32[]{:S(2)}) copy-start(f32[788,128]{1,0:T(8,128)} %copy-done.12) | copy-start | bytes 1210372
  359.9 11.6 %copy-start.68 = (bf16[8,16,16]{2,1,0:T(8,128)(2,1)S(1)}, bf16[8,16,16]{2,1,0:T(8,128)(2,1)}, u32[]{:S(2)}) copy-start(bf16[8,16,16]{2,1,0:T(8,128)(2,1)} %param.37) | copy-start | bytes 12292
  359.9 11.9 %copy-start.76 = (bf16[512,16]{0,1:T(8,128)(2,1)S(1)}, bf16[512,16]{0,1:T(8,128)(2,1)}, u32[]{:S(2)}) copy-start(bf16[512,16]{0,1:T(8,128)(2,1)} %param.29) | copy-start | bytes 49156
  392.8 8.2 copy-start.4
  392.8 8.2 copy-start.70
  392.8 8.1 copy-start.74
  392.8 8.1 copy-start.89
  393.9 7.1 copy-start.26
  413.1 12.6 %slice-start = ((s8[6553600]{0:T(1024)(128)(4,1)}), s8[4194304]{0:T(1024)(128)(4,1)S(1)}, s32[]{:S(2)}) async-start(s8[6553600]{0:T(1024)(128)(4,1)} %bitcast.348), calls=%async_computation.7 | async-start | bytes 8388608
  418.6 7.1 slice-start.1
  442.3 6.8 copy-start.15
  442.3 6.8 copy-start.47
  458.0 7.1 copy-start.38
  458.0 469.3 %all-reduce.11.cloned.1.call-start = ((), (), s32[]{:S(2)}) async-start(), calls=%async_computation.6 | async-start | bytes 20971520 | tf_op jit(solution)/shard_map/psum | solution.py:266
  596.0 338.5 %copy-start.61 = (f32[8,512,16]{1,2,0:T(8,128)S(1)}, f32[8,512,16]{1,2,0:T(8,128)}, u32[]{:S(2)}) copy-start(f32[8,512,16]{1,2,0:T(8,128)} %get-tuple-element.113) | copy-start | bytes 786436
  927.3 10.2 %copy-start.31 = (f32[4,8,16,2048]{3,2,1,0:T(8,128)S(1)}, f32[4,8,16,2048]{3,2,1,0:T(8,128)}, u32[]{:S(2)}) copy-start(f32[4,8,16,2048]{3,2,1,0:T(8,128)} %get-tuple-element.116) | copy-start | bytes 12582916
  937.5 6.7 copy-start.1
  (54 other events, 148.8 us)
Sparse Core Ops, SparseCore 0:
  458.1 137.8 all-reduce.8
  601.1 326.0 all-reduce.10
where the time goes:
time: 957 us; the launch traced here: 951 us
  waiting for transfers between devices  419 us (44%)
  matrix products  200 us (21%)
  local copies, waits for them, and re-layouts  190 us (20%)
  other arithmetic  60.6 us (6%)
  blocking collectives  42.4 us (4%)
  starting transfers between devices  23.2 us (2%)
  between operations  15.7 us (2%)
    psum x1, waiting for transfers between devices, body(): lax.psum((grad_up_a, grad_up_b, grad_down_a, grad_down_b), 'dp')  331 us
    dot_general x36, matrix products, contract(): return jnp.einsum(form, left, right, preferred_element_type=jnp.float32)  187 us
    psum x1, waiting for transfers between devices, body(): lax.psum((grad_qkv_a, grad_qkv_b, grad_out_a, grad_out_b, grad_router_a,...  70.5 us
    psum x1, blocking collectives, body(): lax.psum((grad_qkv_a, grad_qkv_b, grad_out_a, grad_out_b, grad_router_a,...  42.4 us
    unnamed x208, local copies, waits for them, and re-layouts  39.1 us
  transfers between devices with their start and end apart: 7, of which 4 were waited for; matrix products, arithmetic and copies ran while one was open for 22% of the time, Pallas kernels for 0%

commit v1 on v0

v1 whole, which is shorter than its diff:
```python
import functools

import jax
import jax.numpy as jnp
from jax import lax
from jax.experimental import pallas as pl
from jax.experimental.pallas import tpu as pltpu
from jax.sharding import PartitionSpec as P

HEADS = 8
EPSILON = 1e-06
F32 = jnp.float32
LOW = jnp.bfloat16
PIECES = 2
CHUNK = 512


def nn(left, right):
    return lax.dot_general(left, right, (((1,), (0,)), ((), ())), preferred_element_type=F32)


def nt(left, right):
    return lax.dot_general(left, right, (((1,), (1,)), ((), ())), preferred_element_type=F32)


def tn(left, right):
    return lax.dot_general(left, right, (((0,), (0,)), ((), ())), preferred_element_type=F32)


def normalise(values):
    average = jnp.mean(values, axis=-1, keepdims=True)
    centred = values - average
    spread = jnp.mean(centred * centred, axis=-1, keepdims=True)
    factor = lax.rsqrt(spread + EPSILON)
    return centred * factor, factor


def norm_back(grad, normed, factor, gain):
    scaled = grad * gain
    return factor * (
        scaled
        - jnp.mean(scaled, axis=-1, keepdims=True)
        - normed * jnp.mean(scaled * normed, axis=-1, keepdims=True)
    )


def soften(queries, keys, scale, real):
    scores = nt(queries, keys) * scale
    lanes = lax.broadcasted_iota(jnp.int32, scores.shape, 1)
    scores = jnp.where(lanes < real, scores, -1e30)
    powers = jnp.exp(scores - jnp.max(scores, axis=-1, keepdims=True))
    return powers * (1.0 / jnp.sum(powers, axis=-1, keepdims=True))


def pair_gates(first, second):
    top = jnp.maximum(first, second)
    one, two = jnp.exp(first - top), jnp.exp(second - top)
    total = 1.0 / (one + two)
    return one * total, two * total


def forward_kernel(
    real,
    ids_ref,
    images_ref,
    picks_ref,
    pick_rows_ref,
    gain1_ref,
    gain2_ref,
    wqkv_ref,
    wout_ref,
    wrouter_ref,
    qkv_a_ref,
    qkv_b_ref,
    out_a_ref,
    out_b_ref,
    router_a_ref,
    router_b_ref,
    qkv_ref,
    context_ref,
    hidden_ref,
    normed_ref,
    gates_ref,
    gate_rows_ref,
):
    width = images_ref.shape[2]
    size = width // HEADS
    scale = size ** (-0.5)
    inputs = images_ref[0].astype(F32)
    plain, _ = normalise(inputs)
    normed = (plain * gain1_ref[...]).astype(LOW)
    low_one = nt(normed, qkv_a_ref[0]).astype(LOW)
    qkv_ref[0] = (nn(normed, wqkv_ref[...]) + nn(low_one, qkv_b_ref[0])).astype(LOW)
    parts = []
    for head in range(HEADS):
        at = head * size
        probs = soften(
            qkv_ref[0, :, at : at + size],
            qkv_ref[0, :, width + at : width + at + size],
            scale,
            real,
        ).astype(LOW)
        values = qkv_ref[0, :, 2 * width + at : 2 * width + at + size]
        parts.append(nn(probs, values).astype(LOW))
    context = jnp.concatenate(parts, axis=1)
    context_ref[0] = context
    low_two = nt(context, out_a_ref[0]).astype(LOW)
    hidden = inputs + nn(context, wout_ref[...]) + nn(low_two, out_b_ref[0])
    hidden_ref[0] = hidden
    plain_two, _ = normalise(hidden)
    normed_two = (plain_two * gain2_ref[...]).astype(LOW)
    normed_ref[0] = normed_two
    low_router = nt(normed_two, router_a_ref[0]).astype(LOW)
    logits = nt(normed_two, wrouter_ref[...]) + nn(low_router, router_b_ref[0])
    lanes = lax.broadcasted_iota(jnp.int32, logits.shape, 1)
    chosen = [
        jnp.sum(jnp.where(lanes == picks_ref[0, :, k : k + 1], logits, 0.0), axis=1, keepdims=True)
        for k in range(2)
    ]
    gates_ref[0] = jnp.concatenate(pair_gates(*chosen), axis=1)
    low_rows = nt(router_a_ref[0], normed_two).astype(LOW)
    logit_rows = nt(wrouter_ref[...], normed_two) + tn(router_b_ref[0], low_rows)
    places = lax.broadcasted_iota(jnp.int32, logit_rows.shape, 0)
    chosen_rows = [
        jnp.sum(
            jnp.where(places == pick_rows_ref[0, k : k + 1, :], logit_rows, 0.0),
            axis=0,
            keepdims=True,
        )
        for k in range(2)
    ]
    gate_rows_ref[0] = jnp.concatenate(pair_gates(*chosen_rows), axis=0)


def gelu_pair(values):
    half = 0.5 * (1.0 + lax.erf(values * 0.7071067811865476))
    density = jnp.exp(values * values * -0.5) * 0.3989422804014327
    return values * half, half + values * density


def expert_kernel(
    n_here,
    first_ref,
    marks_ref,
    gate_rows_ref,
    tokens_ref,
    upstream_ref,
    up_ref,
    down_ref,
    up_a_ref,
    up_b_ref,
    down_a_ref,
    down_b_ref,
    back_ref,
    grads_ref,
    rows_ref,
    dy_ref,
    mask_ref,
    y_ref,
    dx_ref,
    low_ref,
    low_grad_ref,
    half_ref,
):
    groups, _, capacity, double = back_ref.shape
    width = double // 2
    ff_width = up_ref.shape[2]
    low_cols = up_a_ref.shape[1]
    rank = 16
    start = (first_ref[0] + pl.program_id(0)) * capacity
    for group in range(groups):
        span = slice(group * capacity, (group + 1) * capacity)
        n_tokens = tokens_ref.shape[1]
        slots = lax.broadcasted_iota(jnp.int32, (capacity, n_tokens), 0) + start
        zero = slots == marks_ref[group, 0:1, :]
        one = slots == marks_ref[group, 1:2, :]
        either = jnp.where(zero | one, 1.0, 0.0)
        gate = jnp.sum(
            jnp.where(zero, gate_rows_ref[group, 0:1, :], 0.0)
            + jnp.where(one, gate_rows_ref[group, 1:2, :], 0.0),
            axis=1,
            keepdims=True,
        )
        ids = jnp.sum(
            either * marks_ref[group, 2:3, :].astype(F32), axis=1, keepdims=True
        )
        either = either.astype(LOW)
        rows_ref[span, :] = nn(either, tokens_ref[group]).astype(LOW)
        dy_ref[span, :] = (gate * nn(either, upstream_ref[group])).astype(LOW)
        cols = lax.broadcasted_iota(jnp.int32, (capacity, low_cols), 1) // rank
        mask_ref[span, :] = jnp.where(cols.astype(F32) == ids, 1.0, 0.0)
    mask = mask_ref[...]
    up_low = (nt(rows_ref[...], up_a_ref[0]) * mask).astype(LOW)
    down_low_grad = (nt(dy_ref[...], down_b_ref[0]) * mask).astype(LOW)
    half_ref[0] = up_low.T
    half_ref[1] = down_low_grad.T
    y_ref[...] = jnp.zeros_like(y_ref)
    dx_ref[...] = jnp.zeros_like(dx_ref)
    low_ref[...] = jnp.zeros_like(low_ref)
    low_grad_ref[...] = jnp.zeros_like(low_grad_ref)
    up_b_at, down_a_at, down_b_at = width, width + ff_width, width + 2 * ff_width

    def step(number, carry):
        at = pl.multiple_of(number * CHUNK, CHUNK)
        cols = pl.ds(at, CHUNK)
        pre = nn(rows_ref[...], up_ref[0, :, cols]) + nn(up_low, up_b_ref[0, :, cols])
        hidden, slope = gelu_pair(pre)
        hidden = hidden.astype(LOW)
        grad = nt(dy_ref[...], down_ref[0, cols, :]) + nn(down_low_grad, down_a_ref[0, :, cols])
        grad = (grad * slope).astype(LOW)
        y_ref[...] += nn(hidden, down_ref[0, cols, :])
        low_ref[...] += nt(hidden, down_a_ref[0, :, cols])
        dx_ref[...] += nt(grad, up_ref[0, :, cols])
        low_grad_ref[...] += nt(grad, up_b_ref[0, :, cols])
        grads_ref[0, :, pl.ds(pl.multiple_of(up_b_at + at, CHUNK), CHUNK)] = nn(
            half_ref[0], grad
        ).astype(LOW)
        grads_ref[0, :, pl.ds(pl.multiple_of(down_a_at + at, CHUNK), CHUNK)] = nn(
            half_ref[1], hidden
        ).astype(LOW)
        return carry

    lax.fori_loop(0, ff_width // CHUNK, step, 0)
    down_low = (low_ref[...] * mask).astype(LOW)
    up_low_grad = (low_grad_ref[...] * mask).astype(LOW)
    out = (y_ref[...] + nn(down_low, down_b_ref[0])).astype(LOW)
    dx = (dx_ref[...] + nn(up_low_grad, up_a_ref[0])).astype(LOW)
    back_ref[:, 0, :, :width] = out.reshape(groups, capacity, width)
    back_ref[:, 0, :, width:] = dx.reshape(groups, capacity, width)
    grads_ref[0, :, 0:width] = tn(up_low_grad, rows_ref[...]).astype(LOW)
    grads_ref[0, :, down_b_at : down_b_at + width] = tn(down_low, dy_ref[...]).astype(LOW)


def backward_kernel(
    real,
    ids_ref,
    images_ref,
    upstream_ref,
    hidden_ref,
    normed_ref,
    qkv_ref,
    context_ref,
    gates_ref,
    picks_ref,
    slots_ref,
    gain1_ref,
    gain2_ref,
    wqkv_ref,
    wout_ref,
    wrouter_ref,
    qkv_a_ref,
    qkv_b_ref,
    out_a_ref,
    out_b_ref,
    router_a_ref,
    router_b_ref,
    *rest,
):
    back_refs = rest[:-5]
    out_ref, input_grad_ref, grads_ref, total_ref, dqkv_ref = rest[-5:]
    image = pl.program_id(0)
    own = ids_ref[image]
    width = images_ref.shape[2]
    size = width // HEADS
    scale = size ** (-0.5)
    n_experts = wrouter_ref.shape[0]

    @pl.when(image == 0)
    def _():
        total_ref[...] = jnp.zeros_like(total_ref)

    rows = images_ref.shape[1]
    pair_zero = pair_one = spread = None
    for number, back_ref in enumerate(back_refs):
        n_slots = back_ref.shape[0]
        slots = lax.broadcasted_iota(jnp.int32, (rows, n_slots), 1) + number * n_slots
        zero = jnp.where(slots == slots_ref[0, :, 0:1], 1.0, 0.0).astype(LOW)
        one = jnp.where(slots == slots_ref[0, :, 1:2], 1.0, 0.0).astype(LOW)
        terms = (
            nn(zero, back_ref[:, :width]),
            nn(one, back_ref[:, :width]),
            nn(zero + one, back_ref[:, width:]),
        )
        if number == 0:
            pair_zero, pair_one, spread = terms
        else:
            pair_zero, pair_one, spread = (
                pair_zero + terms[0],
                pair_one + terms[1],
                spread + terms[2],
            )
    gate_zero, gate_one = gates_ref[0, :, 0:1], gates_ref[0, :, 1:2]
    hidden = hidden_ref[0]
    out = (hidden + (gate_zero * pair_zero + gate_one * pair_one)).astype(LOW)
    out_ref[0] = out[:real]
    upstream = upstream_ref[0].astype(F32)
    grad_zero = jnp.sum(upstream * pair_zero, axis=1, keepdims=True)
    grad_one = jnp.sum(upstream * pair_one, axis=1, keepdims=True)
    centre = gate_zero * grad_zero + gate_one * grad_one
    lanes = lax.broadcasted_iota(jnp.int32, (rows, n_experts), 1)
    logits_grad = (
        jnp.where(lanes == picks_ref[0, :, 0:1], gate_zero * (grad_zero - centre), 0.0)
        + jnp.where(lanes == picks_ref[0, :, 1:2], gate_one * (grad_one - centre), 0.0)
    ).astype(LOW)
    normed_two = normed_ref[0]
    low_rows = nt(router_a_ref[0], normed_two).astype(LOW)
    router_low_grad = nt(logits_grad, router_b_ref[0]).astype(LOW)
    qkv_b_at, out_a_at, out_b_at = width, 4 * width, 5 * width
    router_a_at, router_b_at = 6 * width, 7 * width
    total_ref[own, :, router_b_at : router_b_at + n_experts] += nn(low_rows, logits_grad)
    total_ref[own, :, router_a_at : router_a_at + width] += tn(router_low_grad, normed_two)
    spread = spread + nn(logits_grad, wrouter_ref[...]) + nn(router_low_grad, router_a_ref[0])
    plain_two, factor_two = normalise(hidden)
    hidden_grad = upstream + norm_back(spread, plain_two, factor_two, gain2_ref[...])
    branch = hidden_grad.astype(LOW)
    context = context_ref[0]
    low_two = nt(context, out_a_ref[0]).astype(LOW)
    out_low_grad = nt(branch, out_b_ref[0]).astype(LOW)
    total_ref[own, :, out_b_at : out_b_at + width] += tn(low_two, branch)
    total_ref[own, :, out_a_at : out_a_at + width] += tn(out_low_grad, context)
    context_grad = (nt(branch, wout_ref[...]) + nn(out_low_grad, out_a_ref[0])).astype(LOW)
    for head in range(HEADS):
        at = head * size
        queries = qkv_ref[0, :, at : at + size]
        keys = qkv_ref[0, :, width + at : width + at + size]
        values = qkv_ref[0, :, 2 * width + at : 2 * width + at + size]
        own_grad = context_grad[:, at : at + size]
        probs = soften(queries, keys, scale, real)
        probs_grad = nt(own_grad, values)
        score_grad = (
            probs * (probs_grad - jnp.sum(probs_grad * probs, axis=-1, keepdims=True))
        ).astype(LOW)
        dqkv_ref[:, at : at + size] = (nn(score_grad, keys) * scale).astype(LOW)
        dqkv_ref[:, width + at : width + at + size] = (tn(score_grad, queries) * scale).astype(LOW)
        dqkv_ref[:, 2 * width + at : 2 * width + at + size] = tn(
            probs.astype(LOW), own_grad
        ).astype(LOW)
    plain, factor = normalise(images_ref[0].astype(F32))
    normed = (plain * gain1_ref[...]).astype(LOW)
    low_one = nt(normed, qkv_a_ref[0]).astype(LOW)
    dqkv = dqkv_ref[...]
    qkv_low_grad = nt(dqkv, qkv_b_ref[0]).astype(LOW)
    total_ref[own, :, qkv_b_at : qkv_b_at + 3 * width] += tn(low_one, dqkv)
    total_ref[own, :, 0:width] += tn(qkv_low_grad, normed)
    normed_grad = nt(dqkv, wqkv_ref[...]) + nn(qkv_low_grad, qkv_a_ref[0])
    input_grad = hidden_grad + norm_back(normed_grad, plain, factor, gain1_ref[...])
    input_grad_ref[0] = input_grad[:real]

    @pl.when(image == pl.num_programs(0) - 1)
    def _():
        grads_ref[...] = total_ref[...].astype(LOW)


def whole(array):
    rank = len(array.shape)
    return pl.BlockSpec(array.shape, lambda i, s: (0,) * rank)


def per_image(array):
    rank = len(array.shape)
    return pl.BlockSpec((1,) + array.shape[1:], lambda i, s: (i,) + (0,) * (rank - 1))


def per_adapter(array):
    rank = len(array.shape)
    return pl.BlockSpec((1,) + array.shape[1:], lambda i, s: (s[i],) + (0,) * (rank - 1))


def body(
    images,
    adapter_ids,
    expert_ids,
    cotangent,
    ln_gain1,
    ln_gain2,
    qkv_weight,
    out_weight,
    router_weight,
    up_weight,
    down_weight,
    qkv_a,
    qkv_b,
    out_a,
    out_b,
    router_a,
    router_b,
    up_a,
    up_b,
    down_a,
    down_b,
):
    n_images, seq_len, width = images.shape
    tokens = n_images * seq_len
    padded = -(-seq_len // 16) * 16
    rows = n_images * padded
    n_adapt, _, rank = qkv_a.shape
    low_cols = n_adapt * rank
    n_experts = router_weight.shape[1]
    local = up_weight.shape[0]
    ff_width = up_weight.shape[2]
    groups = lax.axis_size("expert")
    capacity = max(2, tokens * 2 * 5 // (4 * n_experts))
    room = -(-capacity // 16) * 16
    here = local // PIECES

    fill = ((0, 0), (0, padded - seq_len), (0, 0))
    images = jnp.pad(images, fill)
    upstream = jnp.pad(cotangent, fill)
    picks = jnp.pad(expert_ids, fill, constant_values=-1)
    pick_rows = picks.transpose(0, 2, 1)
    flat = pick_rows.transpose(1, 0, 2).reshape(2, rows)
    marks = flat[:, None, :] == jnp.arange(n_experts, dtype=jnp.int32)[None, :, None]
    order = jnp.arange(rows, dtype=jnp.int32)
    earlier = (order[:, None] < order[None, :]).astype(LOW)
    before = jnp.dot(
        marks.reshape(2 * n_experts, rows).astype(LOW), earlier, preferred_element_type=F32
    ).reshape(2, n_experts, rows)
    totals = jnp.sum(marks[0].astype(F32), axis=1)
    offset = jnp.stack([jnp.zeros_like(totals), totals])
    places = jnp.sum(
        jnp.where(marks, before + offset[:, :, None], 0.0), axis=1
    ).astype(jnp.int32)
    group_of, inner = flat // local, flat % local
    ranked = ((inner // here) * groups + group_of) * here + inner % here
    kept = (flat >= 0) & (places < capacity)
    slots = jnp.where(kept, ranked * room + places, -1)
    token_ids = jnp.broadcast_to(adapter_ids[:, None], (n_images, padded)).reshape(1, rows)
    slot_columns = slots.reshape(2, n_images, padded).transpose(1, 2, 0)
    side = jnp.concatenate([slots, token_ids], axis=0)
    side_all = lax.all_gather(side, "expert")
    upstream_all = lax.all_gather(upstream.reshape(rows, width), "expert")

    gain_one = ln_gain1.astype(F32).reshape(1, width)
    gain_two = ln_gain2.astype(F32).reshape(1, width)
    router_t = router_weight.T
    qkv_a_t = qkv_a.transpose(0, 2, 1)
    out_a_t = out_a.transpose(0, 2, 1)
    router_a_t = router_a.transpose(0, 2, 1)
    shared = (gain_one, gain_two, qkv_weight, out_weight, router_t)
    adapters = (qkv_a_t, qkv_b, out_a_t, out_b, router_a_t, router_b)
    grid_of = functools.partial(pltpu.PrefetchScalarGridSpec, num_scalar_prefetch=1)
    forward_out = (
        jax.ShapeDtypeStruct((n_images, padded, 3 * width), LOW),
        jax.ShapeDtypeStruct((n_images, padded, width), LOW),
        jax.ShapeDtypeStruct((n_images, padded, width), F32),
        jax.ShapeDtypeStruct((n_images, padded, width), LOW),
        jax.ShapeDtypeStruct((n_images, padded, 2), F32),
        jax.ShapeDtypeStruct((n_images, 2, padded), F32),
    )
    qkv, context, hidden, normed, gates, gate_rows = pl.pallas_call(
        functools.partial(forward_kernel, seq_len),
        out_shape=forward_out,
        grid_spec=grid_of(
            grid=(n_images,),
            in_specs=[per_image(a) for a in (images, picks, pick_rows)]
            + [whole(a) for a in shared]
            + [per_adapter(a) for a in adapters],
            out_specs=[per_image(a) for a in forward_out],
        ),
        name="attend",
    )(adapter_ids, images, picks, pick_rows, *shared, *adapters)

    normed_all = lax.all_gather(normed.reshape(rows, width), "expert")
    gates_all = lax.all_gather(gate_rows.transpose(1, 0, 2).reshape(2, rows), "expert")
    up_a_t = up_a.transpose(0, 1, 3, 2).reshape(local, low_cols, width)
    up_b_flat = up_b.reshape(local, low_cols, ff_width)
    down_a_t = down_a.transpose(0, 1, 3, 2).reshape(local, low_cols, ff_width)
    down_b_flat = down_b.reshape(local, low_cols, width)
    cols = 2 * width + 2 * ff_width
    backs, sums = [], []
    for piece in range(PIECES):
        at = piece * here

        def of_expert(array, at=at):
            rank = len(array.shape)
            return pl.BlockSpec(
                (1,) + array.shape[1:], lambda i, s: (i + at,) + (0,) * (rank - 1)
            )

        weights = (up_weight, down_weight, up_a_t, up_b_flat, down_a_t, down_b_flat)
        first = ((piece * groups + lax.axis_index("expert")) * here).astype(jnp.int32)
        gathered = (side_all, gates_all, normed_all, upstream_all)
        n_rows = groups * room
        back, grads = pl.pallas_call(
            functools.partial(expert_kernel, here),
            out_shape=(
                jax.ShapeDtypeStruct((groups, here, room, 2 * width), LOW),
                jax.ShapeDtypeStruct((here, low_cols, cols), LOW),
            ),
            grid_spec=grid_of(
                grid=(here,),
                in_specs=[whole(a) for a in gathered] + [of_expert(a) for a in weights],
                out_specs=[
                    pl.BlockSpec((groups, 1, room, 2 * width), lambda i, s: (0, i, 0, 0)),
                    pl.BlockSpec((1, low_cols, cols), lambda i, s: (i, 0, 0)),
                ],
                scratch_shapes=[
                    pltpu.VMEM((n_rows, width), LOW),
                    pltpu.VMEM((n_rows, width), LOW),
                    pltpu.VMEM((n_rows, low_cols), F32),
                    pltpu.VMEM((n_rows, width), F32),
                    pltpu.VMEM((n_rows, width), F32),
                    pltpu.VMEM((n_rows, low_cols), F32),
                    pltpu.VMEM((n_rows, low_cols), F32),
                    pltpu.VMEM((2, low_cols, n_rows), LOW),
                ],
            ),
            name=f"experts_{piece}",
        )(first.reshape(1), *gathered, *weights)
        backs.append(lax.all_to_all(back, "expert", split_axis=0, concat_axis=0, tiled=True))
        sums.append(lax.psum(grads, "dp"))
    backs = [back.reshape(groups * here * room, 2 * width) for back in backs]

    grad_cols = 7 * width + 128
    out_types = (
        jax.ShapeDtypeStruct((n_images, seq_len, width), LOW),
        jax.ShapeDtypeStruct((n_images, seq_len, width), F32),
        jax.ShapeDtypeStruct((n_adapt, rank, grad_cols), LOW),
    )
    by_image = (images, upstream, hidden, normed, qkv, context, gates, picks, slot_columns)
    block_out, input_grad, own_grads = pl.pallas_call(
        functools.partial(backward_kernel, seq_len),
        out_shape=out_types,
        grid_spec=grid_of(
            grid=(n_images,),
            in_specs=[per_image(a) for a in by_image]
            + [whole(a) for a in shared]
            + [per_adapter(a) for a in adapters]
            + [whole(a) for a in backs],
            out_specs=[per_image(out_types[0]), per_image(out_types[1]), whole(out_types[2])],
            scratch_shapes=[
                pltpu.VMEM((n_adapt, rank, grad_cols), F32),
                pltpu.VMEM((padded, 3 * width), LOW),
            ],
        ),
        name="attend_back",
    )(adapter_ids, *by_image, *shared, *adapters, *backs)
    own_grads = lax.psum(own_grads, ("dp", "expert")).astype(F32)
    grad_qkv_a = own_grads[:, :, :width].transpose(0, 2, 1)
    grad_qkv_b = own_grads[:, :, width : 4 * width]
    grad_out_a = own_grads[:, :, 4 * width : 5 * width].transpose(0, 2, 1)
    grad_out_b = own_grads[:, :, 5 * width : 6 * width]
    grad_router_a = own_grads[:, :, 6 * width : 7 * width].transpose(0, 2, 1)
    grad_router_b = own_grads[:, :, 7 * width : 7 * width + n_experts]

    def expert_part(start, length):
        parts = [total[:, :, start : start + length].astype(F32) for total in sums]
        return jnp.concatenate(parts, axis=0).reshape(local, n_adapt, rank, length)

    grad_up_a = expert_part(0, width).transpose(0, 1, 3, 2)
    grad_up_b = expert_part(width, ff_width)
    grad_down_a = expert_part(width + ff_width, ff_width).transpose(0, 1, 3, 2)
    grad_down_b = expert_part(width + 2 * ff_width, width)
    return (
        block_out,
        input_grad,
        grad_qkv_a,
        grad_qkv_b,
        grad_out_a,
        grad_out_b,
        grad_router_a,
        grad_router_b,
        grad_up_a,
        grad_up_b,
        grad_down_a,
        grad_down_b,
    )


def solution(mesh):
    tokens = P(("dp", "expert"), None, None)
    experts = P("expert", None, None, None)
    weights = P("expert", None, None)
    placed = (
        (tokens, P(("dp", "expert")), tokens, tokens)
        + (P(),) * 5
        + (weights,) * 2
        + (P(),) * 6
        + (experts,) * 4
    )
    return jax.shard_map(
        body,
        mesh=mesh,
        in_specs=placed,
        out_specs=(tokens, tokens) + (P(),) * 6 + (experts,) * 4,
        check_vma=False,
    )
```

time: 957 us -> 543 us (0.57)
  matrix products: 200 us -> 0.31 us
  local copies, waits for them, and re-layouts: 190 us -> 22.3 us
  Pallas kernels: 0 us -> 115 us
  waiting for transfers between devices: 419 us -> 358 us
  other arithmetic: 60.6 us -> 10.9 us
  blocking collectives: 42.4 us -> 12.8 us
  starting transfers between devices: 23.2 us -> 8.63 us
    dot_general x45 -> x1, matrix products: 200 us -> 0.31 us  [body(): jnp.dot(marks.reshape(2 * n_experts, rows).astype(LOW), earlier, preferre...]
    pallas_call x0 -> x4, Pallas kernels: none -> 115 us  [the longest x2 55.7 us: body(): pl.pallas_call(functools.partial(expert_kernel, here), out_shape=(jax.Sha...]
    psum x2, waiting for transfers between devices: 402 us -> 307 us  [the longest x1 182 us: body(): sums.append(lax.psum(grads, 'dp'))]
    psum x1 -> x0, blocking collectives: 42.4 us -> none  [body(): lax.psum((grad_qkv_a, grad_qkv_b, grad_out_a, grad_out_b, grad_router_a,...]
    convert_element_type x14 -> x1, local copies, waits for them, and re-layouts: 42.5 us -> 0.19 us  [body(): places = jnp.sum(jnp.where(marks, before + offset[:, :, None], 0.0), axis...]
    reshape x16 -> x1, local copies, waits for them, and re-layouts: 39.5 us -> 0.09 us  [body(): jnp.broadcast_to(adapter_ids[:, None], (n_images, padded)).reshape(1, rows)]
    unnamed x208 -> x25, local copies, waits for them, and re-layouts: 39.1 us -> 7.37 us
    gather x4 -> x0, local copies, waits for them, and re-layouts: 29.6 us -> none  [the longest x1 9.18 us: body(): padded_rows[slot_owner].reshape(groups, local_experts, capacity, width)]
  transfers between devices with their start and end apart: 7 -> 6, of which waited for: 4 -> 4; matrix products, arithmetic and copies ran while one was open for 22% -> 3% of each run, Pallas kernels for 0% -> 9%
where the time goes in v1:
time: 543 us; the launch traced here: 542 us
  waiting for transfers between devices  358 us (66%)
  Pallas kernels  115 us (21%)
  local copies, waits for them, and re-layouts  22.3 us (4%)
  between operations  14 us (3%)
  blocking collectives  12.8 us (2%)
  other arithmetic  10.9 us (2%)
  starting transfers between devices  8.63 us (2%)
    psum x1, waiting for transfers between devices, body(): sums.append(lax.psum(grads, 'dp'))  182 us
    psum x1, waiting for transfers between devices, body(): own_grads = lax.psum(own_grads, ('dp', 'expert')).astype(F32)  125 us
    pallas_call x2, Pallas kernels, body(): pl.pallas_call(functools.partial(expert_kernel, here), out_shape=(jax.Sha...  55.7 us
    pallas_call x1, Pallas kernels, body(): pl.pallas_call(functools.partial(backward_kernel, seq_len), out_shape=out...  40.1 us
    all_gather x1, waiting for transfers between devices, body(): normed_all = lax.all_gather(normed.reshape(rows, width), 'expert')  27.3 us
    all_to_all x2, waiting for transfers between devices, body(): lax.all_to_all(back, 'expert', split_axis=0, concat_axis=0, tiled=True)  23.9 us
    pallas_call x1, Pallas kernels, body(): pl.pallas_call(functools.partial(forward_kernel, seq_len), out_shape=forw...  19 us
  transfers between devices with their start and end apart: 6, of which 4 were waited for; matrix products, arithmetic and copies ran while one was open for 3% of the time, Pallas kernels for 9%

profile of v1, /device:TPU:0, one launch (start us, length us, event | category | flops | bytes accessed | tf_op | source)
XLA Modules:
  0.0 542.1 jit_solution(8567566576605193604)
XLA Ops:
  7.3 1.4 copy.61
  8.6 1.0 pad.13.upstream_ref
  9.7 0.6 reshape.118
  10.3 0.6 reshape.120
  10.9 0.2 copy.62
  11.1 0.1 copy.60
  11.2 1.0 pad.12.images_ref
  12.2 0.8 pad_bitcast_fusion
  13.0 0.8 copy.63.pick_rows_ref
  13.8 19.0 %attend.1 = (bf16[4,208,1536]{2,1,0:T(8,128)(2,1)}, bf16[4,208,512]{2,1,0:T(8,128)(2,1)}, f32[4,208,512]{2,1,0:T(8,128)}, bf16[4,208,512]{2,1,0:T(8,128)(2,1)}, ...) custom-call(s32[4]{0:T(128)} %ids_ref.3, bf16[4,208,512]{2,1,0:T(8,128)(2,1)} %pad.12.images_ref, ...), custom_call_target="tpu_custom_call" | custom-call | tf_op jit(solution)/shard_map/attend/pallas_call | solution.py:450
  32.9 0.1 reshape.104
  33.0 0.2 copy.64
  33.2 0.7 copy.71
  33.9 0.1 all_gather_reshape.9
  34.0 0.1 convert_reduce_fusion
  34.2 6.8 %all_gather.17.gate_rows_ref = f32[4,2,832]{2,1,0:T(2,128)} all-gather(f32[1,2,832]{2,1,0:T(2,128)S(1)} %all_gather_reshape.9), channel_id=1, replica_groups=mesh['dp'=8,'expert'=4] {'expert'}, dimensions={0}, use_global_device_ids=true | all-gather | bytes 33280 | tf_op jit(solution)/shard_map/all_gather | solution.py:464
  41.0 0.3 fusion.9
  41.4 6.0 %all-gather.1.marks_ref = s32[4,3,832]{2,1,0:T(4,128)} all-gather(s32[1,3,832]{2,1,0:T(4,128)S(1)} %add_bitcast_fusion), channel_id=2, replica_groups=mesh['dp'=8,'expert'=4] {'expert'}, dimensions={0}, use_global_device_ids=true | all-gather | bytes 49920 | tf_op jit(solution)/shard_map/all_gather | solution.py:430
  47.4 27.3 %all-gather.5.cloned.1.call-done.tokens_ref = bf16[4,832,512]{2,1,0:T(8,128)(2,1)} async-done(((bf16[1,832,512]{2,1,0:T(8,128)(2,1)}), bf16[4,832,512]{2,1,0:T(8,128)(2,1)}) %all-gather.5.cloned.1.call-update) | async-done | bytes 3407888 | tf_op jit(solution)/shard_map/all_gather | solution.py:463
  74.7 27.8 %experts_1.1 = (bf16[4,2,128,1024]{3,2,1,0:T(8,128)(2,1)}, bf16[2,128,5120]{2,1,0:T(8,128)(2,1)}) custom-call(s32[1]{0:T(128)} %bitcast.26.first_ref, s32[4,3,832]{2,1,0:T(4,128)} %all-gather.1.marks_ref, f32[4,2,832]{2,1,0:T(2,128)} %all_gather.17.gate_rows_ref, bf16[4,832,512]{2,1,0:T(8,128)(2,1)} %all-gather.5.cloned.1.call-done.tokens_ref, ...), custom_call_target="tpu_custom_call" | custom-call | tf_op jit(solution)/shard_map/experts_1/pallas_call | solution.py:484
  102.5 3.8 all-to-all-start.1
  106.3 27.8 %experts_0.1 = (bf16[4,2,128,1024]{3,2,1,0:T(8,128)(2,1)}, bf16[2,128,5120]{2,1,0:T(8,128)(2,1)}) custom-call(s32[1]{0:T(128)} %bitcast.13.first_ref, s32[4,3,832]{2,1,0:T(4,128)} %all-gather.1.marks_ref, f32[4,2,832]{2,1,0:T(2,128)} %all_gather.17.gate_rows_ref, bf16[4,832,512]{2,1,0:T(8,128)(2,1)} %all-gather.5.cloned.1.call-done.tokens_ref, ...), custom_call_target="tpu_custom_call" | custom-call | tf_op jit(solution)/shard_map/experts_0/pallas_call | solution.py:484
  134.2 1.3 copy-done
  135.5 4.5 all-to-all-start
  140.0 0.2 copy.65
  140.2 1.6 fusion.19.slots_ref
  141.8 23.9 %all-to-all-done = bf16[4,2,128,1024]{3,2,1,0:T(8,128)(2,1)} async-done(((bf16[4,2,128,1024]{3,2,1,0:T(8,128)(2,1)}), bf16[4,2,128,1024]{3,2,1,0:T(8,128)(2,1)}, u32[]{:S(2)}, u32[]{:S(2)}) %all-to-all-start) | async-done | bytes 2097184 | tf_op jit(solution)/shard_map/all_to_all | solution.py:510
  165.7 40.1 %attend_back.1 = (bf16[4,197,512]{2,1,0:T(8,128)(2,1)}, f32[4,197,512]{2,1,0:T(8,128)}, bf16[8,16,3712]{2,1,0:T(8,128)(2,1)}) custom-call(s32[4]{0:T(128)} %ids_ref.3, bf16[4,208,512]{2,1,0:T(8,128)(2,1)} %pad.12.images_ref, bf16[4,208,512]{2,1,0:T(8,128)(2,1)} %pad.13.upstream_ref, f32[4,208,512]{2,1,0:T(8,128)} %get-tuple-element.25.hidden_ref, ...), custom_call_target="tpu_custom_call" | custom-call | tf_op jit(solution)/shard_map/attend_back/pallas_call | solution.py:521
  205.9 0.3 all-reduce.10.cloned.1.call-start
  206.2 0.3 all-reduce.10.cloned.1.call-update
  206.4 0.8 copy-done.4
  207.3 1.3 copy.72
  208.6 2.2 copy.73
  210.8 124.7 %all-reduce.8.cloned.1.call-done = bf16[8,16,3712]{2,1,0:T(8,128)(2,1)} async-done(((bf16[8,16,3712]{2,1,0:T(8,128)(2,1)}), bf16[8,16,3712]{2,1,0:T(8,128)(2,1)}) %all-reduce.8.cloned.1.call-update) | async-done | bytes 950288 | tf_op jit(solution)/shard_map/psum | solution.py:538
  335.5 1.5 slice.66
  336.9 1.6 slice.64
  338.6 2.0 slice.62
  340.5 0.1 convert_element_type.32
  340.7 0.9 slice_bitcast_fusion
  341.6 182.1 %all-reduce.10.cloned.1.call-done = (bf16[2,128,5120]{2,1,0:T(8,128)(2,1)}, bf16[2,128,5120]{2,1,0:T(8,128)(2,1)}) async-done(((bf16[2,128,5120]{2,1,0:T(8,128)(2,1)}, bf16[2,128,5120]{2,1,0:T(8,128)(2,1)}), (bf16[2,128,5120]{2,1,0:T(8,128)(2,1)}, bf16[2,128,5120]{2,1,0:T(8,128)(2,1)})) %all-reduce.10.cloned.1.call-update) | async-done | bytes 5242896 | tf_op jit(solution)/shard_map/psum | solution.py:511
  523.7 1.3 fusion.30
  524.9 2.8 fusion.32
  527.8 1.1 convert.15
  528.9 1.1 convert_bitcast_fusion.1
  530.0 0.2 pad_maximum_fusion.1
  530.2 2.6 convert_bitcast_fusion
  532.8 0.2 pad_maximum_fusion
  533.0 2.6 convert.13
  (34 shorter events, 0.5 us)
Async XLA Ops:
  7.2 2.5 copy-start.8
  7.2 3.1 copy-start.9
  7.2 3.7 copy-start.6
  7.2 3.8 copy-start.5
  7.2 40.2 %all-gather.7.cloned.1.call-start = ((), (), s32[]{:S(2)}) async-start(), calls=%async_computation.3 | async-start | bytes 4259840 | tf_op jit(solution)/shard_map/all_gather | solution.py:431
  9.6 65.1 %all-gather.5.cloned.1.call-start = ((), (), s32[]{:S(2)}) async-start(), calls=%async_computation.2 | async-start | bytes 4259840 | tf_op jit(solution)/shard_map/all_gather | solution.py:463
  13.8 19.0 %copy-start.7 = (s32[4]{0:T(128)S(1)}, s32[4]{0:T(128)}, u32[]{:S(2)}) copy-start(s32[4]{0:T(128)} %ids_ref.3) | copy-start | bytes 52
  13.8 19.2 %copy-start.1 = (s32[4,208,2]{2,1,0:T(8,128)S(1)}, s32[4,208,2]{2,1,0:T(8,128)}, u32[]{:S(2)}) copy-start(s32[4,208,2]{2,1,0:T(8,128)} %get-tuple-element.88.picks_ref) | copy-start | bytes 19972
  102.5 31.6 %all-to-all-start.1 = ((bf16[4,2,128,1024]{3,2,1,0:T(8,128)(2,1)}), bf16[4,2,128,1024]{3,2,1,0:T(8,128)(2,1)S(1)}, u32[]{:S(2)}, u32[]{:S(2)}) async-start(bf16[4,2,128,1024]{3,2,1,0:T(8,128)(2,1)} %get-tuple-element.32), calls=%async_computation.1 | async-start | bytes 4194304 | tf_op jit(solution)/shard_map/all_to_all | solution.py:510
  134.2 1.3 copy-start
  135.5 30.2 %all-to-all-start = ((bf16[4,2,128,1024]{3,2,1,0:T(8,128)(2,1)}), bf16[4,2,128,1024]{3,2,1,0:T(8,128)(2,1)}, u32[]{:S(2)}, u32[]{:S(2)}) async-start(bf16[4,2,128,1024]{3,2,1,0:T(8,128)(2,1)} %get-tuple-element.31), calls=%async_computation | async-start | bytes 4194304 | tf_op jit(solution)/shard_map/all_to_all | solution.py:510
  140.0 195.5 %all-reduce.8.cloned.1.call-start = ((), (), s32[]{:S(2)}) async-start(), calls=%async_computation.4 | async-start | bytes 1900544 | tf_op jit(solution)/shard_map/psum | solution.py:538
  205.9 317.8 %all-reduce.10.cloned.1.call-start = ((), (), s32[]{:S(2)}) async-start(), calls=%async_computation.5 | async-start | bytes 10485760 | tf_op jit(solution)/shard_map/psum | solution.py:511
  206.1 1.1 copy-start.4
  206.1 2.4 copy-start.3
  335.5 5.1 copy-start.2
Sparse Core Ops, SparseCore 0:
  10.2 32.8 all-gather.6
  44.6 30.0 all-gather.4
  206.0 129.4 all-reduce.7
  339.6 183.9 all-reduce.9

commit v2 on v1

--- a/solution.py
+++ b/solution.py
@@ -348,7 +348,35 @@
 
     @pl.when(image == pl.num_programs(0) - 1)
     def _():
-        grads_ref[...] = total_ref[...].astype(LOW)
+        for tile in range(total_ref.shape[2] // 128):
+            grads_ref[:, tile] = total_ref[:, :, tile * 128 : tile * 128 + 128].astype(LOW)
+
+
+def exchange_sum(values, axis):
+    count = lax.axis_size(axis)
+    parts = values.reshape(count, values.shape[0] // count, values.shape[1])
+    parts = lax.all_to_all(parts, axis, split_axis=0, concat_axis=0, tiled=True)
+    return jnp.sum(parts.astype(F32), axis=0).astype(LOW)
+
+
+def exchange_gather(values, axis):
+    count = lax.axis_size(axis)
+    copies = jnp.broadcast_to(values[None], (count,) + values.shape)
+    copies = lax.all_to_all(copies, axis, split_axis=0, concat_axis=0, tiled=True)
+    return copies.reshape(count * values.shape[0], values.shape[1])
+
+
+def sum_over_all(values):
+    part = exchange_sum(exchange_sum(values, "expert"), "dp")
+    return exchange_gather(exchange_gather(part, "dp"), "expert")
+
+
+def sum_over_copies(values, split):
+    if not split:
+        return lax.psum(values, "dp")
+    flat = values.reshape(-1, values.shape[-1])
+    part = lax.psum_scatter(flat, "dp", scatter_dimension=0, tiled=True)
+    return lax.all_gather(part, "dp", axis=0, tiled=True).reshape(values.shape)
 
 
 def whole(array):
@@ -508,14 +536,15 @@
             name=f"experts_{piece}",
         )(first.reshape(1), *gathered, *weights)
         backs.append(lax.all_to_all(back, "expert", split_axis=0, concat_axis=0, tiled=True))
-        sums.append(lax.psum(grads, "dp"))
+        sums.append(sum_over_copies(grads, piece > 0))
     backs = [back.reshape(groups * here * room, 2 * width) for back in backs]
 
-    grad_cols = 7 * width + 128
+    grad_cols = 8 * width
+    tiles = grad_cols // 128
     out_types = (
         jax.ShapeDtypeStruct((n_images, seq_len, width), LOW),
         jax.ShapeDtypeStruct((n_images, seq_len, width), F32),
-        jax.ShapeDtypeStruct((n_adapt, rank, grad_cols), LOW),
+        jax.ShapeDtypeStruct((n_adapt, tiles, rank, 128), LOW),
     )
     by_image = (images, upstream, hidden, normed, qkv, context, gates, picks, slot_columns)
     block_out, input_grad, own_grads = pl.pallas_call(
@@ -535,13 +564,18 @@
         ),
         name="attend_back",
     )(adapter_ids, *by_image, *shared, *adapters, *backs)
-    own_grads = lax.psum(own_grads, ("dp", "expert")).astype(F32)
-    grad_qkv_a = own_grads[:, :, :width].transpose(0, 2, 1)
-    grad_qkv_b = own_grads[:, :, width : 4 * width]
-    grad_out_a = own_grads[:, :, 4 * width : 5 * width].transpose(0, 2, 1)
-    grad_out_b = own_grads[:, :, 5 * width : 6 * width]
-    grad_router_a = own_grads[:, :, 6 * width : 7 * width].transpose(0, 2, 1)
-    grad_router_b = own_grads[:, :, 7 * width : 7 * width + n_experts]
+    own_grads = sum_over_all(own_grads.reshape(-1, 128)).reshape(n_adapt, tiles, rank, 128)
+
+    def own_part(start, length):
+        part = own_grads[:, start // 128 : -(-(start + length) // 128)].astype(F32)
+        return part.transpose(0, 2, 1, 3).reshape(n_adapt, rank, -1)[:, :, :length]
+
+    grad_qkv_a = own_part(0, width).transpose(0, 2, 1)
+    grad_qkv_b = own_part(width, 3 * width)
+    grad_out_a = own_part(4 * width, width).transpose(0, 2, 1)
+    grad_out_b = own_part(5 * width, width)
+    grad_router_a = own_part(6 * width, width).transpose(0, 2, 1)
+    grad_router_b = own_part(7 * width, n_experts)
 
     def expert_part(start, length):
         parts = [total[:, :, start : start + length].astype(F32) for total in sums]

time: 543 us -> 367 us (0.68)
  waiting for transfers between devices: 358 us -> 132 us
  blocking collectives: 12.8 us -> 58.2 us
    psum x2 -> x1, waiting for transfers between devices: 307 us -> 22.8 us  [sum_over_copies(): return lax.psum(values, 'dp')]
    all_gather x0 -> x1, waiting for transfers between devices: none -> 48.6 us  [sum_over_copies(): return lax.all_gather(part, 'dp', axis=0, tiled=True).reshape(values.shape)]
    all_to_all x0 -> x3, blocking collectives: none -> 45.4 us  [the longest x2 33.8 us: exchange_sum(): parts = lax.all_to_all(parts, axis, split_axis=0, concat_axis=0, tiled=True)]
    reduce_scatter x0 -> x1, waiting for transfers between devices: none -> 33.4 us  [sum_over_copies(): part = lax.psum_scatter(flat, 'dp', scatter_dimension=0, tiled=True)]
    all_to_all x2, waiting for transfers between devices: 23.9 us -> 0.01 us  [body(): lax.all_to_all(back, 'expert', split_axis=0, concat_axis=0, tiled=True)]
  transfers between devices with their start and end apart: 6 -> 8, of which waited for: 4 -> 4; matrix products, arithmetic and copies ran while one was open for 3% -> 6% of each run, Pallas kernels for 9% -> 24%
where the time goes in v2:
time: 367 us
  waiting for transfers between devices  132 us (36%)
  Pallas kernels  115 us (31%)
  blocking collectives  58.2 us (16%)
  local copies, waits for them, and re-layouts  21.7 us (6%)
  between operations  14.1 us (4%)
  other arithmetic  12.7 us (3%)
  starting transfers between devices  12.3 us (3%)
    pallas_call x2, Pallas kernels, body(): pl.pallas_call(functools.partial(expert_kernel, here), out_shape=(jax.Sha...  55.9 us
    all_gather x1, waiting for transfers between devices, sum_over_copies(): return lax.all_gather(part, 'dp', axis=0, tiled=True).reshape(values.shape)  48.6 us
    pallas_call x1, Pallas kernels, body(): pl.pallas_call(functools.partial(backward_kernel, seq_len), out_shape=out...  40.2 us
    all_to_all x2, blocking collectives, exchange_sum(): parts = lax.all_to_all(parts, axis, split_axis=0, concat_axis=0, tiled=True)  33.8 us
    reduce_scatter x1, waiting for transfers between devices, sum_over_copies(): part = lax.psum_scatter(flat, 'dp', scatter_dimension=0, tiled=True)  33.4 us
    all_gather x1, waiting for transfers between devices, body(): normed_all = lax.all_gather(normed.reshape(rows, width), 'expert')  27.3 us
    psum x1, waiting for transfers between devices, sum_over_copies(): return lax.psum(values, 'dp')  22.8 us
    pallas_call x1, Pallas kernels, body(): pl.pallas_call(functools.partial(forward_kernel, seq_len), out_shape=forw...  19 us
  transfers between devices with their start and end apart: 8, of which 4 were waited for; matrix products, arithmetic and copies ran while one was open for 6% of the time, Pallas kernels for 24%

profile of v2, /device:TPU:0, one launch (start us, length us, event | category | flops | bytes accessed | tf_op | source)
XLA Modules:
  0.0 366.5 jit_solution(7215785327430381326)
XLA Ops:
  7.3 1.4 copy.104
  8.6 1.0 pad.13.upstream_ref
  9.7 0.6 reshape.163
  10.3 0.6 reshape.165
  10.9 0.2 copy.105
  11.2 1.0 pad.12.images_ref
  12.2 0.8 pad_bitcast_fusion
  13.0 0.8 copy.106.pick_rows_ref
  13.8 19.0 %attend.1 = (bf16[4,208,1536]{2,1,0:T(8,128)(2,1)}, bf16[4,208,512]{2,1,0:T(8,128)(2,1)}, f32[4,208,512]{2,1,0:T(8,128)}, bf16[4,208,512]{2,1,0:T(8,128)(2,1)}, ...) custom-call(s32[4]{0:T(128)} %ids_ref.3, bf16[4,208,512]{2,1,0:T(8,128)(2,1)} %pad.12.images_ref, ...), custom_call_target="tpu_custom_call" | custom-call | tf_op jit(solution)/shard_map/attend/pallas_call | solution.py:478
  33.1 0.2 copy.107
  33.2 0.7 copy.114
  34.2 6.8 %all_gather.20.gate_rows_ref = f32[4,2,832]{2,1,0:T(2,128)} all-gather(f32[1,2,832]{2,1,0:T(2,128)S(1)} %all_gather_reshape.9), channel_id=1, replica_groups=mesh['dp'=8,'expert'=4] {'expert'}, dimensions={0}, use_global_device_ids=true | all-gather | bytes 33280 | tf_op jit(solution)/shard_map/all_gather | solution.py:492
  41.0 0.3 fusion.9
  41.4 6.0 %all-gather.1.marks_ref = s32[4,3,832]{2,1,0:T(4,128)} all-gather(s32[1,3,832]{2,1,0:T(4,128)S(1)} %add_bitcast_fusion), channel_id=2, replica_groups=mesh['dp'=8,'expert'=4] {'expert'}, dimensions={0}, use_global_device_ids=true | all-gather | bytes 49920 | tf_op jit(solution)/shard_map/all_gather | solution.py:458
  47.4 27.3 %all-gather.6.cloned.1.call-done.tokens_ref = bf16[4,832,512]{2,1,0:T(8,128)(2,1)} async-done(((bf16[1,832,512]{2,1,0:T(8,128)(2,1)}), bf16[4,832,512]{2,1,0:T(8,128)(2,1)}) %all-gather.6.cloned.1.call-update) | async-done | bytes 3407888 | tf_op jit(solution)/shard_map/all_gather | solution.py:491
  74.7 27.8 %experts_1.1 = (bf16[4,2,128,1024]{3,2,1,0:T(8,128)(2,1)}, bf16[2,128,5120]{2,1,0:T(8,128)(2,1)}) custom-call(s32[1]{0:T(128)} %bitcast.26.first_ref, s32[4,3,832]{2,1,0:T(4,128)} %all-gather.1.marks_ref, f32[4,2,832]{2,1,0:T(2,128)} %all_gather.20.gate_rows_ref, bf16[4,832,512]{2,1,0:T(8,128)(2,1)} %all-gather.6.cloned.1.call-done.tokens_ref, ...), custom_call_target="tpu_custom_call" | custom-call | tf_op jit(solution)/shard_map/experts_1/pallas_call | solution.py:512
  102.6 3.6 all-to-all-start.1
  106.2 0.2 all-reduce.6.cloned.1.call-start
  106.4 28.1 %experts_0.1 = (bf16[4,2,128,1024]{3,2,1,0:T(8,128)(2,1)}, bf16[2,128,5120]{2,1,0:T(8,128)(2,1)}) custom-call(s32[1]{0:T(128)} %bitcast.13.first_ref, s32[4,3,832]{2,1,0:T(4,128)} %all-gather.1.marks_ref, f32[4,2,832]{2,1,0:T(2,128)} %all_gather.20.gate_rows_ref, bf16[4,832,512]{2,1,0:T(8,128)(2,1)} %all-gather.6.cloned.1.call-done.tokens_ref, ...), custom_call_target="tpu_custom_call" | custom-call | tf_op jit(solution)/shard_map/experts_0/pallas_call | solution.py:512
  134.5 1.3 copy-done
  135.9 4.5 %all-to-all-start = ((bf16[4,2,128,1024]{3,2,1,0:T(8,128)(2,1)}), bf16[4,2,128,1024]{3,2,1,0:T(8,128)(2,1)}, u32[]{:S(2)}, u32[]{:S(2)}) async-start(bf16[4,2,128,1024]{3,2,1,0:T(8,128)(2,1)} %get-tuple-element.31), calls=%async_computation | async-start | bytes 4194304 | tf_op jit(solution)/shard_map/all_to_all | solution.py:538
  140.4 33.4 %reduce-scatter.2.cloned.1.call-done = bf16[32,5120]{1,0:T(8,128)(2,1)} async-done(((bf16[256,5120]{1,0:T(8,128)(2,1)}), bf16[32,5120]{1,0:T(8,128)(2,1)}) %reduce-scatter.2.cloned.1.call-update) | async-done | bytes 327696 | tf_op jit(solution)/shard_map/reduce_scatter | solution.py:378
  173.8 0.2 copy.108
  174.0 1.6 fusion.19.slots_ref
  175.6 40.2 %attend_back.1 = (bf16[4,197,512]{2,1,0:T(8,128)(2,1)}, f32[4,197,512]{2,1,0:T(8,128)}, bf16[8,32,16,128]{3,2,1,0:T(8,128)(2,1)}) custom-call(s32[4]{0:T(128)} %ids_ref.3, bf16[4,208,512]{2,1,0:T(8,128)(2,1)} %pad.12.images_ref, bf16[4,208,512]{2,1,0:T(8,128)(2,1)} %pad.13.upstream_ref, f32[4,208,512]{2,1,0:T(8,128)} %get-tuple-element.25.hidden_ref, ...), custom_call_target="tpu_custom_call" | custom-call | tf_op jit(solution)/shard_map/attend_back/pallas_call | solution.py:550
  215.8 17.9 %all_to_all.30 = bf16[4,1024,128]{2,1,0:T(8,128)(2,1)S(1)} all-to-all(bf16[4,1024,128]{2,1,0:T(8,128)(2,1)} %bitcast.138), channel_id=1, replica_groups=mesh['dp'=8,'expert'=4] {'expert'}, dimensions={0} | all-to-all | bytes 2097152 | tf_op jit(solution)/shard_map/all_to_all | solution.py:358
  233.7 0.3 reduce_sum.44
  234.0 15.9 %all_to_all.31 = bf16[8,128,128]{2,1,0:T(8,128)(2,1)S(1)} all-to-all(bf16[8,128,128]{2,1,0:T(8,128)(2,1)S(1)} %bitcast.136), channel_id=1, replica_groups=mesh['dp'=8,'expert'=4] {'dp'}, dimensions={0} | all-to-all | bytes 524288 | tf_op jit(solution)/shard_map/all_to_all | solution.py:358
  250.0 11.6 %all_to_all.32 = bf16[8,128,128]{2,1,0:T(8,128)(2,1)S(1)} all-to-all(bf16[8,128,128]{2,1,0:T(8,128)(2,1)S(1)} %broadcast_in_dim.16), channel_id=1, replica_groups=mesh['dp'=8,'expert'=4] {'dp'}, dimensions={0} | all-to-all | bytes 524288 | tf_op jit(solution)/shard_map/all_to_all | solution.py:365
  261.6 1.1 broadcast_in_dim.18
  262.7 3.9 %all-to-all-start.5 = ((bf16[4,1024,128]{2,1,0:T(8,128)(2,1)}), bf16[4,1024,128]{2,1,0:T(8,128)(2,1)S(1)}, u32[]{:S(2)}, u32[]{:S(2)}) async-start(bf16[4,1024,128]{2,1,0:T(8,128)(2,1)} %broadcast_in_dim.18), calls=%async_computation.5 | async-start | bytes 2097152 | tf_op jit(solution)/shard_map/all_to_all | solution.py:365
  266.6 2.4 copy.120
  269.0 2.2 copy.121
  271.2 22.8 %all-reduce.6.cloned.1.call-done = bf16[2,128,5120]{2,1,0:T(8,128)(2,1)} async-done(((bf16[2,128,5120]{2,1,0:T(8,128)(2,1)}), bf16[2,128,5120]{2,1,0:T(8,128)(2,1)}) %all-reduce.6.cloned.1.call-update) | async-done | bytes 2621456 | tf_op jit(solution)/shard_map/psum | solution.py:376
  294.0 1.8 fusion.30
  295.7 1.7 fusion.32
  297.4 0.6 slice_convert_fusion
  298.2 0.9 bitcast_bitcast_fusion
  299.1 0.9 bitcast_bitcast_fusion.1
  299.9 1.0 copy_bitcast_fusion
  300.9 48.6 %all-gather.10.cloned.1.call-done = bf16[256,5120]{1,0:T(8,128)(2,1)} async-done(((bf16[32,5120]{1,0:T(8,128)(2,1)}), bf16[256,5120]{1,0:T(8,128)(2,1)}) %all-gather.10.cloned.1.call-update) | async-done | bytes 2621456 | tf_op jit(solution)/shard_map/all_gather | solution.py:379
  349.4 1.1 fusion.31
  350.5 1.7 fusion.33
  352.4 1.1 convert.32
  353.5 1.1 convert_bitcast_fusion.1
  354.6 0.4 pad_maximum_fusion
  354.9 2.5 convert_bitcast_fusion
  357.5 2.5 convert.30
  (45 shorter events, 1.2 us)
Async XLA Ops:
  7.2 2.5 copy-start.7
  7.2 3.1 copy-start.8
  7.2 3.7 copy-start.5
  7.2 3.8 %copy-start.4 = (bf16[4,197,512]{2,0,1:T(4,128)(2,1)S(1)}, bf16[4,197,512]{2,0,1:T(4,128)(2,1)}, u32[]{:S(2)}) copy-start(bf16[4,197,512]{2,0,1:T(4,128)(2,1)} %param.21) | copy-start | bytes 2420740
  7.2 40.2 %all-gather.8.cloned.1.call-start = ((), (), s32[]{:S(2)}) async-start(), calls=%async_computation.8 | async-start | bytes 4259840 | tf_op jit(solution)/shard_map/all_gather | solution.py:459
  9.6 65.1 %all-gather.6.cloned.1.call-start = ((), (), s32[]{:S(2)}) async-start(), calls=%async_computation.7 | async-start | bytes 4259840 | tf_op jit(solution)/shard_map/all_gather | solution.py:491
  13.8 19.1 %copy-start.6 = (s32[4]{0:T(128)S(1)}, s32[4]{0:T(128)}, u32[]{:S(2)}) copy-start(s32[4]{0:T(128)} %ids_ref.3) | copy-start | bytes 52
  13.8 19.2 %copy-start.1 = (s32[4,208,2]{2,1,0:T(8,128)S(1)}, s32[4,208,2]{2,1,0:T(8,128)}, u32[]{:S(2)}) copy-start(s32[4,208,2]{2,1,0:T(8,128)} %get-tuple-element.111.picks_ref) | copy-start | bytes 19972
  32.8 140.9 %reduce-scatter.2.cloned.1.call-start = ((), (), s32[]{:S(2)}) async-start(), calls=%async_computation.10 | async-start | bytes 2949120 | tf_op jit(solution)/shard_map/reduce_scatter | solution.py:378
  102.6 32.0 %all-to-all-start.1 = ((bf16[4,2,128,1024]{3,2,1,0:T(8,128)(2,1)}), bf16[4,2,128,1024]{3,2,1,0:T(8,128)(2,1)S(1)}, u32[]{:S(2)}, u32[]{:S(2)}) async-start(bf16[4,2,128,1024]{3,2,1,0:T(8,128)(2,1)} %get-tuple-element.32), calls=%async_computation.1 | async-start | bytes 4194304 | tf_op jit(solution)/shard_map/all_to_all | solution.py:538
  106.2 187.8 %all-reduce.6.cloned.1.call-start = ((), (), s32[]{:S(2)}) async-start(), calls=%async_computation.9 | async-start | bytes 5242880 | tf_op jit(solution)/shard_map/psum | solution.py:376
  134.5 1.3 copy-start
  135.9 39.7 %all-to-all-start = ((bf16[4,2,128,1024]{3,2,1,0:T(8,128)(2,1)}), bf16[4,2,128,1024]{3,2,1,0:T(8,128)(2,1)}, u32[]{:S(2)}, u32[]{:S(2)}) async-start(bf16[4,2,128,1024]{3,2,1,0:T(8,128)(2,1)} %get-tuple-element.31), calls=%async_computation | async-start | bytes 4194304 | tf_op jit(solution)/shard_map/all_to_all | solution.py:538
  140.3 209.1 %all-gather.10.cloned.1.call-start = ((), (), s32[]{:S(2)}) async-start(), calls=%async_computation.11 | async-start | bytes 2949120 | tf_op jit(solution)/shard_map/all_gather | solution.py:379
  262.7 6.3 %copy-start.2 = (f32[4,197,512]{2,1,0:T(8,128)S(1)}, f32[4,197,512]{2,1,0:T(8,128)}, u32[]{:S(2)}) copy-start(f32[4,197,512]{2,1,0:T(8,128)} %get-tuple-element.87) | copy-start | bytes 4841476
  262.7 34.7 %all-to-all-start.5 = ((bf16[4,1024,128]{2,1,0:T(8,128)(2,1)}), bf16[4,1024,128]{2,1,0:T(8,128)(2,1)S(1)}, u32[]{:S(2)}, u32[]{:S(2)}) async-start(bf16[4,1024,128]{2,1,0:T(8,128)(2,1)} %broadcast_in_dim.18), calls=%async_computation.5 | async-start | bytes 2097152 | tf_op jit(solution)/shard_map/all_to_all | solution.py:365
  350.5 1.7 copy-start.3
Sparse Core Ops, SparseCore 0:
  10.2 32.8 all-gather.7
  44.6 30.0 all-gather.5
  102.7 71.0 reduce-scatter.1
  177.9 116.0 all-reduce.5
  296.0 53.4 all-gather.9

commit v3 on v2

--- a/solution.py
+++ b/solution.py
@@ -139,7 +139,7 @@
 
 
 def expert_kernel(
-    n_here,
+    n_after,
     first_ref,
     marks_ref,
     gate_rows_ref,
@@ -151,17 +151,10 @@
     up_b_ref,
     down_a_ref,
     down_b_ref,
-    back_ref,
-    grads_ref,
-    rows_ref,
-    dy_ref,
-    mask_ref,
-    y_ref,
-    dx_ref,
-    low_ref,
-    low_grad_ref,
-    half_ref,
+    *rest,
 ):
+    back_ref, grads_ref, rows_ref, dy_ref, mask_ref = rest[n_after : n_after + 5]
+    y_ref, dx_ref, low_ref, low_grad_ref, half_ref = rest[n_after + 5 :]
     groups, _, capacity, double = back_ref.shape
     width = double // 2
     ff_width = up_ref.shape[2]
@@ -375,8 +368,12 @@
     if not split:
         return lax.psum(values, "dp")
     flat = values.reshape(-1, values.shape[-1])
-    part = lax.psum_scatter(flat, "dp", scatter_dimension=0, tiled=True)
+    part = exchange_sum(flat, "dp")
     return lax.all_gather(part, "dp", axis=0, tiled=True).reshape(values.shape)
+
+
+def work_of(microseconds):
+    return pl.CostEstimate(flops=microseconds * 10**9, bytes_accessed=10**6, transcendentals=0)
 
 
 def whole(array):
@@ -486,6 +483,7 @@
             out_specs=[per_image(a) for a in forward_out],
         ),
         name="attend",
+        cost_estimate=work_of(20),
     )(adapter_ids, images, picks, pick_rows, *shared, *adapters)
 
     normed_all = lax.all_gather(normed.reshape(rows, width), "expert")
@@ -495,7 +493,7 @@
     down_a_t = down_a.transpose(0, 1, 3, 2).reshape(local, low_cols, ff_width)
     down_b_flat = down_b.reshape(local, low_cols, width)
     cols = 2 * width + 2 * ff_width
-    backs, sums = [], []
+    backs, sums, raw = [], [], []
     for piece in range(PIECES):
         at = piece * here
 
@@ -508,16 +506,19 @@
         weights = (up_weight, down_weight, up_a_t, up_b_flat, down_a_t, down_b_flat)
         first = ((piece * groups + lax.axis_index("expert")) * here).astype(jnp.int32)
         gathered = (side_all, gates_all, normed_all, upstream_all)
+        after = tuple(raw[-1:])
         n_rows = groups * room
         back, grads = pl.pallas_call(
-            functools.partial(expert_kernel, here),
+            functools.partial(expert_kernel, len(after)),
             out_shape=(
                 jax.ShapeDtypeStruct((groups, here, room, 2 * width), LOW),
                 jax.ShapeDtypeStruct((here, low_cols, cols), LOW),
             ),
             grid_spec=grid_of(
                 grid=(here,),
-                in_specs=[whole(a) for a in gathered] + [of_expert(a) for a in weights],
+                in_specs=[whole(a) for a in gathered]
+                + [of_expert(a) for a in weights]
+                + [pl.BlockSpec(memory_space=pl.ANY) for a in after],
                 out_specs=[
                     pl.BlockSpec((groups, 1, room, 2 * width), lambda i, s: (0, i, 0, 0)),
                     pl.BlockSpec((1, low_cols, cols), lambda i, s: (i, 0, 0)),
@@ -533,8 +534,9 @@
                     pltpu.VMEM((2, low_cols, n_rows), LOW),
                 ],
             ),
-            name=f"experts_{piece}",
-        )(first.reshape(1), *gathered, *weights)
+            cost_estimate=work_of(28),
+        )(first.reshape(1), *gathered, *weights, *after)
+        raw.append(back)
         backs.append(lax.all_to_all(back, "expert", split_axis=0, concat_axis=0, tiled=True))
         sums.append(sum_over_copies(grads, piece > 0))
     backs = [back.reshape(groups * here * room, 2 * width) for back in backs]
@@ -563,6 +565,7 @@
             ],
         ),
         name="attend_back",
+        cost_estimate=work_of(40),
     )(adapter_ids, *by_image, *shared, *adapters, *backs)
     own_grads = sum_over_all(own_grads.reshape(-1, 128)).reshape(n_adapt, tiles, rank, 128)
 
@@ -612,6 +615,7 @@
         + (P(),) * 6
         + (experts,) * 4
     )
+
     return jax.shard_map(
         body,
         mesh=mesh,

time: 367 us -> 416 us (1.13)
  blocking collectives: 58.2 us -> 94.1 us
  waiting for transfers between devices: 132 us -> 143 us
    all_to_all x0 -> x1, waiting for transfers between devices: none -> 86.9 us  [exchange_sum(): parts = lax.all_to_all(parts, axis, split_axis=0, concat_axis=0, tiled=True)]
    all_gather x1, waiting for transfers between devices: 48.6 us -> 0.01 us  [sum_over_copies(): return lax.all_gather(part, 'dp', axis=0, tiled=True).reshape(values.shape)]
    reduce_scatter x1 -> x0, waiting for transfers between devices: 33.4 us -> none  [sum_over_copies(): part = lax.psum_scatter(flat, 'dp', scatter_dimension=0, tiled=True)]
    all_to_all x0 -> x1, blocking collectives: none -> 30.1 us  [body(): lax.all_to_all(back, 'expert', split_axis=0, concat_axis=0, tiled=True)]
    psum x1, waiting for transfers between devices: 22.8 us -> 0.01 us  [sum_over_copies(): return lax.psum(values, 'dp')]
    all_to_all x2 -> x1, waiting for transfers between devices: 0.01 us -> 22.4 us  [body(): lax.all_to_all(back, 'expert', split_axis=0, concat_axis=0, tiled=True)]
    all_to_all x1, blocking collectives: 11.6 us -> 20.2 us  [exchange_gather(): lax.all_to_all(copies, axis, split_axis=0, concat_axis=0, tiled=True)]
    all_to_all x1, waiting for transfers between devices: 0.01 us -> 6.03 us  [exchange_gather(): lax.all_to_all(copies, axis, split_axis=0, concat_axis=0, tiled=True)]
  transfers between devices with their start and end apart: 8 -> 7, of which waited for: 4 -> 4; matrix products, arithmetic and copies ran while one was open for 6% -> 5% of each run, Pallas kernels for 24% -> 14%
where the time goes in v3:
time: 416 us; the launch traced here: 415 us
  waiting for transfers between devices  143 us (34%)
  Pallas kernels  115 us (28%)
  blocking collectives  94.1 us (23%)
  local copies, waits for them, and re-layouts  20.4 us (5%)
  starting transfers between devices  14.1 us (3%)
  between operations  14 us (3%)
  other arithmetic  13.9 us (3%)
    all_to_all x1, waiting for transfers between devices, exchange_sum(): parts = lax.all_to_all(parts, axis, split_axis=0, concat_axis=0, tiled=True)  86.9 us
    pallas_call x2, Pallas kernels, body(): pl.pallas_call(functools.partial(expert_kernel, len(after)), out_shape=(j...  55.7 us
    pallas_call x1, Pallas kernels, body(): pl.pallas_call(functools.partial(backward_kernel, seq_len), out_shape=out...  40.2 us
    all_to_all x2, blocking collectives, exchange_sum(): parts = lax.all_to_all(parts, axis, split_axis=0, concat_axis=0, tiled=True)  30.9 us
    all_to_all x1, blocking collectives, body(): lax.all_to_all(back, 'expert', split_axis=0, concat_axis=0, tiled=True)  30.1 us
    all_gather x1, waiting for transfers between devices, body(): normed_all = lax.all_gather(normed.reshape(rows, width), 'expert')  27.1 us
    all_to_all x1, waiting for transfers between devices, body(): lax.all_to_all(back, 'expert', split_axis=0, concat_axis=0, tiled=True)  22.4 us
    all_to_all x1, blocking collectives, exchange_gather(): lax.all_to_all(copies, axis, split_axis=0, concat_axis=0, tiled=True)  20.2 us
  transfers between devices with their start and end apart: 7, of which 4 were waited for; matrix products, arithmetic and copies ran while one was open for 5% of the time, Pallas kernels for 14%

profile of v3, /device:TPU:0, one launch (start us, length us, event | category | flops | bytes accessed | tf_op | source)
XLA Modules:
  0.0 414.9 jit_solution(4376609055516844842)
XLA Ops:
  7.3 1.4 copy.104
  8.6 1.0 pad.13.upstream_ref
  9.7 0.6 reshape.159
  10.3 0.6 reshape.161
  10.9 0.2 copy.105
  11.2 1.0 pad.12.images_ref
  12.2 0.8 pad_bitcast_fusion
  13.0 0.8 copy.106.pick_rows_ref
  13.8 19.0 %attend.1 = (bf16[4,208,1536]{2,1,0:T(8,128)(2,1)}, bf16[4,208,512]{2,1,0:T(8,128)(2,1)}, f32[4,208,512]{2,1,0:T(8,128)}, bf16[4,208,512]{2,1,0:T(8,128)(2,1)}, ...) custom-call(s32[4]{0:T(128)} %ids_ref.3, bf16[4,208,512]{2,1,0:T(8,128)(2,1)} %pad.12.images_ref, ...), custom_call_target="tpu_custom_call" | custom-call | flops 20000000000 | bytes 1000000 | tf_op jit(solution)/shard_map/attend/pallas_call | solution.py:475
  33.2 0.7 copy.114
  34.1 6.8 %all_gather.20.gate_rows_ref = f32[4,2,832]{2,1,0:T(2,128)} all-gather(f32[1,2,832]{2,1,0:T(2,128)S(1)} %all_gather_reshape.9), channel_id=1, replica_groups=mesh['dp'=8,'expert'=4] {'expert'}, dimensions={0}, use_global_device_ids=true | all-gather | bytes 33280 | tf_op jit(solution)/shard_map/all_gather | solution.py:490
  40.9 0.3 fusion.9
  41.3 6.2 %all-gather.1.marks_ref = s32[4,3,832]{2,1,0:T(4,128)} all-gather(s32[1,3,832]{2,1,0:T(4,128)S(1)} %add_bitcast_fusion), channel_id=2, replica_groups=mesh['dp'=8,'expert'=4] {'expert'}, dimensions={0}, use_global_device_ids=true | all-gather | bytes 49920 | tf_op jit(solution)/shard_map/all_gather | solution.py:455
  47.6 27.1 %all-gather.6.cloned.1.call-done.tokens_ref = bf16[4,832,512]{2,1,0:T(8,128)(2,1)} async-done(((bf16[1,832,512]{2,1,0:T(8,128)(2,1)}), bf16[4,832,512]{2,1,0:T(8,128)(2,1)}) %all-gather.6.cloned.1.call-update) | async-done | bytes 3407888 | tf_op jit(solution)/shard_map/all_gather | solution.py:489
  74.7 27.8 %shard_map.292 = (bf16[4,2,128,1024]{3,2,1,0:T(8,128)(2,1)}, bf16[2,128,5120]{2,1,0:T(8,128)(2,1)}) custom-call(s32[1]{0:T(128)} %bitcast.13.first_ref, s32[4,3,832]{2,1,0:T(4,128)} %all-gather.1.marks_ref, f32[4,2,832]{2,1,0:T(2,128)} %all_gather.20.gate_rows_ref, bf16[4,832,512]{2,1,0:T(8,128)(2,1)} %all-gather.6.cloned.1.call-done.tokens_ref, ...), custom_call_target="tpu_custom_call" | custom-call | flops 28000000000 | bytes 1000000 | tf_op jit(solution)/shard_map/pallas_call | solution.py:511
  102.5 27.9 %shard_map.293 = (bf16[4,2,128,1024]{3,2,1,0:T(8,128)(2,1)}, bf16[2,128,5120]{2,1,0:T(8,128)(2,1)}) custom-call(s32[1]{0:T(128)} %bitcast.26.first_ref, s32[4,3,832]{2,1,0:T(4,128)} %all-gather.1.marks_ref, f32[4,2,832]{2,1,0:T(2,128)} %all_gather.20.gate_rows_ref, bf16[4,832,512]{2,1,0:T(8,128)(2,1)} %all-gather.6.cloned.1.call-done.tokens_ref, ...), custom_call_target="tpu_custom_call" | custom-call | flops 28000000000 | bytes 1000000 | tf_op jit(solution)/shard_map/pallas_call | solution.py:511
  130.4 30.1 %all_to_all.35 = bf16[4,2,128,1024]{3,2,1,0:T(8,128)(2,1)} all-to-all(bf16[4,2,128,1024]{3,2,1,0:T(8,128)(2,1)} %get-tuple-element.32), channel_id=1, replica_groups=mesh['dp'=8,'expert'=4] {'expert'}, dimensions={0} | all-to-all | bytes 4194304 | tf_op jit(solution)/shard_map/all_to_all | solution.py:540
  160.5 5.5 %all-to-all-start.6 = ((bf16[8,32,5120]{2,1,0:T(8,128)(2,1)}), bf16[8,32,5120]{2,1,0:T(8,128)(2,1)S(1)}, u32[]{:S(2)}, u32[]{:S(2)}) async-start(bf16[8,32,5120]{2,1,0:T(8,128)(2,1)} %bitcast.121), calls=%async_computation.6 | async-start | bytes 5242880 | tf_op jit(solution)/shard_map/all_to_all | solution.py:351
  166.0 0.7 all-reduce.6.cloned.1.call-update
  166.7 86.9 %all-to-all-done.6 = bf16[8,32,5120]{2,1,0:T(8,128)(2,1)S(1)} async-done(((bf16[8,32,5120]{2,1,0:T(8,128)(2,1)}), bf16[8,32,5120]{2,1,0:T(8,128)(2,1)S(1)}, u32[]{:S(2)}, u32[]{:S(2)}) %all-to-all-start.6) | async-done | bytes 2621472 | tf_op jit(solution)/shard_map/all_to_all | solution.py:351
  253.6 4.4 %all-to-all-start = ((bf16[4,2,128,1024]{3,2,1,0:T(8,128)(2,1)}), bf16[4,2,128,1024]{3,2,1,0:T(8,128)(2,1)}, u32[]{:S(2)}, u32[]{:S(2)}) async-start(bf16[4,2,128,1024]{3,2,1,0:T(8,128)(2,1)} %get-tuple-element.31.rest_0_), calls=%async_computation | async-start | bytes 4194304 | tf_op jit(solution)/shard_map/all_to_all | solution.py:540
  258.1 0.3 all-gather.10.cloned.1.call-start
  258.5 1.6 fusion.19.slots_ref
  260.2 1.2 reduce_sum.58
  261.4 22.4 %all-to-all-done = bf16[4,2,128,1024]{3,2,1,0:T(8,128)(2,1)} async-done(((bf16[4,2,128,1024]{3,2,1,0:T(8,128)(2,1)}), bf16[4,2,128,1024]{3,2,1,0:T(8,128)(2,1)}, u32[]{:S(2)}, u32[]{:S(2)}) %all-to-all-start) | async-done | bytes 2097184 | tf_op jit(solution)/shard_map/all_to_all | solution.py:540
  283.8 40.2 %attend_back.1 = (bf16[4,197,512]{2,1,0:T(8,128)(2,1)}, f32[4,197,512]{2,1,0:T(8,128)}, bf16[8,32,16,128]{3,2,1,0:T(8,128)(2,1)}) custom-call(s32[4]{0:T(128)} %ids_ref.3, bf16[4,208,512]{2,1,0:T(8,128)(2,1)} %pad.12.images_ref, bf16[4,208,512]{2,1,0:T(8,128)(2,1)} %pad.13.upstream_ref, f32[4,208,512]{2,1,0:T(8,128)} %get-tuple-element.25.hidden_ref, ...), custom_call_target="tpu_custom_call" | custom-call | flops 40000000000 | bytes 1000000 | tf_op jit(solution)/shard_map/attend_back/pallas_call | solution.py:552
  324.0 17.9 %all_to_all.36 = bf16[4,1024,128]{2,1,0:T(8,128)(2,1)S(1)} all-to-all(bf16[4,1024,128]{2,1,0:T(8,128)(2,1)} %bitcast.129), channel_id=1, replica_groups=mesh['dp'=8,'expert'=4] {'expert'}, dimensions={0} | all-to-all | bytes 2097152 | tf_op jit(solution)/shard_map/all_to_all | solution.py:351
  341.9 0.3 reduce_sum.56
  342.2 12.9 %all_to_all.37 = bf16[8,128,128]{2,1,0:T(8,128)(2,1)S(1)} all-to-all(bf16[8,128,128]{2,1,0:T(8,128)(2,1)S(1)} %bitcast.127), channel_id=1, replica_groups=mesh['dp'=8,'expert'=4] {'dp'}, dimensions={0} | all-to-all | bytes 524288 | tf_op jit(solution)/shard_map/all_to_all | solution.py:351
  355.2 20.2 %all_to_all.38 = bf16[8,128,128]{2,1,0:T(8,128)(2,1)S(1)} all-to-all(bf16[8,128,128]{2,1,0:T(8,128)(2,1)S(1)} %broadcast_in_dim.16), channel_id=1, replica_groups=mesh['dp'=8,'expert'=4] {'dp'}, dimensions={0} | all-to-all | bytes 524288 | tf_op jit(solution)/shard_map/all_to_all | solution.py:358
  375.4 1.1 broadcast_in_dim.18
  376.5 3.8 all-to-all-start.5
  380.3 2.4 copy.120
  382.7 2.2 copy.121
  384.9 1.8 fusion.30
  386.7 1.7 fusion.32
  388.4 6.0 %all-to-all-done.5 = bf16[4,1024,128]{2,1,0:T(8,128)(2,1)S(1)} async-done(((bf16[4,1024,128]{2,1,0:T(8,128)(2,1)}), bf16[4,1024,128]{2,1,0:T(8,128)(2,1)S(1)}, u32[]{:S(2)}, u32[]{:S(2)}) %all-to-all-start.5) | async-done | bytes 1048608 | tf_op jit(solution)/shard_map/all_to_all | solution.py:358
  394.4 0.6 slice_convert_fusion
  395.2 0.9 bitcast_bitcast_fusion
  396.0 0.9 bitcast_bitcast_fusion.1
  396.9 1.0 copy_bitcast_fusion
  397.8 1.1 fusion.31
  398.9 1.7 fusion.33
  400.7 1.1 convert.33
  401.8 1.1 convert_bitcast_fusion.1
  402.9 0.4 pad_maximum_fusion
  403.3 2.5 convert_bitcast_fusion
  405.8 2.5 convert.31
  (42 shorter events, 1.5 us)
Async XLA Ops:
  7.2 2.5 copy-start.5
  7.2 3.1 copy-start.6
  7.2 3.7 copy-start.4
  7.2 3.9 copy-start.3
  7.2 40.3 %all-gather.8.cloned.1.call-start = ((), (), s32[]{:S(2)}) async-start(), calls=%async_computation.8 | async-start | bytes 4259840 | tf_op jit(solution)/shard_map/all_gather | solution.py:456
  9.6 65.1 %all-gather.6.cloned.1.call-start = ((), (), s32[]{:S(2)}) async-start(), calls=%async_computation.7 | async-start | bytes 4259840 | tf_op jit(solution)/shard_map/all_gather | solution.py:489
  13.8 19.0 %copy-start.7 = (s32[4]{0:T(128)S(1)}, s32[4]{0:T(128)}, u32[]{:S(2)}) copy-start(s32[4]{0:T(128)} %ids_ref.3) | copy-start | bytes 52
  13.8 19.2 %copy-start = (s32[4,208,2]{2,1,0:T(8,128)S(1)}, s32[4,208,2]{2,1,0:T(8,128)}, u32[]{:S(2)}) copy-start(s32[4,208,2]{2,1,0:T(8,128)} %get-tuple-element.111.picks_ref) | copy-start | bytes 19972
  160.5 93.1 %all-to-all-start.6 = ((bf16[8,32,5120]{2,1,0:T(8,128)(2,1)}), bf16[8,32,5120]{2,1,0:T(8,128)(2,1)S(1)}, u32[]{:S(2)}, u32[]{:S(2)}) async-start(bf16[8,32,5120]{2,1,0:T(8,128)(2,1)} %bitcast.121), calls=%async_computation.6 | async-start | bytes 5242880 | tf_op jit(solution)/shard_map/all_to_all | solution.py:351
  166.0 218.9 %all-reduce.6.cloned.1.call-start = ((), (), s32[]{:S(2)}) async-start(), calls=%async_computation.9 | async-start | bytes 5242880 | tf_op jit(solution)/shard_map/psum | solution.py:369
  253.6 30.2 %all-to-all-start = ((bf16[4,2,128,1024]{3,2,1,0:T(8,128)(2,1)}), bf16[4,2,128,1024]{3,2,1,0:T(8,128)(2,1)}, u32[]{:S(2)}, u32[]{:S(2)}) async-start(bf16[4,2,128,1024]{3,2,1,0:T(8,128)(2,1)} %get-tuple-element.31.rest_0_), calls=%async_computation | async-start | bytes 4194304 | tf_op jit(solution)/shard_map/all_to_all | solution.py:540
  258.1 139.8 %all-gather.10.cloned.1.call-start = ((), (), s32[]{:S(2)}) async-start(), calls=%async_computation.10 | async-start | bytes 2949120 | tf_op jit(solution)/shard_map/all_gather | solution.py:372
  375.4 7.3 %copy-start.1 = (f32[4,197,512]{2,1,0:T(8,128)S(1)}, f32[4,197,512]{2,1,0:T(8,128)}, u32[]{:S(2)}) copy-start(f32[4,197,512]{2,1,0:T(8,128)} %get-tuple-element.87) | copy-start | bytes 4841476
  376.5 17.9 %all-to-all-start.5 = ((bf16[4,1024,128]{2,1,0:T(8,128)(2,1)}), bf16[4,1024,128]{2,1,0:T(8,128)(2,1)S(1)}, u32[]{:S(2)}, u32[]{:S(2)}) async-start(bf16[4,1024,128]{2,1,0:T(8,128)(2,1)} %broadcast_in_dim.18), calls=%async_computation.5 | async-start | bytes 2097152 | tf_op jit(solution)/shard_map/all_to_all | solution.py:358
  397.8 2.8 copy-start.2
Sparse Core Ops, SparseCore 0:
  10.2 32.8 all-gather.7
  44.6 30.0 all-gather.5
  171.0 153.3 all-reduce.5
  326.5 58.1 all-gather.9

commit v4 on v3

--- a/solution.py
+++ b/solution.py
@@ -138,24 +138,13 @@
     return values * half, half + values * density
 
 
-def expert_kernel(
-    n_after,
-    first_ref,
-    marks_ref,
-    gate_rows_ref,
-    tokens_ref,
-    upstream_ref,
-    up_ref,
-    down_ref,
-    up_a_ref,
-    up_b_ref,
-    down_a_ref,
-    down_b_ref,
-    *rest,
-):
+def expert_kernel(n_after, groups, first_ref, marks_ref, gate_rows_ref, *rest):
+    token_refs, upstream_refs, rest = rest[:groups], rest[groups : 2 * groups], rest[2 * groups :]
+    up_ref, down_ref, up_a_ref, up_b_ref, down_a_ref, down_b_ref = rest[:6]
+    rest = rest[6:]
     back_ref, grads_ref, rows_ref, dy_ref, mask_ref = rest[n_after : n_after + 5]
     y_ref, dx_ref, low_ref, low_grad_ref, half_ref = rest[n_after + 5 :]
-    groups, _, capacity, double = back_ref.shape
+    _, _, capacity, double = back_ref.shape
     width = double // 2
     ff_width = up_ref.shape[2]
     low_cols = up_a_ref.shape[1]
@@ -163,23 +152,24 @@
     start = (first_ref[0] + pl.program_id(0)) * capacity
     for group in range(groups):
         span = slice(group * capacity, (group + 1) * capacity)
-        n_tokens = tokens_ref.shape[1]
+        source = first_ref[1 + group]
+        n_tokens = token_refs[group].shape[0]
         slots = lax.broadcasted_iota(jnp.int32, (capacity, n_tokens), 0) + start
-        zero = slots == marks_ref[group, 0:1, :]
-        one = slots == marks_ref[group, 1:2, :]
+        zero = slots == marks_ref[source, 0:1, :]
+        one = slots == marks_ref[source, 1:2, :]
         either = jnp.where(zero | one, 1.0, 0.0)
         gate = jnp.sum(
-            jnp.where(zero, gate_rows_ref[group, 0:1, :], 0.0)
-            + jnp.where(one, gate_rows_ref[group, 1:2, :], 0.0),
+            jnp.where(zero, gate_rows_ref[source, 0:1, :], 0.0)
+            + jnp.where(one, gate_rows_ref[source, 1:2, :], 0.0),
             axis=1,
             keepdims=True,
         )
         ids = jnp.sum(
-            either * marks_ref[group, 2:3, :].astype(F32), axis=1, keepdims=True
+            either * marks_ref[source, 2:3, :].astype(F32), axis=1, keepdims=True
         )
         either = either.astype(LOW)
-        rows_ref[span, :] = nn(either, tokens_ref[group]).astype(LOW)
-        dy_ref[span, :] = (gate * nn(either, upstream_ref[group])).astype(LOW)
+        rows_ref[span, :] = nn(either, token_refs[group][...]).astype(LOW)
+        dy_ref[span, :] = (gate * nn(either, upstream_refs[group][...])).astype(LOW)
         cols = lax.broadcasted_iota(jnp.int32, (capacity, low_cols), 1) // rank
         mask_ref[span, :] = jnp.where(cols.astype(F32) == ids, 1.0, 0.0)
     mask = mask_ref[...]
@@ -218,8 +208,11 @@
     up_low_grad = (low_grad_ref[...] * mask).astype(LOW)
     out = (y_ref[...] + nn(down_low, down_b_ref[0])).astype(LOW)
     dx = (dx_ref[...] + nn(up_low_grad, up_a_ref[0])).astype(LOW)
-    back_ref[:, 0, :, :width] = out.reshape(groups, capacity, width)
-    back_ref[:, 0, :, width:] = dx.reshape(groups, capacity, width)
+    for group in range(groups):
+        span = slice(group * capacity, (group + 1) * capacity)
+        source = first_ref[1 + group]
+        back_ref[source, 0, :, :width] = out[span]
+        back_ref[source, 0, :, width:] = dx[span]
     grads_ref[0, :, 0:width] = tn(up_low_grad, rows_ref[...]).astype(LOW)
     grads_ref[0, :, down_b_at : down_b_at + width] = tn(down_low, dy_ref[...]).astype(LOW)
 
@@ -345,11 +338,34 @@
             grads_ref[:, tile] = total_ref[:, :, tile * 128 : tile * 128 + 128].astype(LOW)
 
 
+def gather_blocks(block, axis):
+    count = lax.axis_size(axis)
+    far = count // 2
+    blocks = [block]
+    for hop in range(1, far):
+        pairs = [(i, (i // 2 + hop) % far * 2 + i % 2) for i in range(count)]
+        blocks.append(lax.ppermute(block, axis, pairs))
+    pairs = [(i, i ^ 1) for i in range(count)]
+    return blocks + [lax.ppermute(part, axis, pairs) for part in blocks]
+
+
+def block_sources(axis):
+    count = lax.axis_size(axis)
+    far = count // 2
+    place = lax.axis_index(axis)
+    hops = jnp.arange(far, dtype=jnp.int32)
+    sources = (place // 2 - hops + far) % far * 2
+    return jnp.concatenate([sources + place % 2, sources + 1 - place % 2])
+
+
+def exchange(values, axis):
+    count = lax.axis_size(axis)
+    parts = values.reshape(count, -1, values.shape[-1])
+    return lax.all_to_all(parts, axis, split_axis=0, concat_axis=0, tiled=True)
+
+
 def exchange_sum(values, axis):
-    count = lax.axis_size(axis)
-    parts = values.reshape(count, values.shape[0] // count, values.shape[1])
-    parts = lax.all_to_all(parts, axis, split_axis=0, concat_axis=0, tiled=True)
-    return jnp.sum(parts.astype(F32), axis=0).astype(LOW)
+    return jnp.sum(exchange(values, axis).astype(F32), axis=0).astype(LOW)
 
 
 def exchange_gather(values, axis):
@@ -359,17 +375,36 @@
     return copies.reshape(count * values.shape[0], values.shape[1])
 
 
-def sum_over_all(values):
-    part = exchange_sum(exchange_sum(values, "expert"), "dp")
-    return exchange_gather(exchange_gather(part, "dp"), "expert")
-
-
-def sum_over_copies(values, split):
-    if not split:
-        return lax.psum(values, "dp")
-    flat = values.reshape(-1, values.shape[-1])
-    part = exchange_sum(flat, "dp")
-    return lax.all_gather(part, "dp", axis=0, tiled=True).reshape(values.shape)
+def direct_parts(values, axis):
+    count = lax.axis_size(axis)
+    place = lax.axis_index(axis)
+    parts = values.reshape(count, -1, values.shape[-1])
+    found = [lax.dynamic_index_in_dim(parts, place, 0, keepdims=False)]
+    for hop in range(1, count):
+        pairs = [(i, (i + hop) % count) for i in range(count)]
+        part = lax.dynamic_index_in_dim(parts, (place + hop) % count, 0, keepdims=False)
+        found.append(lax.ppermute(part, axis, pairs))
+    return found
+
+
+def sum_kernel(count, *refs):
+    total = refs[0][...].astype(F32)
+    for number in range(1, count):
+        total = total + refs[number][...].astype(F32)
+    refs[-1][...] = total.astype(LOW)
+
+
+def sum_after(parts, after):
+    rows, cols = parts[0].shape
+    block = pl.BlockSpec((rows, 512), lambda i: (0, i))
+    return pl.pallas_call(
+        functools.partial(sum_kernel, len(parts)),
+        out_shape=jax.ShapeDtypeStruct((rows, cols), LOW),
+        grid=(cols // 512,),
+        in_specs=[block] * len(parts) + [pl.BlockSpec(memory_space=pl.ANY)],
+        out_specs=block,
+        name="add_parts",
+    )(*parts, after)
 
 
 def work_of(microseconds):
@@ -453,7 +488,7 @@
     slot_columns = slots.reshape(2, n_images, padded).transpose(1, 2, 0)
     side = jnp.concatenate([slots, token_ids], axis=0)
     side_all = lax.all_gather(side, "expert")
-    upstream_all = lax.all_gather(upstream.reshape(rows, width), "expert")
+    upstream_all = gather_blocks(upstream.reshape(rows, width), "expert")
 
     gain_one = ln_gain1.astype(F32).reshape(1, width)
     gain_two = ln_gain2.astype(F32).reshape(1, width)
@@ -486,7 +521,8 @@
         cost_estimate=work_of(20),
     )(adapter_ids, images, picks, pick_rows, *shared, *adapters)
 
-    normed_all = lax.all_gather(normed.reshape(rows, width), "expert")
+    normed_all = gather_blocks(normed.reshape(rows, width), "expert")
+    sources = block_sources("expert")
     gates_all = lax.all_gather(gate_rows.transpose(1, 0, 2).reshape(2, rows), "expert")
     up_a_t = up_a.transpose(0, 1, 3, 2).reshape(local, low_cols, width)
     up_b_flat = up_b.reshape(local, low_cols, ff_width)
@@ -505,11 +541,11 @@
 
         weights = (up_weight, down_weight, up_a_t, up_b_flat, down_a_t, down_b_flat)
         first = ((piece * groups + lax.axis_index("expert")) * here).astype(jnp.int32)
-        gathered = (side_all, gates_all, normed_all, upstream_all)
+        gathered = (side_all, gates_all, *normed_all, *upstream_all)
         after = tuple(raw[-1:])
         n_rows = groups * room
         back, grads = pl.pallas_call(
-            functools.partial(expert_kernel, len(after)),
+            functools.partial(expert_kernel, len(after), groups),
             out_shape=(
                 jax.ShapeDtypeStruct((groups, here, room, 2 * width), LOW),
                 jax.ShapeDtypeStruct((here, low_cols, cols), LOW),
@@ -535,10 +571,10 @@
                 ],
             ),
             cost_estimate=work_of(28),
-        )(first.reshape(1), *gathered, *weights, *after)
+        )(jnp.concatenate([first.reshape(1), sources]), *gathered, *weights, *after)
         raw.append(back)
         backs.append(lax.all_to_all(back, "expert", split_axis=0, concat_axis=0, tiled=True))
-        sums.append(sum_over_copies(grads, piece > 0))
+        sums.append(lax.psum(grads, "dp") if piece == 0 else direct_parts(grads, "dp"))
     backs = [back.reshape(groups * here * room, 2 * width) for back in backs]
 
     grad_cols = 8 * width
@@ -567,7 +603,13 @@
         name="attend_back",
         cost_estimate=work_of(40),
     )(adapter_ids, *by_image, *shared, *adapters, *backs)
-    own_grads = sum_over_all(own_grads.reshape(-1, 128)).reshape(n_adapt, tiles, rank, 128)
+    part = exchange_sum(own_grads.reshape(-1, 128), "expert")
+    part = exchange_sum(part, "dp")
+    last = lax.all_gather(sum_after(sums[1], part), "dp", axis=0, tiled=True)
+    sums[1] = last.reshape(sums[0].shape)
+    part = exchange_gather(part, "dp")
+    part = exchange_gather(part, "expert")
+    own_grads = part.reshape(n_adapt, tiles, rank, 128)
 
     def own_part(start, length):
         part = own_grads[:, start // 128 : -(-(start + length) // 128)].astype(F32)

time: 416 us -> 430 us (1.034)
  starting transfers between devices: 14.1 us -> 51.1 us
  blocking collectives: 94.1 us -> 58.3 us
  Pallas kernels: 115 us -> 122 us
    ppermute x0 -> x13, waiting for transfers between devices: none -> 81.4 us  [the longest x7 44.9 us: direct_parts(): found.append(lax.ppermute(part, axis, pairs))]
    all_to_all x1 -> x2, waiting for transfers between devices: 86.9 us -> 16.1 us  [exchange(): return lax.all_to_all(parts, axis, split_axis=0, concat_axis=0, tiled=True)]
    ppermute x0 -> x13, starting transfers between devices: none -> 34.1 us  [the longest x7 30.3 us: direct_parts(): found.append(lax.ppermute(part, axis, pairs))]
    all_to_all x2 -> x0, blocking collectives: 30.9 us -> none  [exchange_sum(): parts = lax.all_to_all(parts, axis, split_axis=0, concat_axis=0, tiled=True)]
    all_gather x3 -> x1, waiting for transfers between devices: 27.1 us -> 16.2 us  [body(): last = lax.all_gather(sum_after(sums[1], part), 'dp', axis=0, tiled=True)]
    pallas_call x2 -> x3, Pallas kernels: 55.7 us -> 63.1 us  [the longest x2 57 us: body(): pl.pallas_call(functools.partial(expert_kernel, len(after), groups), out_...]
    all_to_all x1 -> x2, starting transfers between devices: 5.51 us -> 9.35 us  [exchange(): return lax.all_to_all(parts, axis, split_axis=0, concat_axis=0, tiled=True)]
  transfers between devices with their start and end apart: 7 -> 19, of which waited for: 4 -> 9; matrix products, arithmetic and copies ran while one was open for 5% -> 5% of each run, Pallas kernels for 14% -> 11%
where the time goes in v4:
time: 430 us; the launch traced here: 429 us
  waiting for transfers between devices  144 us (33%)
  Pallas kernels  122 us (28%)
  blocking collectives  58.3 us (14%)
  starting transfers between devices  51.1 us (12%)
  local copies, waits for them, and re-layouts  23.5 us (5%)
  other arithmetic  14.7 us (3%)
  between operations  14.6 us (3%)
    pallas_call x2, Pallas kernels, body(): pl.pallas_call(functools.partial(expert_kernel, len(after), groups), out_...  57 us
    ppermute x7, waiting for transfers between devices, direct_parts(): found.append(lax.ppermute(part, axis, pairs))  44.9 us
    pallas_call x1, Pallas kernels, body(): pl.pallas_call(functools.partial(backward_kernel, seq_len), out_shape=out...  40.3 us
    ppermute x2, waiting for transfers between devices, gather_blocks(): blocks.append(lax.ppermute(block, axis, pairs))  36.4 us
    ppermute x7, starting transfers between devices, direct_parts(): found.append(lax.ppermute(part, axis, pairs))  30.3 us
    all_to_all x1, blocking collectives, body(): lax.all_to_all(back, 'expert', split_axis=0, concat_axis=0, tiled=True)  30.1 us
    all_to_all x1, waiting for transfers between devices, body(): lax.all_to_all(back, 'expert', split_axis=0, concat_axis=0, tiled=True)  23.4 us
    pallas_call x1, Pallas kernels, body(): pl.pallas_call(functools.partial(forward_kernel, seq_len), out_shape=forw...  19 us
  transfers between devices with their start and end apart: 19, of which 9 were waited for; matrix products, arithmetic and copies ran while one was open for 5% of the time, Pallas kernels for 11%

profile of v4, /device:TPU:0, one launch (start us, length us, event | category | flops | bytes accessed | tf_op | source)
XLA Modules:
  0.0 429.0 jit_solution(12104867738779896140)
XLA Ops:
  7.2 1.0 copy.105
  8.2 0.8 pad_bitcast_fusion
  9.0 0.8 copy.106.pick_rows_ref
  11.1 1.0 pad.12.images_ref
  12.1 19.0 %attend.1 = (bf16[4,208,1536]{2,1,0:T(8,128)(2,1)}, bf16[4,208,512]{2,1,0:T(8,128)(2,1)}, f32[4,208,512]{2,1,0:T(8,128)}, bf16[4,208,512]{2,1,0:T(8,128)(2,1)}, ...) custom-call(s32[4]{0:T(128)} %ids_ref.3, bf16[4,208,512]{2,1,0:T(8,128)(2,1)} %pad.12.images_ref, ...), custom_call_target="tpu_custom_call" | custom-call | flops 20000000000 | bytes 1000000 | tf_op jit(solution)/shard_map/attend/pallas_call | solution.py:510
  31.1 3.1 collective-permute-start
  35.2 19.0 %collective-permute-done.rest_1_ = bf16[832,512]{1,0:T(8,128)(2,1)} collective-permute-done((bf16[832,512]{1,0:T(8,128)(2,1)}, bf16[832,512]{1,0:T(8,128)(2,1)}, u32[]{:S(2)}, u32[]{:S(2)}) %collective-permute-start) | collective-permute-done | bytes 852000 | tf_op jit(solution)/shard_map/ppermute | solution.py:347
  54.3 17.4 %collective-permute-done.3.rest_5_ = bf16[832,512]{1,0:T(8,128)(2,1)} collective-permute-done((bf16[832,512]{1,0:T(8,128)(2,1)S(1)}, bf16[832,512]{1,0:T(8,128)(2,1)}, u32[]{:S(2)}, u32[]{:S(2)}) %collective-permute-start.3) | collective-permute-done | bytes 852000 | tf_op jit(solution)/shard_map/ppermute | solution.py:347
  72.2 5.8 %all_gather.14.gate_rows_ref = f32[4,2,832]{2,1,0:T(2,128)} all-gather(f32[1,2,832]{2,1,0:T(2,128)S(1)} %all_gather_reshape.3), channel_id=1, replica_groups=mesh['dp'=8,'expert'=4] {'expert'}, dimensions={0}, use_global_device_ids=true | all-gather | bytes 33280 | tf_op jit(solution)/shard_map/all_gather | solution.py:526
  78.4 5.9 %all-gather.1.marks_ref = s32[4,3,832]{2,1,0:T(4,128)} all-gather(s32[1,3,832]{2,1,0:T(4,128)S(1)} %add_bitcast_fusion), channel_id=2, replica_groups=mesh['dp'=8,'expert'=4] {'expert'}, dimensions={0}, use_global_device_ids=true | all-gather | bytes 49920 | tf_op jit(solution)/shard_map/all_gather | solution.py:490
  84.9 28.5 %shard_map.292 = (bf16[4,2,128,1024]{3,2,1,0:T(8,128)(2,1)}, bf16[2,128,5120]{2,1,0:T(8,128)(2,1)}) custom-call(s32[5]{0:T(128)} %get-tuple-element.121.first_ref, s32[4,3,832]{2,1,0:T(4,128)} %all-gather.1.marks_ref, f32[4,2,832]{2,1,0:T(2,128)} %all_gather.14.gate_rows_ref, bf16[832,512]{1,0:T(8,128)(2,1)} %bitcast.171, ...), custom_call_target="tpu_custom_call" | custom-call | flops 28000000000 | bytes 1000000 | tf_op jit(solution)/shard_map/pallas_call | solution.py:547
  113.4 28.5 %shard_map.293 = (bf16[4,2,128,1024]{3,2,1,0:T(8,128)(2,1)}, bf16[2,128,5120]{2,1,0:T(8,128)(2,1)}) custom-call(s32[5]{0:T(128)} %get-tuple-element.120.first_ref, s32[4,3,832]{2,1,0:T(4,128)} %all-gather.1.marks_ref, f32[4,2,832]{2,1,0:T(2,128)} %all_gather.14.gate_rows_ref, bf16[832,512]{1,0:T(8,128)(2,1)} %bitcast.172, ...), custom_call_target="tpu_custom_call" | custom-call | flops 28000000000 | bytes 1000000 | tf_op jit(solution)/shard_map/pallas_call | solution.py:547
  141.8 30.1 %all_to_all.30 = bf16[4,2,128,1024]{3,2,1,0:T(8,128)(2,1)} all-to-all(bf16[4,2,128,1024]{3,2,1,0:T(8,128)(2,1)} %get-tuple-element.32), channel_id=1, replica_groups=mesh['dp'=8,'expert'=4] {'expert'}, dimensions={0} | all-to-all | bytes 4194304 | tf_op jit(solution)/shard_map/all_to_all | solution.py:576
  172.0 3.6 all-to-all-start
  176.2 1.6 fusion.19.slots_ref
  177.8 23.4 %all-to-all-done = bf16[4,2,128,1024]{3,2,1,0:T(8,128)(2,1)S(1)} async-done(((bf16[4,2,128,1024]{3,2,1,0:T(8,128)(2,1)}), bf16[4,2,128,1024]{3,2,1,0:T(8,128)(2,1)S(1)}, u32[]{:S(2)}, u32[]{:S(2)}) %all-to-all-start) | async-done | bytes 2097184 | tf_op jit(solution)/shard_map/all_to_all | solution.py:576
  201.2 1.3 copy-done
  202.6 40.3 %attend_back.1 = (bf16[4,197,512]{2,1,0:T(8,128)(2,1)}, f32[4,197,512]{2,1,0:T(8,128)}, bf16[8,32,16,128]{3,2,1,0:T(8,128)(2,1)}) custom-call(s32[4]{0:T(128)} %ids_ref.3, bf16[4,208,512]{2,1,0:T(8,128)(2,1)} %pad.12.images_ref, bf16[4,208,512]{2,1,0:T(8,128)(2,1)} %copy-done.5, f32[4,208,512]{2,1,0:T(8,128)} %get-tuple-element.25.hidden_ref, ...), custom_call_target="tpu_custom_call" | custom-call | flops 40000000000 | bytes 1000000 | tf_op jit(solution)/shard_map/attend_back/pallas_call | solution.py:588
  242.9 3.5 all-to-all-start.2
  246.4 2.9 dynamic-slice_bitcast_fusion
  249.3 3.5 collective-permute-start.10
  252.8 1.4 collective-permute-start.11
  254.1 6.7 %all-to-all-done.2 = bf16[4,1024,128]{2,1,0:T(8,128)(2,1)S(1)} async-done(((bf16[4,1024,128]{2,1,0:T(8,128)(2,1)}), bf16[4,1024,128]{2,1,0:T(8,128)(2,1)S(1)}, u32[]{:S(2)}, u32[]{:S(2)}) %all-to-all-start.2) | async-done | bytes 1048608 | tf_op jit(solution)/shard_map/all_to_all | solution.py:364
  260.8 0.9 reduce_sum.44
  261.7 5.8 %all-to-all-start.3 = ((bf16[8,128,128]{2,1,0:T(8,128)(2,1)}), bf16[8,128,128]{2,1,0:T(8,128)(2,1)S(1)}, u32[]{:S(2)}, u32[]{:S(2)}) async-start(bf16[8,128,128]{2,1,0:T(8,128)(2,1)} %bitcast.31), calls=%async_computation.3 | async-start | bytes 524288 | tf_op jit(solution)/shard_map/all_to_all | solution.py:364
  267.6 4.7 %collective-permute-start.12 = (bf16[32,5120]{1,0:T(8,128)(2,1)S(1)}, bf16[32,5120]{1,0:T(8,128)(2,1)S(1)}, u32[]{:S(2)}, u32[]{:S(2)}) collective-permute-start(bf16[32,5120]{1,0:T(8,128)(2,1)S(1)} %get-tuple-element.106), channel_id=1, source_target_pairs={{0,28},{4,0},{8,4},{12,8},{16,12},{20,16},{24,20},{28,24},{1,29},{... | collective-permute-start | bytes 983048 | tf_op jit(solution)/shard_map/ppermute | solution.py:386
  272.3 2.6 collective-permute-start.8
  274.8 18.2 %collective-permute-start.9 = (bf16[32,5120]{1,0:T(8,128)(2,1)S(1)}, bf16[32,5120]{1,0:T(8,128)(2,1)S(1)}, u32[]{:S(2)}, u32[]{:S(2)}) collective-permute-start(bf16[32,5120]{1,0:T(8,128)(2,1)S(1)} %get-tuple-element.109), channel_id=1, source_target_pairs={{0,16},{4,20},{8,24},{12,28},{16,0},{20,4},{24,8},{28,12},{1,17},{... | collective-permute-start | bytes 983048 | tf_op jit(solution)/shard_map/ppermute | solution.py:386
  293.1 9.4 %all-to-all-done.3 = bf16[8,128,128]{2,1,0:T(8,128)(2,1)S(1)} async-done(((bf16[8,128,128]{2,1,0:T(8,128)(2,1)}), bf16[8,128,128]{2,1,0:T(8,128)(2,1)S(1)}, u32[]{:S(2)}, u32[]{:S(2)}) %all-to-all-start.3) | async-done | bytes 262176 | tf_op jit(solution)/shard_map/all_to_all | solution.py:364
  303.2 28.5 %collective-permute-done.8.refs_3_ = bf16[32,5120]{1,0:T(8,128)(2,1)} collective-permute-done((bf16[32,5120]{1,0:T(8,128)(2,1)S(1)}, bf16[32,5120]{1,0:T(8,128)(2,1)}, u32[]{:S(2)}, u32[]{:S(2)}) %collective-permute-start.8) | collective-permute-done | bytes 327712 | tf_op jit(solution)/shard_map/ppermute | solution.py:386
  331.6 16.4 %collective-permute-done.9.refs_4_ = bf16[32,5120]{1,0:T(8,128)(2,1)S(1)} collective-permute-done((bf16[32,5120]{1,0:T(8,128)(2,1)S(1)}, bf16[32,5120]{1,0:T(8,128)(2,1)S(1)}, u32[]{:S(2)}, u32[]{:S(2)}) %collective-permute-start.9) | collective-permute-done | bytes 327712 | tf_op jit(solution)/shard_map/ppermute | solution.py:386
  348.8 6.2 %add_parts.1 = bf16[32,5120]{1,0:T(8,128)(2,1)} custom-call(bf16[32,5120]{1,0:T(8,128)(2,1)} %get-tuple-element.113.refs_0_, bf16[32,5120]{1,0:T(8,128)(2,1)} %copy-done.10, bf16[32,5120]{1,0:T(8,128)(2,1)} %copy-done.11, bf16[32,5120]{1,0:T(8,128)(2,1)} %collective-permute-done.8.refs_3_, bf16[32,5120]{1,0:T(8,128)(2,1)} %copy-done.12, ...), custom_call_target="tpu_custom_call" | custom-call | tf_op jit(solution)/shard_map/add_parts/pallas_call | solution.py:400
  355.0 16.5 %all_to_all.31 = bf16[8,128,128]{2,1,0:T(8,128)(2,1)S(1)} all-to-all(bf16[8,128,128]{2,1,0:T(8,128)(2,1)S(1)} %broadcast_in_dim.16), channel_id=1, replica_groups=mesh['dp'=8,'expert'=4] {'dp'}, dimensions={0} | all-to-all | bytes 524288 | tf_op jit(solution)/shard_map/all_to_all | solution.py:374
  371.5 1.1 broadcast_in_dim.18
  372.6 3.8 all-to-all-start.5
  376.4 2.2 copy.121
  378.6 1.3 copy.120
  379.9 1.9 fusion.32
  381.8 1.7 fusion.34
  383.5 7.1 %all-to-all-done.5 = bf16[4,1024,128]{2,1,0:T(8,128)(2,1)S(1)} async-done(((bf16[4,1024,128]{2,1,0:T(8,128)(2,1)}), bf16[4,1024,128]{2,1,0:T(8,128)(2,1)S(1)}, u32[]{:S(2)}, u32[]{:S(2)}) %all-to-all-start.5) | async-done | bytes 1048608 | tf_op jit(solution)/shard_map/all_to_all | solution.py:374
  394.2 1.0 copy_bitcast_fusion
  395.2 16.2 %all-gather.4.cloned.1.call-done = bf16[256,5120]{1,0:T(8,128)(2,1)} async-done(((bf16[32,5120]{1,0:T(8,128)(2,1)}), bf16[256,5120]{1,0:T(8,128)(2,1)}) %all-gather.4.cloned.1.call-update) | async-done | bytes 2621456 | tf_op jit(solution)/shard_map/all_gather | solution.py:608
  411.4 1.1 fusion.33
  412.5 1.8 fusion.35
  414.4 1.1 convert.32
  415.7 2.6 convert_bitcast_fusion
  418.5 2.6 convert.30
  421.1 1.1 convert_bitcast_fusion.1
  (91 shorter events, 9.9 us)
Async XLA Ops:
  7.2 2.6 copy-start.7
  7.2 2.7 copy-start.15
  7.2 3.3 copy-start.16
  12.1 22.1 %copy-start.8 = (bf16[4,197,512]{2,0,1:T(4,128)(2,1)S(1)}, bf16[4,197,512]{2,0,1:T(4,128)(2,1)}, u32[]{:S(2)}) copy-start(bf16[4,197,512]{2,0,1:T(4,128)(2,1)} %param.24) | copy-start | bytes 2420740
  31.1 3.4 copy-start.18
  31.1 4.0 copy-start.1
  31.1 40.7 %copy-start.17 = (s32[4]{0:T(128)S(1)}, s32[4]{0:T(128)}, u32[]{:S(2)}) copy-start(s32[4]{0:T(128)} %ids_ref.3) | copy-start | bytes 52
  31.1 40.8 %copy-start.14 = (f32[4,2,208]{2,1,0:T(2,128)S(1)}, f32[4,2,208]{2,1,0:T(2,128)}, u32[]{:S(2)}) copy-start(f32[4,2,208]{2,1,0:T(2,128)} %get-tuple-element.30) | copy-start | bytes 19972
  31.1 23.2 %collective-permute-start = (bf16[832,512]{1,0:T(8,128)(2,1)}, bf16[832,512]{1,0:T(8,128)(2,1)}, u32[]{:S(2)}, u32[]{:S(2)}) collective-permute-start(bf16[832,512]{1,0:T(8,128)(2,1)} %bitcast.170), channel_id=1, source_target_pairs={{0,2},{1,3},{2,0},{3,1},{4,6},{5,7},{6,4},{7,5},{8,10},{9,11},{10,... | collective-permute-start | bytes 2555912 | tf_op jit(solution)/shard_map/ppermute | solution.py:347
  34.4 50.5 %copy-start.5 = (bf16[4,208,512]{2,1,0:T(8,128)(2,1)}, bf16[4,208,512]{2,1,0:T(8,128)(2,1)S(1)}, u32[]{:S(2)}) copy-start(bf16[4,208,512]{2,1,0:T(8,128)(2,1)S(1)} %pad.13.upstream_ref) | copy-start | bytes 2555908
  34.4 37.3 %collective-permute-start.3 = (bf16[832,512]{1,0:T(8,128)(2,1)S(1)}, bf16[832,512]{1,0:T(8,128)(2,1)}, u32[]{:S(2)}, u32[]{:S(2)}) collective-permute-start(bf16[832,512]{1,0:T(8,128)(2,1)S(1)} %bitcast.152), channel_id=1, source_target_pairs={{0,2},{1,3},{2,0},{3,1},{4,6},{5,7},{6,4},{7,5},{8,10},{9,11},{10,... | collective-permute-start | bytes 2555912 | tf_op jit(solution)/shard_map/ppermute | solution.py:347
  34.5 50.4 %collective-permute-start.1 = (bf16[832,512]{1,0:T(8,128)(2,1)S(1)}, bf16[832,512]{1,0:T(8,128)(2,1)}, u32[]{:S(2)}, u32[]{:S(2)}) collective-permute-start(bf16[832,512]{1,0:T(8,128)(2,1)S(1)} %bitcast.173), channel_id=1, source_target_pairs={{0,1},{1,0},{2,3},{3,2},{4,5},{5,4},{6,7},{7,6},{8,9},{9,8},{10,11... | collective-permute-start | bytes 2555912 | tf_op jit(solution)/shard_map/ppermute | solution.py:349
  34.6 50.3 %collective-permute-start.4 = (bf16[832,512]{1,0:T(8,128)(2,1)S(1)}, bf16[832,512]{1,0:T(8,128)(2,1)}, u32[]{:S(2)}, u32[]{:S(2)}) collective-permute-start(bf16[832,512]{1,0:T(8,128)(2,1)S(1)} %bitcast.153), channel_id=1, source_target_pairs={{0,1},{1,0},{2,3},{3,2},{4,5},{5,4},{6,7},{7,6},{8,9},{9,8},{10,11... | collective-permute-start | bytes 2555912 | tf_op jit(solution)/shard_map/ppermute | solution.py:349
  54.3 30.6 %collective-permute-start.2 = (bf16[832,512]{1,0:T(8,128)(2,1)}, bf16[832,512]{1,0:T(8,128)(2,1)}, u32[]{:S(2)}, u32[]{:S(2)}) collective-permute-start(bf16[832,512]{1,0:T(8,128)(2,1)} %collective-permute-done.rest_1_), channel_id=1, source_target_pairs={{0,1},{1,0},{2,3},{3,2},{4,5},{5,4},{6,7},{7,6},{8,9},{9,8},{10,11... | collective-permute-start | bytes 2555912 | tf_op jit(solution)/shard_map/ppermute | solution.py:349
  71.7 13.2 %collective-permute-start.5 = (bf16[832,512]{1,0:T(8,128)(2,1)}, bf16[832,512]{1,0:T(8,128)(2,1)}, u32[]{:S(2)}, u32[]{:S(2)}) collective-permute-start(bf16[832,512]{1,0:T(8,128)(2,1)} %collective-permute-done.3.rest_5_), channel_id=1, source_target_pairs={{0,1},{1,0},{2,3},{3,2},{4,5},{5,4},{6,7},{7,6},{8,9},{9,8},{10,11... | collective-permute-start | bytes 2555912 | tf_op jit(solution)/shard_map/ppermute | solution.py:349
  172.0 29.2 %all-to-all-start = ((bf16[4,2,128,1024]{3,2,1,0:T(8,128)(2,1)}), bf16[4,2,128,1024]{3,2,1,0:T(8,128)(2,1)S(1)}, u32[]{:S(2)}, u32[]{:S(2)}) async-start(bf16[4,2,128,1024]{3,2,1,0:T(8,128)(2,1)} %get-tuple-element.31.rest_14_), calls=%async_computation | async-start | bytes 4194304 | tf_op jit(solution)/shard_map/all_to_all | solution.py:576
  175.6 204.3 %all-reduce.6.cloned.1.call-start = ((), (), s32[]{:S(2)}) async-start(), calls=%async_computation.6 | async-start | bytes 5242880 | tf_op jit(solution)/shard_map/psum | solution.py:577
  201.2 1.3 copy-start
  242.9 17.9 %all-to-all-start.2 = ((bf16[4,1024,128]{2,1,0:T(8,128)(2,1)}), bf16[4,1024,128]{2,1,0:T(8,128)(2,1)S(1)}, u32[]{:S(2)}, u32[]{:S(2)}) async-start(bf16[4,1024,128]{2,1,0:T(8,128)(2,1)} %bitcast.151), calls=%async_computation.2 | async-start | bytes 2097152 | tf_op jit(solution)/shard_map/all_to_all | solution.py:364
  249.3 23.0 %collective-permute-start.10 = (bf16[32,5120]{1,0:T(8,128)(2,1)}, bf16[32,5120]{1,0:T(8,128)(2,1)}, u32[]{:S(2)}, u32[]{:S(2)}) collective-permute-start(bf16[32,5120]{1,0:T(8,128)(2,1)} %get-tuple-element.108), channel_id=1, source_target_pairs={{0,20},{4,24},{8,28},{12,0},{16,4},{20,8},{24,12},{28,16},{1,21},{... | collective-permute-start | bytes 983048 | tf_op jit(solution)/shard_map/ppermute | solution.py:386
  252.8 22.1 %collective-permute-start.11 = (bf16[32,5120]{1,0:T(8,128)(2,1)S(1)}, bf16[32,5120]{1,0:T(8,128)(2,1)}, u32[]{:S(2)}, u32[]{:S(2)}) collective-permute-start(bf16[32,5120]{1,0:T(8,128)(2,1)S(1)} %get-tuple-element.107), channel_id=1, source_target_pairs={{0,24},{4,28},{8,0},{12,4},{16,8},{20,12},{24,16},{28,20},{1,25},{... | collective-permute-start | bytes 983048 | tf_op jit(solution)/shard_map/ppermute | solution.py:386
  261.7 40.7 %all-to-all-start.3 = ((bf16[8,128,128]{2,1,0:T(8,128)(2,1)}), bf16[8,128,128]{2,1,0:T(8,128)(2,1)S(1)}, u32[]{:S(2)}, u32[]{:S(2)}) async-start(bf16[8,128,128]{2,1,0:T(8,128)(2,1)} %bitcast.31), calls=%async_computation.3 | async-start | bytes 524288 | tf_op jit(solution)/shard_map/all_to_all | solution.py:364
  267.5 143.9 %all-gather.4.cloned.1.call-start = ((), (), s32[]{:S(2)}) async-start(), calls=%async_computation.7 | async-start | bytes 2949120 | tf_op jit(solution)/shard_map/all_gather | solution.py:608
  267.6 35.6 %collective-permute-start.12 = (bf16[32,5120]{1,0:T(8,128)(2,1)S(1)}, bf16[32,5120]{1,0:T(8,128)(2,1)S(1)}, u32[]{:S(2)}, u32[]{:S(2)}) collective-permute-start(bf16[32,5120]{1,0:T(8,128)(2,1)S(1)} %get-tuple-element.106), channel_id=1, source_target_pairs={{0,28},{4,0},{8,4},{12,8},{16,12},{20,16},{24,20},{28,24},{1,29},{... | collective-permute-start | bytes 983048 | tf_op jit(solution)/shard_map/ppermute | solution.py:386
  272.2 30.9 %collective-permute-start.6 = (bf16[32,5120]{1,0:T(8,128)(2,1)S(1)}, bf16[32,5120]{1,0:T(8,128)(2,1)S(1)}, u32[]{:S(2)}, u32[]{:S(2)}) collective-permute-start(bf16[32,5120]{1,0:T(8,128)(2,1)S(1)} %get-tuple-element.112), channel_id=1, source_target_pairs={{0,4},{4,8},{8,12},{12,16},{16,20},{20,24},{24,28},{28,0},{1,5},{5... | collective-permute-start | bytes 983048 | tf_op jit(solution)/shard_map/ppermute | solution.py:386
  272.2 30.9 %collective-permute-start.7 = (bf16[32,5120]{1,0:T(8,128)(2,1)S(1)}, bf16[32,5120]{1,0:T(8,128)(2,1)S(1)}, u32[]{:S(2)}, u32[]{:S(2)}) collective-permute-start(bf16[32,5120]{1,0:T(8,128)(2,1)S(1)} %get-tuple-element.111), channel_id=1, source_target_pairs={{0,8},{4,12},{8,16},{12,20},{16,24},{20,28},{24,0},{28,4},{1,9},{5... | collective-permute-start | bytes 983048 | tf_op jit(solution)/shard_map/ppermute | solution.py:386
  272.3 59.4 %collective-permute-start.8 = (bf16[32,5120]{1,0:T(8,128)(2,1)S(1)}, bf16[32,5120]{1,0:T(8,128)(2,1)}, u32[]{:S(2)}, u32[]{:S(2)}) collective-permute-start(bf16[32,5120]{1,0:T(8,128)(2,1)S(1)} %get-tuple-element.110), channel_id=1, source_target_pairs={{0,12},{4,16},{8,20},{12,24},{16,28},{20,0},{24,4},{28,8},{1,13},{... | collective-permute-start | bytes 983048 | tf_op jit(solution)/shard_map/ppermute | solution.py:386
  274.8 73.2 %collective-permute-start.9 = (bf16[32,5120]{1,0:T(8,128)(2,1)S(1)}, bf16[32,5120]{1,0:T(8,128)(2,1)S(1)}, u32[]{:S(2)}, u32[]{:S(2)}) collective-permute-start(bf16[32,5120]{1,0:T(8,128)(2,1)S(1)} %get-tuple-element.109), channel_id=1, source_target_pairs={{0,16},{4,20},{8,24},{12,28},{16,0},{20,4},{24,8},{28,12},{1,17},{... | collective-permute-start | bytes 983048 | tf_op jit(solution)/shard_map/ppermute | solution.py:386
  303.1 51.9 %copy-start.13 = (bf16[128,128]{1,0:T(8,128)(2,1)S(1)}, bf16[128,128]{1,0:T(8,128)(2,1)}, u32[]{:S(2)}) copy-start(bf16[128,128]{1,0:T(8,128)(2,1)} %reduce_sum.45.refs_8_) | copy-start | bytes 98308
  303.1 44.9 %copy-start.9 = (bf16[32,5120]{1,0:T(8,128)(2,1)}, bf16[32,5120]{1,0:T(8,128)(2,1)S(1)}, u32[]{:S(2)}) copy-start(bf16[32,5120]{1,0:T(8,128)(2,1)S(1)} %collective-permute-done.12.refs_7_) | copy-start | bytes 983044
  303.1 44.9 %copy-start.10 = (bf16[32,5120]{1,0:T(8,128)(2,1)}, bf16[32,5120]{1,0:T(8,128)(2,1)S(1)}, u32[]{:S(2)}) copy-start(bf16[32,5120]{1,0:T(8,128)(2,1)S(1)} %collective-permute-done.6.refs_1_) | copy-start | bytes 983044
  303.1 44.9 %copy-start.11 = (bf16[32,5120]{1,0:T(8,128)(2,1)}, bf16[32,5120]{1,0:T(8,128)(2,1)S(1)}, u32[]{:S(2)}) copy-start(bf16[32,5120]{1,0:T(8,128)(2,1)S(1)} %collective-permute-done.7.refs_2_) | copy-start | bytes 983044
  348.1 0.7 copy-start.12
  355.0 21.4 %copy-start.2 = (f32[4,197,512]{2,1,0:T(8,128)S(1)}, f32[4,197,512]{2,1,0:T(8,128)}, u32[]{:S(2)}) copy-start(f32[4,197,512]{2,1,0:T(8,128)} %get-tuple-element.87) | copy-start | bytes 4841476
  372.6 17.9 %all-to-all-start.5 = ((bf16[4,1024,128]{2,1,0:T(8,128)(2,1)}), bf16[4,1024,128]{2,1,0:T(8,128)(2,1)S(1)}, u32[]{:S(2)}, u32[]{:S(2)}) async-start(bf16[4,1024,128]{2,1,0:T(8,128)(2,1)} %broadcast_in_dim.18), calls=%async_computation.5 | async-start | bytes 2097152 | tf_op jit(solution)/shard_map/all_to_all | solution.py:374
  376.4 2.2 copy-start.6
  412.5 1.8 copy-start.4
  418.4 2.6 copy-start.3
Sparse Core Ops, SparseCore 0:
  180.7 167.2 all-reduce.5
  355.1 56.2 all-gather.3

commit v5 on v4

--- a/solution.py
+++ b/solution.py
@@ -11,7 +11,6 @@
 EPSILON = 1e-06
 F32 = jnp.float32
 LOW = jnp.bfloat16
-PIECES = 2
 CHUNK = 512
 
 
@@ -138,8 +137,10 @@
     return values * half, half + values * density
 
 
-def expert_kernel(n_after, groups, first_ref, marks_ref, gate_rows_ref, *rest):
-    token_refs, upstream_refs, rest = rest[:groups], rest[groups : 2 * groups], rest[2 * groups :]
+def expert_kernel(n_after, groups, first_ref, *rest):
+    mark_refs, gate_refs = rest[:groups], rest[groups : 2 * groups]
+    token_refs, upstream_refs = rest[2 * groups : 3 * groups], rest[3 * groups : 4 * groups]
+    rest = rest[4 * groups :]
     up_ref, down_ref, up_a_ref, up_b_ref, down_a_ref, down_b_ref = rest[:6]
     rest = rest[6:]
     back_ref, grads_ref, rows_ref, dy_ref, mask_ref = rest[n_after : n_after + 5]
@@ -152,20 +153,20 @@
     start = (first_ref[0] + pl.program_id(0)) * capacity
     for group in range(groups):
         span = slice(group * capacity, (group + 1) * capacity)
-        source = first_ref[1 + group]
+        marks_ref, gate_rows_ref = mark_refs[group], gate_refs[group]
         n_tokens = token_refs[group].shape[0]
         slots = lax.broadcasted_iota(jnp.int32, (capacity, n_tokens), 0) + start
-        zero = slots == marks_ref[source, 0:1, :]
-        one = slots == marks_ref[source, 1:2, :]
+        zero = slots == marks_ref[0:1, :]
+        one = slots == marks_ref[1:2, :]
         either = jnp.where(zero | one, 1.0, 0.0)
         gate = jnp.sum(
-            jnp.where(zero, gate_rows_ref[source, 0:1, :], 0.0)
-            + jnp.where(one, gate_rows_ref[source, 1:2, :], 0.0),
+            jnp.where(zero, gate_rows_ref[0:1, :], 0.0)
+            + jnp.where(one, gate_rows_ref[1:2, :], 0.0),
             axis=1,
             keepdims=True,
         )
         ids = jnp.sum(
-            either * marks_ref[source, 2:3, :].astype(F32), axis=1, keepdims=True
+            either * marks_ref[2:3, :].astype(F32), axis=1, keepdims=True
         )
         either = either.astype(LOW)
         rows_ref[span, :] = nn(either, token_refs[group][...]).astype(LOW)
@@ -257,9 +258,11 @@
 
     rows = images_ref.shape[1]
     pair_zero = pair_one = spread = None
+    offset = 0
     for number, back_ref in enumerate(back_refs):
         n_slots = back_ref.shape[0]
-        slots = lax.broadcasted_iota(jnp.int32, (rows, n_slots), 1) + number * n_slots
+        slots = lax.broadcasted_iota(jnp.int32, (rows, n_slots), 1) + offset
+        offset += n_slots
         zero = jnp.where(slots == slots_ref[0, :, 0:1], 1.0, 0.0).astype(LOW)
         one = jnp.where(slots == slots_ref[0, :, 1:2], 1.0, 0.0).astype(LOW)
         terms = (
@@ -387,6 +390,20 @@
     return found
 
 
+def direct_gather(part, axis):
+    count = lax.axis_size(axis)
+    place = lax.axis_index(axis)
+    whole_sum = jnp.zeros((count,) + part.shape, part.dtype)
+    found = [part]
+    for hop in range(1, count):
+        pairs = [(i, (i + hop) % count) for i in range(count)]
+        found.append(lax.ppermute(part, axis, pairs))
+    for hop, block in enumerate(found):
+        spot = (place - hop + count) % count
+        whole_sum = lax.dynamic_update_index_in_dim(whole_sum, block, spot, 0)
+    return whole_sum.reshape(-1, part.shape[-1])
+
+
 def sum_kernel(count, *refs):
     total = refs[0][...].astype(F32)
     for number in range(1, count):
@@ -461,7 +478,8 @@
     groups = lax.axis_size("expert")
     capacity = max(2, tokens * 2 * 5 // (4 * n_experts))
     room = -(-capacity // 16) * 16
-    here = local // PIECES
+    sizes = (local - 2 * (local // 4), local // 4, local // 4)
+    starts = (0, sizes[0], sizes[0] + sizes[1])
 
     fill = ((0, 0), (0, padded - seq_len), (0, 0))
     images = jnp.pad(images, fill)
@@ -481,13 +499,16 @@
         jnp.where(marks, before + offset[:, :, None], 0.0), axis=1
     ).astype(jnp.int32)
     group_of, inner = flat // local, flat % local
-    ranked = ((inner // here) * groups + group_of) * here + inner % here
+    base, size = jnp.zeros_like(inner), jnp.full_like(inner, sizes[0])
+    base = jnp.where(inner >= sizes[0], sizes[0], base)
+    size = jnp.where(inner >= sizes[0], local - sizes[0], size)
+    ranked = base * groups + group_of * size + inner - base
     kept = (flat >= 0) & (places < capacity)
     slots = jnp.where(kept, ranked * room + places, -1)
     token_ids = jnp.broadcast_to(adapter_ids[:, None], (n_images, padded)).reshape(1, rows)
     slot_columns = slots.reshape(2, n_images, padded).transpose(1, 2, 0)
     side = jnp.concatenate([slots, token_ids], axis=0)
-    side_all = lax.all_gather(side, "expert")
+    side_all = gather_blocks(side, "expert")
     upstream_all = gather_blocks(upstream.reshape(rows, width), "expert")
 
     gain_one = ln_gain1.astype(F32).reshape(1, width)
@@ -523,15 +544,14 @@
 
     normed_all = gather_blocks(normed.reshape(rows, width), "expert")
     sources = block_sources("expert")
-    gates_all = lax.all_gather(gate_rows.transpose(1, 0, 2).reshape(2, rows), "expert")
+    gates_all = gather_blocks(gate_rows.transpose(1, 0, 2).reshape(2, rows), "expert")
     up_a_t = up_a.transpose(0, 1, 3, 2).reshape(local, low_cols, width)
     up_b_flat = up_b.reshape(local, low_cols, ff_width)
     down_a_t = down_a.transpose(0, 1, 3, 2).reshape(local, low_cols, ff_width)
     down_b_flat = down_b.reshape(local, low_cols, width)
     cols = 2 * width + 2 * ff_width
     backs, sums, raw = [], [], []
-    for piece in range(PIECES):
-        at = piece * here
+    for piece, (at, here) in enumerate(zip(starts, sizes)):
 
         def of_expert(array, at=at):
             rank = len(array.shape)
@@ -540,8 +560,10 @@
             )
 
         weights = (up_weight, down_weight, up_a_t, up_b_flat, down_a_t, down_b_flat)
-        first = ((piece * groups + lax.axis_index("expert")) * here).astype(jnp.int32)
-        gathered = (side_all, gates_all, *normed_all, *upstream_all)
+        lowest, together = (0, sizes[0]) if piece == 0 else (sizes[0], local - sizes[0])
+        first = lowest * groups + lax.axis_index("expert") * together + at - lowest
+        first = first.astype(jnp.int32)
+        gathered = (*side_all, *gates_all, *normed_all, *upstream_all)
         after = tuple(raw[-1:])
         n_rows = groups * room
         back, grads = pl.pallas_call(
@@ -570,12 +592,19 @@
                     pltpu.VMEM((2, low_cols, n_rows), LOW),
                 ],
             ),
-            cost_estimate=work_of(28),
+            cost_estimate=work_of(14 * here),
         )(jnp.concatenate([first.reshape(1), sources]), *gathered, *weights, *after)
         raw.append(back)
-        backs.append(lax.all_to_all(back, "expert", split_axis=0, concat_axis=0, tiled=True))
-        sums.append(lax.psum(grads, "dp") if piece == 0 else direct_parts(grads, "dp"))
-    backs = [back.reshape(groups * here * room, 2 * width) for back in backs]
+        if piece != 1:
+            back = back if piece == 0 else jnp.concatenate(raw[1:], axis=1)
+            back = lax.all_to_all(back, "expert", split_axis=0, concat_axis=0, tiled=True)
+            backs.append(back)
+        sums.append(grads)
+        if piece == 1:
+            sums = list(lax.psum(tuple(sums), "dp"))
+        if piece == 2:
+            sums[2] = direct_parts(grads, "dp")
+    backs = [back.reshape(-1, 2 * width) for back in backs]
 
     grad_cols = 8 * width
     tiles = grad_cols // 128
@@ -603,10 +632,10 @@
         name="attend_back",
         cost_estimate=work_of(40),
     )(adapter_ids, *by_image, *shared, *adapters, *backs)
+    last = direct_gather(sum_after(sums[2], own_grads), "dp")
+    sums[2] = last.reshape((sizes[2],) + sums[0].shape[1:])
     part = exchange_sum(own_grads.reshape(-1, 128), "expert")
     part = exchange_sum(part, "dp")
-    last = lax.all_gather(sum_after(sums[1], part), "dp", axis=0, tiled=True)
-    sums[1] = last.reshape(sums[0].shape)
     part = exchange_gather(part, "dp")
     part = exchange_gather(part, "expert")
     own_grads = part.reshape(n_adapt, tiles, rank, 128)

time: 430 us -> 401 us (0.933)
  blocking collectives: 58.3 us -> 28.9 us
  waiting for transfers between devices: 144 us -> 130 us
  starting transfers between devices: 51.1 us -> 60.2 us
  Pallas kernels: 122 us -> 128 us
    psum x1, waiting for transfers between devices: 0.01 us -> 47.3 us  [body(): sums = list(lax.psum(tuple(sums), 'dp'))]
    ppermute x7, waiting for transfers between devices: 44.9 us -> 0.02 us  [direct_parts(): found.append(lax.ppermute(part, axis, pairs))]
    all_to_all x1 -> x0, blocking collectives: 16.5 us -> none  [exchange_gather(): lax.all_to_all(copies, axis, split_axis=0, concat_axis=0, tiled=True)]
    ppermute x7, starting transfers between devices: 30.3 us -> 13.9 us  [direct_parts(): found.append(lax.ppermute(part, axis, pairs))]
    all_gather x1 -> x0, waiting for transfers between devices: 16.2 us -> none  [body(): last = lax.all_gather(sum_after(sums[1], part), 'dp', axis=0, tiled=True)]
    all_to_all x1, waiting for transfers between devices: 23.4 us -> 7.65 us  [body(): lax.all_to_all(back, 'expert', split_axis=0, concat_axis=0, tiled=True)]
    ppermute x0 -> x7, waiting for transfers between devices: none -> 13.8 us  [direct_gather(): found.append(lax.ppermute(part, axis, pairs))]
    ppermute x0 -> x7, starting transfers between devices: none -> 12.5 us  [direct_gather(): found.append(lax.ppermute(part, axis, pairs))]
  transfers between devices with their start and end apart: 19 -> 32, of which waited for: 9 -> 14; matrix products, arithmetic and copies ran while one was open for 5% -> 6% of each run, Pallas kernels for 11% -> 12%
where the time goes in v5:
time: 401 us; the launch traced here: 400 us
  waiting for transfers between devices  130 us (32%)
  Pallas kernels  128 us (32%)
  starting transfers between devices  60.2 us (15%)
  blocking collectives  28.9 us (7%)
  local copies, waits for them, and re-layouts  22.5 us (6%)
  other arithmetic  15.2 us (4%)
  between operations  14.8 us (4%)
    pallas_call x3, Pallas kernels, body(): pl.pallas_call(functools.partial(expert_kernel, len(after), groups), out_...  62.8 us
    psum x1, waiting for transfers between devices, body(): sums = list(lax.psum(tuple(sums), 'dp'))  47.3 us
    pallas_call x1, Pallas kernels, body(): pl.pallas_call(functools.partial(backward_kernel, seq_len), out_shape=out...  40.2 us
    ppermute x4, waiting for transfers between devices, gather_blocks(): blocks.append(lax.ppermute(block, axis, pairs))  36.4 us
    all_to_all x1, blocking collectives, body(): lax.all_to_all(back, 'expert', split_axis=0, concat_axis=0, tiled=True)  28.9 us
    pallas_call x1, Pallas kernels, body(): pl.pallas_call(functools.partial(forward_kernel, seq_len), out_shape=forw...  19 us
    all_to_all x2, starting transfers between devices, exchange(): return lax.all_to_all(parts, axis, split_axis=0, concat_axis=0, tiled=True)  14.9 us
    ppermute x7, starting transfers between devices, direct_parts(): found.append(lax.ppermute(part, axis, pairs))  13.9 us
  transfers between devices with their start and end apart: 32, of which 14 were waited for; matrix products, arithmetic and copies ran while one was open for 6% of the time, Pallas kernels for 12%

profile of v5, /device:TPU:0, one launch (start us, length us, event | category | flops | bytes accessed | tf_op | source)
XLA Modules:
  0.0 399.5 jit_solution(18169930440000767145)
XLA Ops:
  12.1 19.0 %attend.1 = (bf16[4,208,1536]{2,1,0:T(8,128)(2,1)}, bf16[4,208,512]{2,1,0:T(8,128)(2,1)}, f32[4,208,512]{2,1,0:T(8,128)}, bf16[4,208,512]{2,1,0:T(8,128)(2,1)}, ...) custom-call(s32[4]{0:T(128)} %ids_ref.3, bf16[4,208,512]{2,1,0:T(8,128)(2,1)} %pad.12.images_ref, ...), custom_call_target="tpu_custom_call" | custom-call | flops 20000000000 | bytes 1000000 | tf_op jit(solution)/shard_map/attend/pallas_call | solution.py:531
  31.1 3.0 collective-permute-start.6
  35.2 2.0 collective-permute-start.3
  37.4 16.9 %collective-permute-done.6.rest_9_ = bf16[832,512]{1,0:T(8,128)(2,1)} collective-permute-done((bf16[832,512]{1,0:T(8,128)(2,1)}, bf16[832,512]{1,0:T(8,128)(2,1)}, u32[]{:S(2)}, u32[]{:S(2)}) %collective-permute-start.6) | collective-permute-done | bytes 852000 | tf_op jit(solution)/shard_map/ppermute | solution.py:350
  54.3 17.5 %collective-permute-done.9.rest_13_ = bf16[832,512]{1,0:T(8,128)(2,1)} collective-permute-done((bf16[832,512]{1,0:T(8,128)(2,1)S(1)}, bf16[832,512]{1,0:T(8,128)(2,1)}, u32[]{:S(2)}, u32[]{:S(2)}) %collective-permute-start.9) | collective-permute-done | bytes 852000 | tf_op jit(solution)/shard_map/ppermute | solution.py:350
  73.1 1.4 collective-permute-done.4.rest_6_
  74.5 1.7 collective-permute-start
  76.2 2.0 collective-permute-done.rest_1_
  82.4 28.5 %shard_map.292 = (bf16[4,2,128,1024]{3,2,1,0:T(8,128)(2,1)}, bf16[2,128,5120]{2,1,0:T(8,128)(2,1)}) custom-call(s32[5]{0:T(128)} %get-tuple-element.108.first_ref, s32[3,832]{1,0:T(4,128)} %copy-done.15, s32[3,832]{1,0:T(4,128)} %copy-done.22, s32[3,832]{1,0:T(4,128)} %copy-done.23, s32[3,832]{1,0:T(4,128)} %copy-done.24, f32[2,832]{1,0:T(2,128)} %copy-done.17, ...), custom_call_target="tpu_custom_call" | custom-call | flops 28000000000 | bytes 1000000 | tf_op jit(solution)/shard_map/pallas_call | solution.py:569
  110.9 17.2 %shard_map.293 = (bf16[4,1,128,1024]{3,2,1,0:T(8,128)(2,1)}, bf16[1,128,5120]{2,1,0:T(8,128)(2,1)}) custom-call(s32[5]{0:T(128)} %get-tuple-element.106.first_ref, s32[3,832]{1,0:T(4,128)} %copy-done.15, s32[3,832]{1,0:T(4,128)} %copy-done.22, s32[3,832]{1,0:T(4,128)} %copy-done.23, s32[3,832]{1,0:T(4,128)} %copy-done.24, f32[2,832]{1,0:T(2,128)} %copy-done.17, ...), custom_call_target="tpu_custom_call" | custom-call | flops 14000000000 | bytes 1000000 | tf_op jit(solution)/shard_map/pallas_call | solution.py:569
  128.0 17.1 %shard_map.294 = (bf16[4,1,128,1024]{3,2,1,0:T(8,128)(2,1)}, bf16[1,128,5120]{2,1,0:T(8,128)(2,1)}) custom-call(s32[5]{0:T(128)} %get-tuple-element.107.first_ref, s32[3,832]{1,0:T(4,128)} %copy-done.15, s32[3,832]{1,0:T(4,128)} %copy-done.22, s32[3,832]{1,0:T(4,128)} %copy-done.23, s32[3,832]{1,0:T(4,128)} %copy-done.24, f32[2,832]{1,0:T(2,128)} %copy-done.17, ...), custom_call_target="tpu_custom_call" | custom-call | flops 14000000000 | bytes 1000000 | tf_op jit(solution)/shard_map/pallas_call | solution.py:569
  145.2 1.4 pad_maximum_fusion
  146.6 28.9 %all_to_all.30 = bf16[4,2,128,1024]{3,2,1,0:T(8,128)(2,1)} all-to-all(bf16[4,2,128,1024]{3,2,1,0:T(8,128)(2,1)S(1)} %pad_maximum_fusion), channel_id=1, replica_groups=mesh['dp'=8,'expert'=4] {'expert'}, dimensions={0} | all-to-all | bytes 4194304 | tf_op jit(solution)/shard_map/all_to_all | solution.py:600
  175.5 3.6 all-to-all-start
  179.5 2.3 dynamic-slice_bitcast_fusion
  181.9 1.7 collective-permute-start.12
  183.6 1.6 collective-permute-start.13
  185.1 1.3 fusion.17.slots_ref
  186.4 2.6 collective-permute-start.14
  189.0 1.2 collective-permute-start.15
  190.2 2.6 collective-permute-start.16
  192.9 1.4 collective-permute-start.17
  194.3 2.8 collective-permute-start.18
  197.1 7.6 %all-to-all-done = bf16[4,2,128,1024]{3,2,1,0:T(8,128)(2,1)S(1)} async-done(((bf16[4,2,128,1024]{3,2,1,0:T(8,128)(2,1)}), bf16[4,2,128,1024]{3,2,1,0:T(8,128)(2,1)S(1)}, u32[]{:S(2)}, u32[]{:S(2)}) %all-to-all-start) | async-done | bytes 2097184 | tf_op jit(solution)/shard_map/all_to_all | solution.py:600
  204.7 1.3 copy-done
  206.1 40.2 %attend_back.1 = (bf16[4,197,512]{2,1,0:T(8,128)(2,1)}, f32[4,197,512]{2,1,0:T(8,128)}, bf16[8,32,16,128]{3,2,1,0:T(8,128)(2,1)}) custom-call(s32[4]{0:T(128)} %ids_ref.3, bf16[4,208,512]{2,1,0:T(8,128)(2,1)} %pad.12.images_ref, bf16[4,208,512]{2,1,0:T(8,128)(2,1)} %copy-done.5, f32[4,208,512]{2,1,0:T(8,128)} %get-tuple-element.27.hidden_ref, ...), custom_call_target="tpu_custom_call" | custom-call | flops 40000000000 | bytes 1000000 | tf_op jit(solution)/shard_map/attend_back/pallas_call | solution.py:617
  247.2 5.9 %add_parts.1 = bf16[16,5120]{1,0:T(8,128)(2,1)} custom-call(bf16[16,5120]{1,0:T(8,128)(2,1)} %get-tuple-element.99.refs_0_, bf16[16,5120]{1,0:T(8,128)(2,1)} %copy-done.10, bf16[16,5120]{1,0:T(8,128)(2,1)} %collective-permute-done.13.refs_2_, bf16[16,5120]{1,0:T(8,128)(2,1)} %copy-done.11, bf16[16,5120]{1,0:T(8,128)(2,1)} %copy-done.12, ...), custom_call_target="tpu_custom_call" | custom-call | tf_op jit(solution)/shard_map/add_parts/pallas_call | solution.py:417
  253.0 1.7 collective-permute-start.19
  254.7 1.6 collective-permute-start.20
  256.3 2.7 collective-permute-start.21
  260.1 2.6 collective-permute-start.23
  262.7 3.6 all-to-all-start.2
  266.6 1.2 copy-done.2
  267.8 2.2 copy.84
  270.0 1.3 copy.83
  271.3 1.3 collective-permute-start.24
  272.7 1.5 collective-permute-start.25
  274.2 2.1 collective-permute-done.21
  276.6 11.4 %collective-permute-done.24 = bf16[16,5120]{1,0:T(8,128)(2,1)S(1)} collective-permute-done((bf16[16,5120]{1,0:T(8,128)(2,1)S(1)}, bf16[16,5120]{1,0:T(8,128)(2,1)S(1)}, u32[]{:S(2)}, u32[]{:S(2)}) %collective-permute-start.24) | collective-permute-done | bytes 163872 | tf_op jit(solution)/shard_map/ppermute | solution.py:400
  289.0 11.2 %all-to-all-start.3 = ((bf16[8,128,128]{2,1,0:T(8,128)(2,1)}), bf16[8,128,128]{2,1,0:T(8,128)(2,1)S(1)}, u32[]{:S(2)}, u32[]{:S(2)}) async-start(bf16[8,128,128]{2,1,0:T(8,128)(2,1)} %bitcast.31), calls=%async_computation.3 | async-start | bytes 524288 | tf_op jit(solution)/shard_map/all_to_all | solution.py:367
  300.2 8.3 %all-to-all-done.3 = bf16[8,128,128]{2,1,0:T(8,128)(2,1)S(1)} async-done(((bf16[8,128,128]{2,1,0:T(8,128)(2,1)}), bf16[8,128,128]{2,1,0:T(8,128)(2,1)S(1)}, u32[]{:S(2)}, u32[]{:S(2)}) %all-to-all-start.3) | async-done | bytes 262176 | tf_op jit(solution)/shard_map/all_to_all | solution.py:367
  309.3 3.4 all-to-all-start.4
  312.8 12.3 %all-to-all-done.4 = bf16[8,128,128]{2,1,0:T(8,128)(2,1)S(1)} async-done(((bf16[8,128,128]{2,1,0:T(8,128)(2,1)}), bf16[8,128,128]{2,1,0:T(8,128)(2,1)S(1)}, u32[]{:S(2)}, u32[]{:S(2)}) %all-to-all-start.4) | async-done | bytes 262176 | tf_op jit(solution)/shard_map/all_to_all | solution.py:377
  326.2 3.5 all-to-all-start.5
  329.7 47.3 %all-reduce.7.cloned.1.call-done = (bf16[1,128,5120]{2,1,0:T(8,128)(2,1)}, bf16[2,128,5120]{2,1,0:T(8,128)(2,1)}) async-done(((bf16[1,128,5120]{2,1,0:T(8,128)(2,1)}, bf16[2,128,5120]{2,1,0:T(8,128)(2,1)}), (bf16[1,128,5120]{2,1,0:T(8,128)(2,1)}, bf16[2,128,5120]{2,1,0:T(8,128)(2,1)})) %all-reduce.7.cloned.1.call-update) | async-done | bytes 3932176 | tf_op jit(solution)/shard_map/psum | solution.py:604
  378.1 1.8 fusion.28
  381.5 2.5 convert.30
  385.5 2.5 convert_bitcast_fusion
  (144 shorter events, 25.6 us)
Async XLA Ops:
  7.2 2.6 copy-start.7
  12.1 22.1 %copy-start.8 = (bf16[4,197,512]{2,0,1:T(4,128)(2,1)S(1)}, bf16[4,197,512]{2,0,1:T(4,128)(2,1)}, u32[]{:S(2)}) copy-start(bf16[4,197,512]{2,0,1:T(4,128)(2,1)} %param.24) | copy-start | bytes 2420740
  31.1 3.4 copy-start.21
  31.1 4.0 %copy-start.16 = (f32[4,2,208]{2,1,0:T(2,128)S(1)}, f32[4,2,208]{2,1,0:T(2,128)}, u32[]{:S(2)}) copy-start(f32[4,2,208]{2,1,0:T(2,128)} %get-tuple-element.32) | copy-start | bytes 19972
  31.1 6.1 %copy-start.1 = (s32[4,208,2]{2,1,0:T(8,128)S(1)}, s32[4,208,2]{2,1,0:T(8,128)}, u32[]{:S(2)}) copy-start(s32[4,208,2]{2,1,0:T(8,128)} %get-tuple-element.105.picks_ref) | copy-start | bytes 19972
  31.1 23.2 %collective-permute-start.6 = (bf16[832,512]{1,0:T(8,128)(2,1)}, bf16[832,512]{1,0:T(8,128)(2,1)}, u32[]{:S(2)}, u32[]{:S(2)}) collective-permute-start(bf16[832,512]{1,0:T(8,128)(2,1)} %bitcast.191), channel_id=1, source_target_pairs={{0,2},{1,3},{2,0},{3,1},{4,6},{5,7},{6,4},{7,5},{8,10},{9,11},{10,... | collective-permute-start | bytes 2555912 | tf_op jit(solution)/shard_map/ppermute | solution.py:350
  34.3 38.0 %copy-start.20 = (s32[4]{0:T(128)S(1)}, s32[4]{0:T(128)}, u32[]{:S(2)}) copy-start(s32[4]{0:T(128)} %ids_ref.3) | copy-start | bytes 52
  34.4 47.4 %copy-start.5 = (bf16[4,208,512]{2,1,0:T(8,128)(2,1)}, bf16[4,208,512]{2,1,0:T(8,128)(2,1)S(1)}, u32[]{:S(2)}) copy-start(bf16[4,208,512]{2,1,0:T(8,128)(2,1)S(1)} %pad.13.upstream_ref) | copy-start | bytes 2555908
  34.4 37.4 %collective-permute-start.9 = (bf16[832,512]{1,0:T(8,128)(2,1)S(1)}, bf16[832,512]{1,0:T(8,128)(2,1)}, u32[]{:S(2)}, u32[]{:S(2)}) collective-permute-start(bf16[832,512]{1,0:T(8,128)(2,1)S(1)} %bitcast.170), channel_id=1, source_target_pairs={{0,2},{1,3},{2,0},{3,1},{4,6},{5,7},{6,4},{7,5},{8,10},{9,11},{10,... | collective-permute-start | bytes 2555912 | tf_op jit(solution)/shard_map/ppermute | solution.py:350
  34.5 47.3 %collective-permute-start.7 = (bf16[832,512]{1,0:T(8,128)(2,1)S(1)}, bf16[832,512]{1,0:T(8,128)(2,1)}, u32[]{:S(2)}, u32[]{:S(2)}) collective-permute-start(bf16[832,512]{1,0:T(8,128)(2,1)S(1)} %bitcast.195), channel_id=1, source_target_pairs={{0,1},{1,0},{2,3},{3,2},{4,5},{5,4},{6,7},{7,6},{8,9},{9,8},{10,11... | collective-permute-start | bytes 2555912 | tf_op jit(solution)/shard_map/ppermute | solution.py:352
  34.6 47.2 %collective-permute-start.10 = (bf16[832,512]{1,0:T(8,128)(2,1)S(1)}, bf16[832,512]{1,0:T(8,128)(2,1)}, u32[]{:S(2)}, u32[]{:S(2)}) collective-permute-start(bf16[832,512]{1,0:T(8,128)(2,1)S(1)} %bitcast.171), channel_id=1, source_target_pairs={{0,1},{1,0},{2,3},{3,2},{4,5},{5,4},{6,7},{7,6},{8,9},{9,8},{10,11... | collective-permute-start | bytes 2555912 | tf_op jit(solution)/shard_map/ppermute | solution.py:352
  35.2 46.6 %copy-start.17 = (f32[2,832]{1,0:T(2,128)}, f32[2,832]{1,0:T(2,128)S(1)}, u32[]{:S(2)}) copy-start(f32[2,832]{1,0:T(2,128)S(1)} %reshape.149.rest_4_) | copy-start | bytes 19972
  35.2 37.3 %collective-permute-start.3 = (f32[2,832]{1,0:T(2,128)S(1)}, f32[2,832]{1,0:T(2,128)S(1)}, u32[]{:S(2)}, u32[]{:S(2)}) collective-permute-start(f32[2,832]{1,0:T(2,128)S(1)} %reshape.149.rest_4_), channel_id=1, source_target_pairs={{0,2},{1,3},{2,0},{3,1},{4,6},{5,7},{6,4},{7,5},{8,10},{9,11},{10,... | collective-permute-start | bytes 19976 | tf_op jit(solution)/shard_map/ppermute | solution.py:350
  54.3 27.5 %collective-permute-start.8 = (bf16[832,512]{1,0:T(8,128)(2,1)}, bf16[832,512]{1,0:T(8,128)(2,1)}, u32[]{:S(2)}, u32[]{:S(2)}) collective-permute-start(bf16[832,512]{1,0:T(8,128)(2,1)} %collective-permute-done.6.rest_9_), channel_id=1, source_target_pairs={{0,1},{1,0},{2,3},{3,2},{4,5},{5,4},{6,7},{7,6},{8,9},{9,8},{10,11... | collective-permute-start | bytes 2555912 | tf_op jit(solution)/shard_map/ppermute | solution.py:352
  71.8 10.0 %collective-permute-start.11 = (bf16[832,512]{1,0:T(8,128)(2,1)}, bf16[832,512]{1,0:T(8,128)(2,1)}, u32[]{:S(2)}, u32[]{:S(2)}) collective-permute-start(bf16[832,512]{1,0:T(8,128)(2,1)} %collective-permute-done.9.rest_13_), channel_id=1, source_target_pairs={{0,1},{1,0},{2,3},{3,2},{4,5},{5,4},{6,7},{7,6},{8,9},{9,8},{10,11... | collective-permute-start | bytes 2555912 | tf_op jit(solution)/shard_map/ppermute | solution.py:352
  72.5 9.3 %copy-start.25 = (f32[2,832]{1,0:T(2,128)}, f32[2,832]{1,0:T(2,128)S(1)}, u32[]{:S(2)}) copy-start(f32[2,832]{1,0:T(2,128)S(1)} %collective-permute-done.3.rest_5_) | copy-start | bytes 19972
  72.5 2.0 collective-permute-start.4
  73.1 8.7 %copy-start.15 = (s32[3,832]{1,0:T(4,128)}, s32[3,832]{1,0:T(4,128)S(1)}, u32[]{:S(2)}) copy-start(s32[3,832]{1,0:T(4,128)S(1)} %pad_add_fusion.rest_0_) | copy-start | bytes 29956
  74.5 7.3 %copy-start.26 = (f32[2,832]{1,0:T(2,128)}, f32[2,832]{1,0:T(2,128)S(1)}, u32[]{:S(2)}) copy-start(f32[2,832]{1,0:T(2,128)S(1)} %collective-permute-done.4.rest_6_) | copy-start | bytes 19972
  74.5 3.7 collective-permute-start
  78.2 3.6 copy-start.22
  78.2 1.2 collective-permute-start.1
  79.4 1.2 collective-permute-start.5
  80.6 1.2 collective-permute-start.2
  128.0 17.1 %copy-start.4 = (bf16[4,1,128,1024]{3,2,1,0:T(8,128)(2,1)S(1)}, bf16[4,1,128,1024]{3,2,1,0:T(8,128)(2,1)}, u32[]{:S(2)}) copy-start(bf16[4,1,128,1024]{3,2,1,0:T(8,128)(2,1)} %get-tuple-element.34.rest_22_) | copy-start | bytes 3145732
  175.5 29.2 %all-to-all-start = ((bf16[4,2,128,1024]{3,2,1,0:T(8,128)(2,1)}), bf16[4,2,128,1024]{3,2,1,0:T(8,128)(2,1)S(1)}, u32[]{:S(2)}, u32[]{:S(2)}) async-start(bf16[4,2,128,1024]{3,2,1,0:T(8,128)(2,1)} %get-tuple-element.33.rest_22_), calls=%async_computation | async-start | bytes 4194304 | tf_op jit(solution)/shard_map/all_to_all | solution.py:600
  179.1 197.9 %all-reduce.7.cloned.1.call-start = ((), (), s32[]{:S(2)}) async-start(), calls=%async_computation.6 | async-start | bytes 7864320 | tf_op jit(solution)/shard_map/psum | solution.py:604
  181.9 11.0 %collective-permute-start.12 = (bf16[16,5120]{1,0:T(8,128)(2,1)}, bf16[16,5120]{1,0:T(8,128)(2,1)S(1)}, u32[]{:S(2)}, u32[]{:S(2)}) collective-permute-start(bf16[16,5120]{1,0:T(8,128)(2,1)} %get-tuple-element.98), channel_id=1, source_target_pairs={{0,4},{4,8},{8,12},{12,16},{16,20},{20,24},{24,28},{28,0},{1,5},{5... | collective-permute-start | bytes 491528 | tf_op jit(solution)/shard_map/ppermute | solution.py:389
  183.6 10.7 %collective-permute-start.13 = (bf16[16,5120]{1,0:T(8,128)(2,1)}, bf16[16,5120]{1,0:T(8,128)(2,1)}, u32[]{:S(2)}, u32[]{:S(2)}) collective-permute-start(bf16[16,5120]{1,0:T(8,128)(2,1)} %get-tuple-element.97), channel_id=1, source_target_pairs={{0,8},{4,12},{8,16},{12,20},{16,24},{20,28},{24,0},{28,4},{1,9},{5... | collective-permute-start | bytes 491528 | tf_op jit(solution)/shard_map/ppermute | solution.py:389
  186.4 59.9 %collective-permute-start.14 = (bf16[16,5120]{1,0:T(8,128)(2,1)}, bf16[16,5120]{1,0:T(8,128)(2,1)S(1)}, u32[]{:S(2)}, u32[]{:S(2)}) collective-permute-start(bf16[16,5120]{1,0:T(8,128)(2,1)} %get-tuple-element.96), channel_id=1, source_target_pairs={{0,12},{4,16},{8,20},{12,24},{16,28},{20,0},{24,4},{28,8},{1,13},{... | collective-permute-start | bytes 491528 | tf_op jit(solution)/shard_map/ppermute | solution.py:389
  189.0 57.4 %collective-permute-start.15 = (bf16[16,5120]{1,0:T(8,128)(2,1)}, bf16[16,5120]{1,0:T(8,128)(2,1)S(1)}, u32[]{:S(2)}, u32[]{:S(2)}) collective-permute-start(bf16[16,5120]{1,0:T(8,128)(2,1)} %get-tuple-element.95), channel_id=1, source_target_pairs={{0,16},{4,20},{8,24},{12,28},{16,0},{20,4},{24,8},{28,12},{1,17},{... | collective-permute-start | bytes 491528 | tf_op jit(solution)/shard_map/ppermute | solution.py:389
  190.2 56.2 %collective-permute-start.16 = (bf16[16,5120]{1,0:T(8,128)(2,1)}, bf16[16,5120]{1,0:T(8,128)(2,1)S(1)}, u32[]{:S(2)}, u32[]{:S(2)}) collective-permute-start(bf16[16,5120]{1,0:T(8,128)(2,1)} %get-tuple-element.94), channel_id=1, source_target_pairs={{0,20},{4,24},{8,28},{12,0},{16,4},{20,8},{24,12},{28,16},{1,21},{... | collective-permute-start | bytes 491528 | tf_op jit(solution)/shard_map/ppermute | solution.py:389
  192.9 53.5 %copy-start.10 = (bf16[16,5120]{1,0:T(8,128)(2,1)}, bf16[16,5120]{1,0:T(8,128)(2,1)S(1)}, u32[]{:S(2)}) copy-start(bf16[16,5120]{1,0:T(8,128)(2,1)S(1)} %collective-permute-done.12.refs_1_) | copy-start | bytes 491524
  192.9 53.5 %collective-permute-start.17 = (bf16[16,5120]{1,0:T(8,128)(2,1)S(1)}, bf16[16,5120]{1,0:T(8,128)(2,1)S(1)}, u32[]{:S(2)}, u32[]{:S(2)}) collective-permute-start(bf16[16,5120]{1,0:T(8,128)(2,1)S(1)} %get-tuple-element.93), channel_id=1, source_target_pairs={{0,24},{4,28},{8,0},{12,4},{16,8},{20,12},{24,16},{28,20},{1,25},{... | collective-permute-start | bytes 491528 | tf_op jit(solution)/shard_map/ppermute | solution.py:389
  194.3 52.1 %collective-permute-start.18 = (bf16[16,5120]{1,0:T(8,128)(2,1)S(1)}, bf16[16,5120]{1,0:T(8,128)(2,1)}, u32[]{:S(2)}, u32[]{:S(2)}) collective-permute-start(bf16[16,5120]{1,0:T(8,128)(2,1)S(1)} %get-tuple-element.92), channel_id=1, source_target_pairs={{0,28},{4,0},{8,4},{12,8},{16,12},{20,16},{24,20},{28,24},{1,29},{... | collective-permute-start | bytes 491528 | tf_op jit(solution)/shard_map/ppermute | solution.py:389
  253.0 18.3 %collective-permute-start.19 = (bf16[16,5120]{1,0:T(8,128)(2,1)}, bf16[16,5120]{1,0:T(8,128)(2,1)S(1)}, u32[]{:S(2)}, u32[]{:S(2)}) collective-permute-start(bf16[16,5120]{1,0:T(8,128)(2,1)} %add_parts.1), channel_id=1, source_target_pairs={{0,4},{4,8},{8,12},{12,16},{16,20},{20,24},{24,28},{28,0},{1,5},{5... | collective-permute-start | bytes 491528 | tf_op jit(solution)/shard_map/ppermute | solution.py:400
  254.7 17.9 %collective-permute-start.20 = (bf16[16,5120]{1,0:T(8,128)(2,1)}, bf16[16,5120]{1,0:T(8,128)(2,1)S(1)}, u32[]{:S(2)}, u32[]{:S(2)}) collective-permute-start(bf16[16,5120]{1,0:T(8,128)(2,1)} %add_parts.1), channel_id=1, source_target_pairs={{0,8},{4,12},{8,16},{12,20},{16,24},{20,28},{24,0},{28,4},{1,9},{5... | collective-permute-start | bytes 491528 | tf_op jit(solution)/shard_map/ppermute | solution.py:400
  256.3 20.0 %collective-permute-start.21 = (bf16[16,5120]{1,0:T(8,128)(2,1)}, bf16[16,5120]{1,0:T(8,128)(2,1)S(1)}, u32[]{:S(2)}, u32[]{:S(2)}) collective-permute-start(bf16[16,5120]{1,0:T(8,128)(2,1)} %add_parts.1), channel_id=1, source_target_pairs={{0,12},{4,16},{8,20},{12,24},{16,28},{20,0},{24,4},{28,8},{1,13},{... | collective-permute-start | bytes 491528 | tf_op jit(solution)/shard_map/ppermute | solution.py:400
  259.1 17.5 %collective-permute-start.22 = (bf16[16,5120]{1,0:T(8,128)(2,1)}, bf16[16,5120]{1,0:T(8,128)(2,1)S(1)}, u32[]{:S(2)}, u32[]{:S(2)}) collective-permute-start(bf16[16,5120]{1,0:T(8,128)(2,1)} %add_parts.1), channel_id=1, source_target_pairs={{0,16},{4,20},{8,24},{12,28},{16,0},{20,4},{24,8},{28,12},{1,17},{... | collective-permute-start | bytes 491528 | tf_op jit(solution)/shard_map/ppermute | solution.py:400
  260.1 16.4 %collective-permute-start.23 = (bf16[16,5120]{1,0:T(8,128)(2,1)}, bf16[16,5120]{1,0:T(8,128)(2,1)S(1)}, u32[]{:S(2)}, u32[]{:S(2)}) collective-permute-start(bf16[16,5120]{1,0:T(8,128)(2,1)} %add_parts.1), channel_id=1, source_target_pairs={{0,20},{4,24},{8,28},{12,0},{16,4},{20,8},{24,12},{28,16},{1,21},{... | collective-permute-start | bytes 491528 | tf_op jit(solution)/shard_map/ppermute | solution.py:400
  262.7 3.8 copy-start.9
  262.7 25.3 %all-to-all-start.2 = ((bf16[4,1024,128]{2,1,0:T(8,128)(2,1)}), bf16[4,1024,128]{2,1,0:T(8,128)(2,1)S(1)}, u32[]{:S(2)}, u32[]{:S(2)}) async-start(bf16[4,1024,128]{2,1,0:T(8,128)(2,1)} %bitcast.30), calls=%async_computation.2 | async-start | bytes 2097152 | tf_op jit(solution)/shard_map/all_to_all | solution.py:367
  266.6 3.5 copy-start.6
  271.3 16.7 %collective-permute-start.24 = (bf16[16,5120]{1,0:T(8,128)(2,1)S(1)}, bf16[16,5120]{1,0:T(8,128)(2,1)S(1)}, u32[]{:S(2)}, u32[]{:S(2)}) collective-permute-start(bf16[16,5120]{1,0:T(8,128)(2,1)S(1)} %copy-done.9), channel_id=1, source_target_pairs={{0,24},{4,28},{8,0},{12,4},{16,8},{20,12},{24,16},{28,20},{1,25},{... | collective-permute-start | bytes 491528 | tf_op jit(solution)/shard_map/ppermute | solution.py:400
  272.7 27.5 %collective-permute-start.25 = (bf16[16,5120]{1,0:T(8,128)(2,1)S(1)}, bf16[16,5120]{1,0:T(8,128)(2,1)S(1)}, u32[]{:S(2)}, u32[]{:S(2)}) collective-permute-start(bf16[16,5120]{1,0:T(8,128)(2,1)S(1)} %copy-done.9), channel_id=1, source_target_pairs={{0,28},{4,0},{8,4},{12,8},{16,12},{20,16},{24,20},{28,24},{1,29},{... | collective-permute-start | bytes 491528 | tf_op jit(solution)/shard_map/ppermute | solution.py:400
  289.0 19.6 %all-to-all-start.3 = ((bf16[8,128,128]{2,1,0:T(8,128)(2,1)}), bf16[8,128,128]{2,1,0:T(8,128)(2,1)S(1)}, u32[]{:S(2)}, u32[]{:S(2)}) async-start(bf16[8,128,128]{2,1,0:T(8,128)(2,1)} %bitcast.31), calls=%async_computation.3 | async-start | bytes 524288 | tf_op jit(solution)/shard_map/all_to_all | solution.py:367
  309.3 15.8 %all-to-all-start.4 = ((bf16[8,128,128]{2,1,0:T(8,128)(2,1)}), bf16[8,128,128]{2,1,0:T(8,128)(2,1)S(1)}, u32[]{:S(2)}, u32[]{:S(2)}) async-start(bf16[8,128,128]{2,1,0:T(8,128)(2,1)} %broadcast_in_dim.62), calls=%async_computation.4 | async-start | bytes 524288 | tf_op jit(solution)/shard_map/all_to_all | solution.py:377
  326.2 61.9 %all-to-all-start.5 = ((bf16[4,1024,128]{2,1,0:T(8,128)(2,1)}), bf16[4,1024,128]{2,1,0:T(8,128)(2,1)S(1)}, u32[]{:S(2)}, u32[]{:S(2)}) async-start(bf16[4,1024,128]{2,1,0:T(8,128)(2,1)} %broadcast_in_dim.64), calls=%async_computation.5 | async-start | bytes 2097152 | tf_op jit(solution)/shard_map/all_to_all | solution.py:377
  (12 other events, 16.1 us)
Sparse Core Ops, SparseCore 0:
  193.0 183.9 all-reduce.6
